TPU v7x, 512 devices: a whole 4x8x8 slice. The times are simulated.
512 devices in a mesh: pipe: 16 (over y, core), tensor: 32 (over z, x).
Axes of the slice: x: 4, y: 8, z: 8, core: 2. Of those that a mesh axis runs over, the one named last changes fastest.
Arguments:
- patches: bfloat16 [262144, 1280], P(('pipe', 'tensor')), may hold values from -6 to 6
- attn_gain: float32 [1280], replicated, may hold values from 0.25 to 1.75
- w_qkv: bfloat16 [1280, 3840], P('tensor', 'pipe'), may hold values from -0.1118034 to 0.1118034
- w_out: bfloat16 [1280, 1280], P('tensor', 'pipe'), may hold values from -0.15625 to 0.15625
- merge_gain: float32 [1280], replicated, may hold values from 0.25 to 1.75
- window_ids: int32 [262144], P(('pipe', 'tensor')), may hold values from 0 to 127, as said below
- image_patches: int32 [2048], P(('pipe', 'tensor')), may hold values from 0 to 512, as said below
- image_sample: int32 [2048], P(('pipe', 'tensor')), may hold values from 0 to 7
Outputs:
- vision_seq: bfloat16 [16, 128, 32, 5120], P('pipe', None, 'tensor')
Inputs may be any that keep to these rules, and one draw needn't show every extreme that they name: `window_ids`: Non-decreasing within each bundle and equal over each 4 consecutive slots; every window lies within one aligned block of 64 slots of a bundle. `image_patches`: multiples of 128; the images of one bundle take at most 512 slots and at least half of them, and in every micro-batch some bundle is full.
All inputs are finite; a program needn't handle non-finite values.
Results may differ from a plain program's by a relative error of at most 0.0053.
Values may be sent and summed in bfloat16 or wider, within the bound.
No kernel may reach another device: no remote copies, remote signals or barrier semaphores. Data moves between devices by JAX's collectives and lax.ppermute only.
A program may use at most 64 MiB of HBM per device.

v0:
```python
import math

import jax
import jax.numpy as jnp
from jax import lax
from jax.sharding import PartitionSpec as P

HEADS = 16
WINDOW = 64
SAMPLES = 8


epsilon = 1e-06


def joined_along(blocks, dim):
    dims = list(blocks.shape[1:])
    dims[dim] *= blocks.shape[0]
    return jnp.moveaxis(blocks, 0, dim).reshape(dims)


def copy_for_each(x, axis):
    size = lax.axis_size(axis)
    return lax.all_to_all(jnp.broadcast_to(x[None], (size, *x.shape)), axis, 0, 0, tiled=True)


def gather_directly(x, axis, dim):
    return joined_along(copy_for_each(x, axis), dim)


def normalize(values, gain_row):
    return (
        values * lax.rsqrt(jnp.mean(values * values, axis=-1, keepdims=True) + epsilon) * gain_row
    )


def token_positions(starts, merged_count, token_count):
    offsets = jnp.cumsum(merged_count) - merged_count
    token_index = jnp.arange(token_count, dtype=jnp.int32)
    inside = (token_index[None, :] >= offsets[:, None]) & (
        token_index[None, :] < (offsets + merged_count)[:, None]
    )
    position = jnp.sum(
        jnp.where(inside, starts[:, None] + token_index[None, :] - offsets[:, None], 0), axis=0
    )
    return jnp.where(jnp.any(inside, axis=0), position, -1)


def body(patches, attn_gain, w_qkv, w_out, merge_gain, window_ids, image_patches, image_sample):
    patch_count, feature_width = patches.shape
    token_count = patch_count // 4
    group_size = lax.axis_size("tensor")
    own_index = lax.axis_index("tensor")
    residual = patches.astype(jnp.float32)
    normed = normalize(residual, attn_gain).astype(jnp.bfloat16)
    qkv_rows = gather_directly(w_qkv, "tensor", 0)
    qkv = jnp.dot(
        normed,
        lax.all_gather(qkv_rows, "pipe", axis=1, tiled=True),
        preferred_element_type=jnp.float32,
    ).astype(jnp.bfloat16)
    head_width = feature_width // HEADS
    tile_count = patch_count // WINDOW

    def split_heads(block):
        return block.reshape(tile_count, WINDOW, HEADS, head_width)

    queries = split_heads(qkv[:, :feature_width])
    keys_tile = split_heads(qkv[:, feature_width : 2 * feature_width])
    values_tile = split_heads(qkv[:, 2 * feature_width :])
    scores = jnp.einsum(
        "tqhd,tkhd->thqk", queries, keys_tile, preferred_element_type=jnp.float32
    ) * (1.0 / math.sqrt(head_width))
    live_row = jnp.arange(patch_count, dtype=jnp.int32) < jnp.sum(image_patches)
    window_tile = window_ids.reshape(tile_count, WINDOW)
    live_tile = live_row.reshape(tile_count, WINDOW)
    allowed = (window_tile[:, :, None] == window_tile[:, None, :]) & live_tile[:, None, :]
    scores = jnp.where(allowed[:, None, :, :], scores, -1e30)
    row_max = jnp.max(scores, axis=-1, keepdims=True)
    exponent = jnp.exp(scores - row_max)
    weights = (exponent / jnp.sum(exponent, axis=-1, keepdims=True)).astype(jnp.bfloat16)
    context = jnp.einsum(
        "thqk,tkhd->tqhd", weights, values_tile, preferred_element_type=jnp.float32
    ).reshape(patch_count, feature_width)
    context = jnp.where(live_row[:, None], context, 0.0).astype(jnp.bfloat16)
    proj_rows = lax.all_gather(w_out, "tensor", axis=0, tiled=True)
    attended = jnp.dot(
        context,
        lax.all_gather(proj_rows, "pipe", axis=1, tiled=True),
        preferred_element_type=jnp.float32,
    )
    hidden = residual + attended
    merged = (
        normalize(hidden, merge_gain).astype(jnp.bfloat16).reshape(token_count, 4 * feature_width)
    )
    outgoing = merged.reshape(token_count // group_size, group_size, 4 * feature_width)
    merged_count = image_patches // 4
    sample_hot = image_sample[:, None] == jnp.arange(SAMPLES, dtype=jnp.int32)[None, :]
    sample_tally = jnp.sum(jnp.where(sample_hot, merged_count[:, None], 0), axis=0)
    all_tallies = gather_directly(sample_tally[None, :], "tensor", 0)
    source_ranks = jnp.arange(group_size, dtype=jnp.int32)
    before = jnp.sum(jnp.where((source_ranks < own_index)[:, None], all_tallies, 0), axis=0)
    totals = jnp.sum(all_tallies, axis=0)
    sample_index = jnp.arange(SAMPLES, dtype=jnp.int32)
    sample_base = jnp.sum(
        jnp.where(sample_index[None, :] < sample_index[:, None], totals[None, :], 0), axis=1
    )
    image_order = jnp.arange(image_sample.shape[0], dtype=jnp.int32)
    same_before = (image_sample[None, :] == image_sample[:, None]) & (
        image_order[None, :] < image_order[:, None]
    )
    earlier = jnp.sum(jnp.where(same_before, merged_count[None, :], 0), axis=1)
    starts = jnp.sum(jnp.where(sample_hot, (sample_base + before)[None, :], 0), axis=1) + earlier
    position = token_positions(starts, merged_count, token_count)
    outgoing_position = position.reshape(token_count // group_size, group_size)
    received, received_position = (
        lax.all_to_all(outgoing, "tensor", split_axis=1, concat_axis=0, tiled=True),
        lax.all_to_all(outgoing_position, "tensor", split_axis=1, concat_axis=0, tiled=True),
    )
    dest_rows = received_position.reshape(token_count) // group_size
    placement = (jnp.arange(token_count, dtype=jnp.int32)[:, None] == dest_rows[None, :]).astype(
        jnp.bfloat16
    )
    placed = jnp.dot(
        placement,
        received.reshape(token_count, 4 * feature_width),
        preferred_element_type=jnp.float32,
    )
    return placed.astype(jnp.bfloat16).reshape(1, token_count, 1, 4 * feature_width)


def solution(mesh):
    return jax.shard_map(
        body,
        mesh=mesh,
        in_specs=(
            P(("pipe", "tensor"), None),
            P(),
            P("tensor", "pipe"),
            P("tensor", "pipe"),
            P(),
            P(("pipe", "tensor")),
            P(("pipe", "tensor")),
            P(("pipe", "tensor")),
        ),
        out_specs=P("pipe", None, "tensor", None),
        check_vma=False,
    )
```

profile of v0, /device:TPU:4, one launch (start us, length us, event | category | flops | bytes accessed | tf_op | source)
XLA Modules:
  0.0 208.7 jit_solution(4896109178755569658)
XLA Ops:
  6.6 0.9 broadcast_in_dim.144
  7.5 32.9 %all_to_all.38 = bf16[32,40,240]{2,1,0:T(8,128)(2,1)S(1)} all-to-all(bf16[32,40,240]{2,1,0:T(8,128)(2,1)S(1)} %broadcast_in_dim.144), channel_id=1, replica_groups=mesh['pipe'=16,'tensor'=32] {'tensor'}, dimensions={0} | all-to-all | bytes 1228800 | tf_op jit(solution)/shard_map/all_to_all | solution.py:24
  40.4 1.1 copy.60
  41.5 47.5 %all_gather.10 = bf16[1280,80]{1,0:T(8,128)(2,1)S(1)} all-gather(bf16[40,80]{1,0:T(8,128)(2,1)S(1)} %copy-done.3), channel_id=1, replica_groups=mesh['pipe'=16,'tensor'=32] {'tensor'}, dimensions={0}, use_global_device_ids=true | all-gather | bytes 211200 | tf_op jit(solution)/shard_map/all_gather | solution.py:86
  89.0 0.9 copy.66
  91.3 6.7 %all-to-all-start = ((s32[32,1,8]{2,1,0:T(1,128)}), s32[32,1,8]{2,1,0:T(1,128)S(1)}, u32[]{:S(2)}, u32[]{:S(2)}) async-start(s32[32,1,8]{2,1,0:T(1,128)} %broadcast_in_dim.96), calls=%async_computation | async-start | bytes 32768 | tf_op jit(solution)/shard_map/all_to_all | solution.py:24
  100.4 5.4 %all-to-all-done = s32[32,1,8]{2,1,0:T(1,128)S(1)} async-done(((s32[32,1,8]{2,1,0:T(1,128)}), s32[32,1,8]{2,1,0:T(1,128)S(1)}, u32[]{:S(2)}, u32[]{:S(2)}) %all-to-all-start) | async-done | bytes 1056 | tf_op jit(solution)/shard_map/all_to_all | solution.py:24
  107.1 5.7 %all-to-all-start.1 = ((s32[4,32,1]{0,2,1:T(1,128)}), s32[4,32,1]{0,2,1:T(1,128)S(1)}, u32[]{:S(2)}, u32[]{:S(2)}) async-start(s32[4,32,1]{0,2,1:T(1,128)} %copy.59), calls=%async_computation.1 | async-start | bytes 32768 | tf_op jit(solution)/shard_map/all_to_all | solution.py:118
  112.9 9.5 %convolution_convert_fusion.1 = bf16[512,3840]{1,0:T(8,128)(2,1)S(1)} fusion(bf16[1280,3840]{0,1:T(8,128)(2,1)} %all-gather.3.cloned.1.call-done, bf16[512,1280]{1,0:T(8,128)(2,1)S(1)} %copy-done.1, f32[1280]{0:T(1024)S(1)} %copy-done.7, f32[512]{0:T(512)S(1)} %add_rsqrt_fusion.1), kind=kOutput, calls=%fused_computation.2 | convolution fusion | flops 5037752320 | bytes 15080448 | tf_op jit(solution)/shard_map/dot_general | solution.py:57
  122.4 1.7 fusion.26
  124.1 4.1 %reshape.170 = bf16[8,64,16,80]{3,2,1,0:T(8,128)(2,1)S(1)} reshape(bf16[512,1280]{1,0:T(8,128)(2,1)} %get-tuple-element.7) | data formatting | bytes 2621440 | tf_op jit(solution)/shard_map/reshape | solution.py:66
  128.2 5.1 %reshape.171 = bf16[8,64,16,80]{3,2,1,0:T(8,128)(2,1)} reshape(bf16[512,1280]{1,0:T(8,128)(2,1)} %get-tuple-element.6) | data formatting | bytes 2621440 | tf_op jit(solution)/shard_map/reshape | solution.py:66
  133.3 4.1 %reshape.169 = bf16[8,64,16,80]{3,2,1,0:T(8,128)(2,1)} reshape(bf16[512,1280]{1,0:T(8,128)(2,1)S(1)} %get-tuple-element.5) | data formatting | bytes 2621440 | tf_op jit(solution)/shard_map/reshape | solution.py:66
  137.4 2.8 %fusion.7 = f32[8,16,64,64]{2,3,1,0:T(8,128)S(1)} fusion(bf16[8,64,16,80]{3,2,1,0:T(8,128)(2,1)} %reshape.171, bf16[8,64,16,80]{3,2,1,0:T(8,128)(2,1)S(1)} %reshape.170), kind=kOutput, calls=%fused_computation.19 | convolution fusion | flops 83886080 | bytes 4718592 | tf_op jit(solution)/shard_map/tqhd,tkhd->thqk/dot_general | solution.py:71
  140.2 1.5 fusion.27
  141.8 1.2 convolution_bitcast_fusion
  143.0 1.4 copy.65
  144.4 3.3 %reshape.172 = bf16[512,1280]{1,0:T(8,128)(2,1)} reshape(bf16[8,64,16,80]{3,2,1,0:T(8,128)(2,1)S(1)} %copy.65) | data formatting | bytes 2621440 | tf_op jit(solution)/shard_map/reshape | solution.py:84
  147.8 4.4 %multiply_reduce_fusion = (f32[512]{0:T(512)S(1)}, f32[512,1280]{1,0:T(8,128)S(1)}) fusion(bf16[1280,1280]{0,1:T(8,128)(2,1)} %all-gather.5.cloned.1.call-done, bf16[512,1280]{1,0:T(8,128)(2,1)} %reshape.172, pred[512]{0:T(512)(128)(4,1)S(1)} %iota_compare_fusion.3, bf16[512,1280]{1,0:T(8,128)(2,1)S(1)} %copy-done.2), kind=kOutput, calls=%fused_computation.15 | convolution fusion | flops 1680997888 | bytes 8522240 | tf_op jit(solution)/shard_map/dot_general | solution.py:87
  152.5 0.8 reshape_reshape.3
  153.3 2.1 copy.67
  155.4 10.5 %all-to-all-start.3 = ((bf16[4,32,5120]{2,0,1:T(4,128)(2,1)}), bf16[4,32,5120]{2,0,1:T(4,128)(2,1)S(1)}, u32[]{:S(2)}, u32[]{:S(2)}) async-start(bf16[4,32,5120]{2,0,1:T(4,128)(2,1)} %copy.67), calls=%async_computation.3 | async-start | bytes 2621440 | tf_op jit(solution)/shard_map/all_to_all | solution.py:117
  166.1 33.9 %all-to-all-done.3 = bf16[4,32,5120]{2,0,1:T(4,128)(2,1)S(1)} async-done(((bf16[4,32,5120]{2,0,1:T(4,128)(2,1)}), bf16[4,32,5120]{2,0,1:T(4,128)(2,1)S(1)}, u32[]{:S(2)}, u32[]{:S(2)}) %all-to-all-start.3) | async-done | bytes 1310752 | tf_op jit(solution)/shard_map/all_to_all | solution.py:117
  200.3 1.6 fusion.1
  (55 shorter events, 6.3 us)
Async XLA Ops:
  6.5 35.0 %copy-start.3 = (bf16[40,80]{1,0:T(8,128)(2,1)S(1)}, bf16[40,80]{1,0:T(8,128)(2,1)}, u32[]{:S(2)}) copy-start(bf16[40,80]{1,0:T(8,128)(2,1)} %param.11) | copy-start | bytes 19204
  6.5 83.4 %copy-start.8 = (s32[4]{0:T(128)S(1)}, s32[4]{0:T(128)}, u32[]{:S(2)}) copy-start(s32[4]{0:T(128)} %param.14) | copy-start | bytes 52
  6.5 84.1 %copy-start.6 = (s32[4]{0:T(128)S(1)}, s32[4]{0:T(128)}, u32[]{:S(2)}) copy-start(s32[4]{0:T(128)} %param.15) | copy-start | bytes 52
  6.5 91.5 %copy-start.5 = (s32[512]{0:T(512)S(1)}, s32[512]{0:T(512)}, u32[]{:S(2)}) copy-start(s32[512]{0:T(512)} %param.13) | copy-start | bytes 6148
  6.5 93.3 %copy-start.1 = (bf16[512,1280]{1,0:T(8,128)(2,1)S(1)}, bf16[512,1280]{1,0:T(8,128)(2,1)}, u32[]{:S(2)}) copy-start(bf16[512,1280]{1,0:T(8,128)(2,1)} %param.8) | copy-start | bytes 3932164
  6.6 106.3 %all-gather.3.cloned.1.call-start = ((), (), s32[]{:S(2)}) async-start(), calls=%async_computation.4 | async-start | bytes 10444800 | tf_op jit(solution)/shard_map/all_gather | solution.py:59
  7.5 105.4 %copy-start.7 = (f32[1280]{0:T(1024)S(1)}, f32[1280]{0:T(1024)}, u32[]{:S(2)}) copy-start(f32[1280]{0:T(1024)} %param.9) | copy-start | bytes 15364
  41.4 106.4 %all-gather.5.cloned.1.call-start = ((), (), s32[]{:S(2)}) async-start(), calls=%async_computation.5 | async-start | bytes 3481600 | tf_op jit(solution)/shard_map/all_gather | solution.py:89
  91.3 14.5 %all-to-all-start = ((s32[32,1,8]{2,1,0:T(1,128)}), s32[32,1,8]{2,1,0:T(1,128)S(1)}, u32[]{:S(2)}, u32[]{:S(2)}) async-start(s32[32,1,8]{2,1,0:T(1,128)} %broadcast_in_dim.96), calls=%async_computation | async-start | bytes 32768 | tf_op jit(solution)/shard_map/all_to_all | solution.py:24
  107.1 48.3 %all-to-all-start.1 = ((s32[4,32,1]{0,2,1:T(1,128)}), s32[4,32,1]{0,2,1:T(1,128)S(1)}, u32[]{:S(2)}, u32[]{:S(2)}) async-start(s32[4,32,1]{0,2,1:T(1,128)} %copy.59), calls=%async_computation.1 | async-start | bytes 32768 | tf_op jit(solution)/shard_map/all_to_all | solution.py:118
  140.2 1.6 copy-start
  144.4 3.5 %copy-start.2 = (bf16[512,1280]{1,0:T(8,128)(2,1)S(1)}, bf16[512,1280]{1,0:T(8,128)(2,1)}, u32[]{:S(2)}) copy-start(bf16[512,1280]{1,0:T(8,128)(2,1)} %param.8) | copy-start | bytes 3932164
  147.6 4.5 %copy-start.4 = (f32[1280]{0:T(1024)S(1)}, f32[1280]{0:T(1024)}, u32[]{:S(2)}) copy-start(f32[1280]{0:T(1024)} %param.12) | copy-start | bytes 15364
  155.4 44.6 %all-to-all-start.3 = ((bf16[4,32,5120]{2,0,1:T(4,128)(2,1)}), bf16[4,32,5120]{2,0,1:T(4,128)(2,1)S(1)}, u32[]{:S(2)}, u32[]{:S(2)}) async-start(bf16[4,32,5120]{2,0,1:T(4,128)(2,1)} %copy.67), calls=%async_computation.3 | async-start | bytes 2621440 | tf_op jit(solution)/shard_map/all_to_all | solution.py:117
Sparse Core Ops, SparseCore 0:
  41.6 61.6 all-gather.2
  105.4 42.3 all-gather.4
where the time goes:
time: 209 us
  blocking collectives  80.4 us (38%)
  waiting for transfers between devices  39.5 us (19%)
  local copies, waits for them, and re-layouts  27.4 us (13%)
  starting transfers between devices  23 us (11%)
  matrix products  19.4 us (9%)
  between operations  13.6 us (7%)
  other arithmetic  5.39 us (3%)
    all_gather x1, blocking collectives, body(): proj_rows = lax.all_gather(w_out, 'tensor', axis=0, tiled=True)  47.5 us
    all_to_all x1, waiting for transfers between devices, body(): lax.all_to_all(outgoing, 'tensor', split_axis=1, concat_axis=0, tiled=True)  33.9 us
    all_to_all x1, blocking collectives, copy_for_each(): lax.all_to_all(jnp.broadcast_to(x[None], (size, *x.shape)), axis, 0, 0, t...  32.9 us
    reshape x3, local copies, waits for them, and re-layouts, split_heads(): return block.reshape(tile_count, WINDOW, HEADS, head_width)  13.2 us
    all_to_all x1, starting transfers between devices, body(): lax.all_to_all(outgoing, 'tensor', split_axis=1, concat_axis=0, tiled=True)  10.5 us
    dot_general x1, matrix products, body(): jnp.dot(normed, lax.all_gather(qkv_rows, 'pipe', axis=1, tiled=True), pre...  9.5 us
    all_to_all x1, starting transfers between devices, copy_for_each(): lax.all_to_all(jnp.broadcast_to(x[None], (size, *x.shape)), axis, 0, 0, t...  6.7 us
    all_to_all x1, starting transfers between devices, body(): lax.all_to_all(outgoing_position, 'tensor', split_axis=1, concat_axis=0,...  5.71 us
  transfers between devices with their start and end apart: 5, of which 3 were waited for; matrix products, arithmetic and copies ran while one was open for 23% of the time, Pallas kernels for 0%

commit v1 on v0

v1 whole, which is shorter than its diff:
```python
import math

import jax
import jax.numpy as jnp
from jax import lax
from jax.sharding import PartitionSpec as P

HEADS = 16
WINDOW = 64


epsilon = 1e-06


def copy_for_each(x, axis):
    size = lax.axis_size(axis)
    return lax.all_to_all(jnp.broadcast_to(x[None], (size, *x.shape)), axis, 0, 0, tiled=True)


def normalize(values, gain_row):
    return (
        values * lax.rsqrt(jnp.mean(values * values, axis=-1, keepdims=True) + epsilon) * gain_row
    )


def destination_rows(image_patches, image_sample):
    info = copy_for_each(jnp.concatenate([image_patches, image_sample]), "tensor")
    slots = image_patches.shape[0]
    units = info[:, :slots] // 128
    samples = info[:, slots:].reshape(-1)
    flat = units.reshape(-1)
    order = jnp.arange(flat.shape[0], dtype=jnp.int32)
    ahead = (samples[:, None] < samples[None, :]) | (
        (samples[:, None] == samples[None, :]) & (order[:, None] < order[None, :])
    )
    starts = jnp.sum(jnp.where(ahead, flat[:, None], 0), axis=0).reshape(units.shape)
    slot = jnp.arange(slots, dtype=jnp.int32)
    offsets = jnp.sum(jnp.where(slot[:, None] < slot[None, :], units[:, :, None], 0), axis=1)
    unit = slot[None, None, :]
    inside = (unit >= offsets[:, :, None]) & (unit < (offsets + units)[:, :, None])
    row = jnp.sum(jnp.where(inside, (starts - offsets)[:, :, None] + unit, 0), axis=1)
    return jnp.where(jnp.any(inside, axis=1), row, -1)


def body(patches, attn_gain, w_qkv, w_out, merge_gain, window_ids, image_patches, image_sample):
    patch_count, feature_width = patches.shape
    token_count = patch_count // 4
    group_size = lax.axis_size("tensor")
    residual = patches.astype(jnp.float32)
    normed = normalize(residual, attn_gain).astype(jnp.bfloat16)
    qkv_part = w_qkv.shape[1]
    slabs = lax.all_gather(
        jnp.concatenate([w_qkv, w_out], axis=1), ("pipe", "tensor"), axis=0, tiled=True
    ).reshape(lax.axis_size("pipe"), feature_width, -1)
    qkv = (
        jnp.einsum(
            "nk,pkc->npc", normed, slabs[:, :, :qkv_part], preferred_element_type=jnp.float32
        )
        .astype(jnp.bfloat16)
        .reshape(patch_count, 3 * feature_width)
    )
    head_width = feature_width // HEADS
    tile_count = patch_count // WINDOW

    def split_heads(block):
        return block.reshape(tile_count, WINDOW, HEADS, head_width)

    queries = split_heads(qkv[:, :feature_width])
    keys_tile = split_heads(qkv[:, feature_width : 2 * feature_width])
    values_tile = split_heads(qkv[:, 2 * feature_width :])
    scores = jnp.einsum(
        "tqhd,tkhd->thqk", queries, keys_tile, preferred_element_type=jnp.float32
    ) * (1.0 / math.sqrt(head_width))
    live_row = jnp.arange(patch_count, dtype=jnp.int32) < jnp.sum(image_patches)
    window_tile = window_ids.reshape(tile_count, WINDOW)
    live_tile = live_row.reshape(tile_count, WINDOW)
    allowed = (window_tile[:, :, None] == window_tile[:, None, :]) & live_tile[:, None, :]
    scores = jnp.where(allowed[:, None, :, :], scores, -1e30)
    row_max = jnp.max(scores, axis=-1, keepdims=True)
    exponent = jnp.exp(scores - row_max)
    weights = (exponent / jnp.sum(exponent, axis=-1, keepdims=True)).astype(jnp.bfloat16)
    context = jnp.einsum(
        "thqk,tkhd->tqhd", weights, values_tile, preferred_element_type=jnp.float32
    ).reshape(patch_count, feature_width)
    context = jnp.where(live_row[:, None], context, 0.0).astype(jnp.bfloat16)
    attended = jnp.einsum(
        "nk,pkc->npc", context, slabs[:, :, qkv_part:], preferred_element_type=jnp.float32
    ).reshape(patch_count, feature_width)
    hidden = residual + attended
    merged = (
        normalize(hidden, merge_gain).astype(jnp.bfloat16).reshape(token_count, 4 * feature_width)
    )
    outgoing = merged.reshape(token_count // group_size, group_size, 4 * feature_width)
    dest_rows = destination_rows(image_patches, image_sample)
    received = lax.all_to_all(outgoing, "tensor", split_axis=1, concat_axis=0, tiled=True)
    placement = (jnp.arange(token_count, dtype=jnp.int32)[:, None] == dest_rows.reshape(1, token_count)).astype(
        jnp.bfloat16
    )
    placed = jnp.dot(
        placement,
        received.reshape(token_count, 4 * feature_width),
        preferred_element_type=jnp.float32,
    )
    return placed.astype(jnp.bfloat16).reshape(1, token_count, 1, 4 * feature_width)


def solution(mesh):
    return jax.shard_map(
        body,
        mesh=mesh,
        in_specs=(
            P(("pipe", "tensor"), None),
            P(),
            P("tensor", "pipe"),
            P("tensor", "pipe"),
            P(),
            P(("pipe", "tensor")),
            P(("pipe", "tensor")),
            P(("pipe", "tensor")),
        ),
        out_specs=P("pipe", None, "tensor", None),
        check_vma=False,
    )
```

time: 209 us -> 279 us (1.33)
  waiting for transfers between devices: 39.5 us -> 154 us
  blocking collectives: 80.4 us -> 0 us
  local copies, waits for them, and re-layouts: 27.4 us -> 60.8 us
  other arithmetic: 5.39 us -> 8.86 us
    all_gather x2 -> x1, waiting for transfers between devices: 0.19 us -> 122 us  [body(): lax.all_gather(jnp.concatenate([w_qkv, w_out], axis=1), ('pipe', 'tensor'...]
    all_gather x1 -> x0, blocking collectives: 47.5 us -> none  [body(): proj_rows = lax.all_gather(w_out, 'tensor', axis=0, tiled=True)]
    all_to_all x1 -> x0, blocking collectives: 32.9 us -> none  [copy_for_each(): lax.all_to_all(jnp.broadcast_to(x[None], (size, *x.shape)), axis, 0, 0, t...]
    dot_general x0 -> x2, local copies, waits for them, and re-layouts: none -> 15.6 us  [body(): jnp.einsum('nk,pkc->npc', context, slabs[:, :, qkv_part:], preferred_elem...]
    unnamed x18 -> x11, local copies, waits for them, and re-layouts: 0.12 us -> 14.6 us
    dot_general x2 -> x1, matrix products: 13.9 us -> 4.36 us  [body(): jnp.einsum('nk,pkc->npc', context, slabs[:, :, qkv_part:], preferred_elem...]
    slice x0 -> x2, local copies, waits for them, and re-layouts: none -> 8.93 us  [the longest x1 8.84 us: body(): slabs[:, :, :qkv_part]]
    unnamed x0 -> x1, matrix products: none -> 8.1 us
  transfers between devices with their start and end apart: 5 -> 3, of which waited for: 3 -> 2; matrix products, arithmetic and copies ran while one was open for 23% -> 31% of each run, Pallas kernels for 0% -> 0%
where the time goes in v1:
time: 279 us; the launch traced here: 278 us
  waiting for transfers between devices  154 us (55%)
  local copies, waits for them, and re-layouts  60.8 us (22%)
  starting transfers between devices  21.5 us (8%)
  matrix products  18.8 us (7%)
  between operations  13.6 us (5%)
  other arithmetic  8.86 us (3%)
    all_gather x1, waiting for transfers between devices, body(): lax.all_gather(jnp.concatenate([w_qkv, w_out], axis=1), ('pipe', 'tensor'...  122 us
    all_to_all x1, waiting for transfers between devices, body(): lax.all_to_all(outgoing, 'tensor', split_axis=1, concat_axis=0, tiled=True)  32.9 us
    dot_general x2, local copies, waits for them, and re-layouts, body(): jnp.einsum('nk,pkc->npc', context, slabs[:, :, qkv_part:], preferred_elem...  15.6 us
    unnamed x11, local copies, waits for them, and re-layouts  14.6 us
    all_to_all x1, starting transfers between devices, copy_for_each(): lax.all_to_all(jnp.broadcast_to(x[None], (size, *x.shape)), axis, 0, 0, t...  13.4 us
    reshape x3, local copies, waits for them, and re-layouts, split_heads(): return block.reshape(tile_count, WINDOW, HEADS, head_width)  9.87 us
    slice x1, local copies, waits for them, and re-layouts, body(): slabs[:, :, :qkv_part]  8.84 us
    unnamed x1, matrix products  8.1 us
  transfers between devices with their start and end apart: 3, of which 2 were waited for; matrix products, arithmetic and copies ran while one was open for 31% of the time, Pallas kernels for 0%

profile of v1, /device:TPU:4, one launch (start us, length us, event | category | flops | bytes accessed | tf_op | source)
XLA Modules:
  0.0 277.9 jit_solution(15656463326498306071)
XLA Ops:
  6.5 1.4 pad_maximum_fusion
  9.4 13.4 %all-to-all-start = ((s32[32,1,8]{2,1,0:T(1,128)}), s32[32,1,8]{2,1,0:T(1,128)S(1)}, u32[]{:S(2)}, u32[]{:S(2)}) async-start(s32[32,1,8]{2,1,0:T(1,128)} %broadcast_in_dim.83), calls=%async_computation | async-start | bytes 32768 | tf_op jit(solution)/shard_map/all_to_all | solution.py:17
  22.8 1.3 reduce_sum.66
  25.5 1.6 fusion.3
  27.4 121.5 %all-gather.2.cloned.1.call-done = bf16[20480,320]{1,0:T(8,128)(2,1)} async-done(((bf16[40,320]{1,0:T(8,128)(2,1)}), bf16[20480,320]{1,0:T(8,128)(2,1)}) %all-gather.2.cloned.1.call-update) | async-done | bytes 13107216 | tf_op jit(solution)/shard_map/all_gather | solution.py:52
  148.9 8.2 %slice_bitcast_fusion = bf16[16,80,1280]{1,2,0:T(8,128)(2,1)} fusion(bf16[16,1280,320]{2,1,0:T(8,128)(2,1)} %bitcast.32), kind=kLoop, calls=%fused_computation.3 | loop fusion | bytes 6553600 | tf_op jit(solution)/shard_map/nk,pkc->npc/dot_general | solution.py:86
  157.2 8.8 %slice.28 = bf16[16,1280,240]{2,1,0:T(8,128)(2,1)} slice(bf16[16,1280,320]{2,1,0:T(8,128)(2,1)} %bitcast.33), slice={[0:16], [0:1280], [0:240]} | slice | bytes 19660800 | tf_op jit(solution)/shard_map/slice | solution.py:57
  166.0 7.4 %copy.60 = bf16[16,80,1280]{2,1,0:T(8,128)(2,1)} copy(bf16[16,80,1280]{1,2,0:T(8,128)(2,1)} %slice_bitcast_fusion) | data formatting | bytes 6553600 | tf_op jit(solution)/shard_map/nk,pkc->npc/dot_general | solution.py:86
  173.4 14.6 %copy.65 = bf16[16,1280,240]{1,2,0:T(8,128)(2,1)} copy(bf16[16,1280,240]{2,1,0:T(8,128)(2,1)} %slice.28) | data formatting | bytes 19660800
  187.9 8.1 %fusion.18 = f32[512,3840]{0,1:S(1)} fusion(bf16[1280,3840]{0,1:T(8,128)(2,1)} %bitcast.35, bf16[512,1280]{1,0:T(8,128)(2,1)S(1)} %copy-done.1, f32[1280]{0:T(1024)S(1)} %copy-done.4, f32[512]{0:T(512)S(1)} %add_rsqrt_fusion.1), kind=kOutput, calls=%fused_computation.27 | convolution fusion | flops 5035786240 | bytes 19012608
  196.7 1.8 fusion.31
  198.5 2.4 reshape.111
  200.9 3.1 %reshape.112 = bf16[8,64,16,80]{1,0,3,2:T(8,128)(2,1)S(1)} reshape(bf16[512,1280]{0,1:T(8,128)(2,1)} %get-tuple-element.8) | data formatting | bytes 2621440 | tf_op jit(solution)/shard_map/reshape | solution.py:66
  204.0 4.3 %reshape.113 = bf16[8,64,16,80]{1,0,3,2:T(8,128)(2,1)} reshape(bf16[512,1280]{0,1:T(8,128)(2,1)} %get-tuple-element.9) | data formatting | bytes 2621440 | tf_op jit(solution)/shard_map/reshape | solution.py:66
  208.3 3.0 %fusion.6 = f32[8,16,64,64]{2,3,1,0:T(8,128)S(1)} fusion(bf16[8,64,16,80]{1,0,3,2:T(8,128)(2,1)} %reshape.113, bf16[8,64,16,80]{1,0,3,2:T(8,128)(2,1)S(1)} %reshape.112), kind=kOutput, calls=%fused_computation.15 | convolution fusion | flops 83886080 | bytes 4718592 | tf_op jit(solution)/shard_map/tqhd,tkhd->thqk/dot_general | solution.py:71
  211.4 1.7 fusion.34
  213.1 1.7 fusion.11
  214.8 1.4 copy.59
  216.2 3.3 %convert_element_type.34 = bf16[512,1280]{1,0:T(8,128)(2,1)} reshape(bf16[8,64,16,80]{3,2,1,0:T(8,128)(2,1)S(1)} %copy.59) | data formatting | bytes 2621440 | tf_op jit(solution)/shard_map/convert_element_type | solution.py:85
  219.5 4.4 %multiply_reduce_fusion = (f32[512]{0:T(512)S(1)}, f32[512,1280]{1,0:T(8,128)S(1)}) fusion(bf16[512,1280]{1,0:T(8,128)(2,1)} %convert_element_type.34, bf16[1280,1280]{1,0:T(8,128)(2,1)} %bitcast.38, bf16[512,1280]{1,0:T(8,128)(2,1)S(1)} %copy-done.2), kind=kOutput, calls=%fused_computation.21 | convolution fusion | flops 1680342528 | bytes 8521728 | tf_op jit(solution)/shard_map/nk,pkc->npc/dot_general | solution.py:86
  225.0 2.1 copy.61
  227.1 8.1 %all-to-all-start.1 = ((bf16[4,32,5120]{2,0,1:T(4,128)(2,1)}), bf16[4,32,5120]{2,0,1:T(4,128)(2,1)S(1)}, u32[]{:S(2)}, u32[]{:S(2)}) async-start(bf16[4,32,5120]{2,0,1:T(4,128)(2,1)} %copy.61), calls=%async_computation.1 | async-start | bytes 2621440 | tf_op jit(solution)/shard_map/all_to_all | solution.py:95
  236.3 32.9 %all-to-all-done.1 = bf16[4,32,5120]{2,0,1:T(4,128)(2,1)S(1)} async-done(((bf16[4,32,5120]{2,0,1:T(4,128)(2,1)}), bf16[4,32,5120]{2,0,1:T(4,128)(2,1)S(1)}, u32[]{:S(2)}, u32[]{:S(2)}) %all-to-all-start.1) | async-done | bytes 1310752 | tf_op jit(solution)/shard_map/all_to_all | solution.py:95
  269.6 1.6 fusion.1
  (41 shorter events, 6.2 us)
Async XLA Ops:
  6.5 142.4 %all-gather.2.cloned.1.call-start = ((), (), s32[]{:S(2)}) async-start(), calls=%async_computation.2 | async-start | bytes 15759360 | tf_op jit(solution)/shard_map/all_gather | solution.py:52
  9.4 217.7 %all-to-all-start = ((s32[32,1,8]{2,1,0:T(1,128)}), s32[32,1,8]{2,1,0:T(1,128)S(1)}, u32[]{:S(2)}, u32[]{:S(2)}) async-start(s32[32,1,8]{2,1,0:T(1,128)} %broadcast_in_dim.83), calls=%async_computation | async-start | bytes 32768 | tf_op jit(solution)/shard_map/all_to_all | solution.py:17
  173.4 14.6 %copy-start.1 = (bf16[512,1280]{1,0:T(8,128)(2,1)S(1)}, bf16[512,1280]{1,0:T(8,128)(2,1)}, u32[]{:S(2)}) copy-start(bf16[512,1280]{1,0:T(8,128)(2,1)} %param.8) | copy-start | bytes 3932164
  173.4 14.6 %copy-start.4 = (f32[1280]{0:T(1024)S(1)}, f32[1280]{0:T(1024)}, u32[]{:S(2)}) copy-start(f32[1280]{0:T(1024)} %param.9) | copy-start | bytes 15364
  211.4 1.7 copy-start
  216.2 3.3 %copy-start.2 = (bf16[512,1280]{1,0:T(8,128)(2,1)S(1)}, bf16[512,1280]{1,0:T(8,128)(2,1)}, u32[]{:S(2)}) copy-start(bf16[512,1280]{1,0:T(8,128)(2,1)} %param.8) | copy-start | bytes 3932164
  219.5 4.4 %copy-start.3 = (f32[1280]{0:T(1024)S(1)}, f32[1280]{0:T(1024)}, u32[]{:S(2)}) copy-start(f32[1280]{0:T(1024)} %param.12) | copy-start | bytes 15364
  227.1 42.1 %all-to-all-start.1 = ((bf16[4,32,5120]{2,0,1:T(4,128)(2,1)}), bf16[4,32,5120]{2,0,1:T(4,128)(2,1)S(1)}, u32[]{:S(2)}, u32[]{:S(2)}) async-start(bf16[4,32,5120]{2,0,1:T(4,128)(2,1)} %copy.61), calls=%async_computation.1 | async-start | bytes 2621440 | tf_op jit(solution)/shard_map/all_to_all | solution.py:95
Sparse Core Ops, SparseCore 0:
  11.8 137.0 all-gather.1

commit v2 on v1

v2 whole, which is shorter than its diff:
```python
import math

import jax
import jax.numpy as jnp
from jax import lax
from jax.experimental import pallas as pl
from jax.experimental.pallas import tpu as pltpu
from jax.sharding import PartitionSpec as P

HEADS = 16
UNIT = 128

epsilon = 1e-06


def copy_for_each(x, axis):
    size = lax.axis_size(axis)
    return lax.all_to_all(jnp.broadcast_to(x[None], (size, *x.shape)), axis, 0, 0, tiled=True)


def partner_copy(x):
    size = lax.axis_size("pipe")
    return lax.ppermute(x, "pipe", [(p, p ^ 1) for p in range(size)])


def attention_kernel(
    x_ref, gain_ref, w_ref, row_ref, col_ref, out_ref, normed_ref, qkv_ref, *, head_width
):
    step = pl.program_id(0)
    chunk = w_ref.shape[1]
    part = out_ref.shape[1]

    @pl.when(step == 0)
    def _():
        x = x_ref[...].astype(jnp.float32)
        scale = lax.rsqrt(jnp.mean(x * x, axis=-1, keepdims=True) + epsilon)
        normed_ref[...] = (x * scale * gain_ref[...]).astype(jnp.bfloat16)

    qkv_ref[step] = jnp.dot(
        normed_ref[...], w_ref[...], preferred_element_type=jnp.float32
    ).astype(jnp.bfloat16)

    @pl.when(step == pl.num_programs(0) - 1)
    def _():
        def lanes(rows, first, count):
            return jnp.concatenate(
                [
                    qkv_ref[(at * 128) // chunk, rows, pl.ds((at * 128) % chunk, 128)]
                    for at in range(first // 128, (first + count) // 128)
                ],
                axis=1,
            )

        def unit(index, carry):
            rows = pl.ds(pl.multiple_of(index * UNIT, UNIT), UNIT)
            row_id = row_ref[rows, :]
            allowed = row_id == col_ref[pl.ds(index, 1), :]
            columns = [jnp.zeros((UNIT, 128), jnp.float32) for _ in range(part // 128)]
            for head in range(part // head_width):
                first = head * head_width
                base = first // 128 * 128
                count = -(-(first + head_width) // 128) * 128 - base
                lane = lax.broadcasted_iota(jnp.int32, (1, count), 1) + base
                own = (lane >= first) & (lane < first + head_width)
                query = jnp.where(own, lanes(rows, base, count), 0).astype(jnp.bfloat16)
                scores = lax.dot_general(
                    query,
                    lanes(rows, part + base, count),
                    (((1,), (1,)), ((), ())),
                    preferred_element_type=jnp.float32,
                )
                scores = jnp.where(allowed, scores, -1e30)
                highest = jnp.max(scores, axis=-1, keepdims=True)
                weights = jnp.exp((scores - highest) * (1.0 / math.sqrt(head_width)))
                weights = weights * (1.0 / jnp.sum(weights, axis=-1, keepdims=True))
                mixed = jnp.dot(
                    weights.astype(jnp.bfloat16),
                    lanes(rows, 2 * part + base, count),
                    preferred_element_type=jnp.float32,
                )
                for at in range(count // 128):
                    piece = slice(at * 128, at * 128 + 128)
                    place = base // 128 + at
                    columns[place] = jnp.where(own[:, piece], mixed[:, piece], columns[place])
            for place, column in enumerate(columns):
                out_ref[rows, place * 128 : place * 128 + 128] = jnp.where(
                    row_id >= 0, column, 0.0
                ).astype(jnp.bfloat16)
            return carry

        lax.fori_loop(0, out_ref.shape[0] // UNIT, unit, 0)


def half_attention(x, gain, w, row_id, col_id):
    count, width = x.shape
    part = w.shape[1] // 3
    chunk = 384
    head_width = width // HEADS
    whole = lambda *shape: pl.BlockSpec(shape, lambda n: (0,) * len(shape))
    return pl.pallas_call(
        lambda *refs: attention_kernel(*refs, head_width=head_width),
        grid=(w.shape[1] // chunk,),
        in_specs=[
            whole(count, width),
            whole(1, width),
            pl.BlockSpec((width, chunk), lambda n: (0, n)),
            whole(count, 1),
            whole(count // UNIT, UNIT),
        ],
        out_specs=whole(count, part),
        out_shape=jax.ShapeDtypeStruct((count, part), jnp.bfloat16),
        scratch_shapes=[
            pltpu.VMEM((count, width), jnp.bfloat16),
            pltpu.VMEM((w.shape[1] // chunk, count, chunk), jnp.bfloat16),
        ],
        compiler_params=pltpu.CompilerParams(
            dimension_semantics=("arbitrary",), vmem_limit_bytes=28 << 20
        ),
        name="half_attention",
    )(x, gain, w, row_id, col_id)


def merge_kernel(
    core_ref, own_ref, other_ref, w_own_ref, w_other_ref, x_ref, gain_ref, out_ref, hidden_ref, merged_ref
):
    core = core_ref[0]
    count, half = own_ref.shape
    width = 2 * half
    own_rows = pl.ds(pl.multiple_of(core * half, half), half)
    other_rows = pl.ds(pl.multiple_of((1 - core) * half, half), half)
    for w_ref, place in ((w_own_ref, core), (w_other_ref, 1 - core)):
        hidden_ref[place] = jnp.dot(
            own_ref[...], w_ref[own_rows, :], preferred_element_type=jnp.float32
        ) + jnp.dot(other_ref[...], w_ref[other_rows, :], preferred_element_type=jnp.float32)
    low = x_ref[:, :half].astype(jnp.float32) + hidden_ref[0]
    high = x_ref[:, half:].astype(jnp.float32) + hidden_ref[1]
    square = jnp.sum(low * low, axis=-1, keepdims=True) + jnp.sum(
        high * high, axis=-1, keepdims=True
    )
    scale = lax.rsqrt(square * (1.0 / width) + epsilon)
    merged_ref[:, :half] = (low * scale * gain_ref[:, :half]).astype(jnp.bfloat16)
    merged_ref[:, half:] = (high * scale * gain_ref[:, half:]).astype(jnp.bfloat16)
    tokens = out_ref.shape[0]
    units = count // UNIT
    to_row = lax.broadcasted_iota(jnp.int32, (tokens, count), 0)
    from_row = lax.broadcasted_iota(jnp.int32, (tokens, count), 1)
    first_row = (to_row % units) * UNIT + (to_row // units) * 4
    for member in range(4):
        choice = (from_row == first_row + member).astype(jnp.bfloat16)
        out_ref[:, member * width : (member + 1) * width] = jnp.dot(
            choice, merged_ref[...], preferred_element_type=jnp.float32
        ).astype(jnp.bfloat16)


def on_chip(x):
    return pltpu.with_memory_space_constraint(x, pltpu.VMEM)


def in_vmem(count):
    return [pl.BlockSpec(memory_space=pltpu.VMEM)] * count


def merge_tokens(core, own, other, w_own, w_other, x, gain):
    count, width = x.shape
    return pl.pallas_call(
        merge_kernel,
        in_specs=[pl.BlockSpec(memory_space=pltpu.SMEM)] + in_vmem(6),
        out_specs=pl.BlockSpec(memory_space=pltpu.VMEM),
        out_shape=jax.ShapeDtypeStruct((count // 4, 4 * width), jnp.bfloat16),
        scratch_shapes=[
            pltpu.VMEM((2, count, width // 2), jnp.float32),
            pltpu.VMEM((count, width), jnp.bfloat16),
        ],
        compiler_params=pltpu.CompilerParams(vmem_limit_bytes=28 << 20),
        name="merge_tokens",
    )(core, own, on_chip(other), w_own, on_chip(w_other), x, gain)


def unpack_kernel(core_ref, blocks_ref, qkv_ref, out_ref, full_ref, *, qkv_part):
    members, _, columns = blocks_ref.shape
    half = out_ref.shape[1]
    core = core_ref[0]
    for first, last, target in ((0, qkv_part, qkv_ref), (qkv_part, columns, out_ref)):
        pieces = [blocks_ref[p].astype(jnp.float32)[:, first:last] for p in range(members)]
        width = (last - first) * members
        full_ref[:, :width] = jnp.concatenate(pieces, axis=1)
        for at in range(width // (2 * half)):
            start = pl.multiple_of((2 * at + core) * half, 128)
            target[:, at * half : (at + 1) * half] = full_ref[:, pl.ds(start, half)].astype(
                jnp.bfloat16
            )


def unpack_weights(core, blocks, qkv_part):
    members, rows, columns = blocks.shape
    width = members * (columns - qkv_part)
    return pl.pallas_call(
        lambda *refs: unpack_kernel(*refs, qkv_part=qkv_part),
        in_specs=[pl.BlockSpec(memory_space=pltpu.SMEM)] + in_vmem(1),
        out_specs=in_vmem(2),
        out_shape=[
            jax.ShapeDtypeStruct((rows, members * qkv_part // 2), jnp.bfloat16),
            jax.ShapeDtypeStruct((rows, width // 2), jnp.bfloat16),
        ],
        scratch_shapes=[pltpu.VMEM((rows, members * qkv_part), jnp.float32)],
        compiler_params=pltpu.CompilerParams(vmem_limit_bytes=8 << 20),
        name="unpack_weights",
    )(core, on_chip(blocks))


def destination_rows(image_patches, image_sample):
    info = copy_for_each(jnp.concatenate([image_patches, image_sample]), "tensor")
    slots = image_patches.shape[0]
    units = info[:, :slots] // UNIT
    samples = info[:, slots:].reshape(-1)
    flat = units.reshape(-1)
    order = jnp.arange(flat.shape[0], dtype=jnp.int32)
    ahead = (samples[:, None] < samples[None, :]) | (
        (samples[:, None] == samples[None, :]) & (order[:, None] < order[None, :])
    )
    starts = jnp.sum(jnp.where(ahead, flat[:, None], 0), axis=0).reshape(units.shape)
    slot = jnp.arange(slots, dtype=jnp.int32)
    offsets = jnp.sum(jnp.where(slot[:, None] < slot[None, :], units[:, :, None], 0), axis=1)
    unit = slot[None, None, :]
    inside = (unit >= offsets[:, :, None]) & (unit < (offsets + units)[:, :, None])
    row = jnp.sum(jnp.where(inside, (starts - offsets)[:, :, None] + unit, 0), axis=1)
    return jnp.where(jnp.any(inside, axis=1), row, -1)


def body(patches, attn_gain, w_qkv, w_out, merge_gain, window_ids, image_patches, image_sample):
    patch_count, width = patches.shape
    token_count = patch_count // 4
    group_size = lax.axis_size("tensor")
    core = (lax.axis_index("pipe") % 2).astype(jnp.int32).reshape(1)

    blocks = copy_for_each(jnp.concatenate([w_qkv, w_out], axis=1), "pipe")
    qkv_rows, out_rows = unpack_weights(core, blocks, w_qkv.shape[1])
    w_half = lax.all_gather(qkv_rows, "tensor", axis=0, tiled=True)
    out_own = lax.all_gather(out_rows, "tensor", axis=0, tiled=True)

    live = jnp.arange(patch_count, dtype=jnp.int32) < jnp.sum(image_patches)
    ids = jnp.where(live, window_ids, -1)
    other_patches = partner_copy(patches)
    other_ids = partner_copy(ids.reshape(patch_count // UNIT, UNIT)).reshape(patch_count)
    dest_rows = destination_rows(image_patches, image_sample)

    def row_and_column(ids):
        return jnp.where(ids < 0, -2, ids)[:, None], ids.reshape(patch_count // UNIT, UNIT)

    other_patches, other_ids, dest_rows = lax.optimization_barrier(
        (other_patches, other_ids, dest_rows)
    )
    gain = attn_gain[None, :]
    sent = half_attention(other_patches, gain, w_half, *row_and_column(other_ids))
    sent, out_own = lax.optimization_barrier((sent, out_own))
    context_other = partner_copy(sent)
    out_other = partner_copy(out_own)
    context_own = half_attention(patches, gain, w_half, *row_and_column(ids))
    tokens = merge_tokens(
        core,
        context_own,
        context_other,
        out_own,
        out_other,
        patches,
        merge_gain[None, :],
    )
    outgoing = tokens.reshape(group_size, token_count // group_size, 4 * width)
    received = lax.all_to_all(outgoing, "tensor", split_axis=0, concat_axis=0, tiled=True)
    placement = (
        jnp.arange(token_count, dtype=jnp.int32)[:, None] == dest_rows.reshape(1, token_count)
    ).astype(jnp.bfloat16)
    placed = jnp.dot(
        placement, received.reshape(token_count, 4 * width), preferred_element_type=jnp.float32
    )
    return placed.astype(jnp.bfloat16).reshape(1, token_count, 1, 4 * width)


def solution(mesh):
    return jax.shard_map(
        body,
        mesh=mesh,
        in_specs=(
            P(("pipe", "tensor"), None),
            P(),
            P("tensor", "pipe"),
            P("tensor", "pipe"),
            P(),
            P(("pipe", "tensor")),
            P(("pipe", "tensor")),
            P(("pipe", "tensor")),
        ),
        out_specs=P("pipe", None, "tensor", None),
        check_vma=False,
    )
```

time: 279 us -> 284 us (1.018)
  local copies, waits for them, and re-layouts: 60.8 us -> 12.5 us
  Pallas kernels: 0 us -> 31.5 us
  waiting for transfers between devices: 154 us -> 184 us
  matrix products: 18.8 us -> 1.56 us
  starting transfers between devices: 21.5 us -> 37.6 us
  other arithmetic: 8.86 us -> 2.57 us
    pallas_call x0 -> x4, Pallas kernels: none -> 31.5 us  [the longest x2 25.7 us: half_attention(): pl.pallas_call(lambda *refs: attention_kernel(*refs, head_width=head_widt...]
    all_to_all x1 -> x2, waiting for transfers between devices: 0.01 us -> 23 us  [copy_for_each(): lax.all_to_all(jnp.broadcast_to(x[None], (size, *x.shape)), axis, 0, 0, t...]
    dot_general x2 -> x0, local copies, waits for them, and re-layouts: 15.6 us -> none  [body(): jnp.einsum('nk,pkc->npc', context, slabs[:, :, qkv_part:], preferred_elem...]
    slice x2 -> x0, local copies, waits for them, and re-layouts: 10.6 us -> none  [the longest x1 8.84 us: body(): slabs[:, :, :qkv_part]]
    ppermute x0 -> x4, starting transfers between devices: none -> 9.73 us  [partner_copy(): return lax.ppermute(x, 'pipe', [(p, p ^ 1) for p in range(size)])]
    dot_general x4 -> x1, matrix products: 10.7 us -> 1.56 us  [body(): jnp.dot(placement, received.reshape(token_count, 4 * width), preferred_el...]
    reshape x4 -> x2, local copies, waits for them, and re-layouts: 10.2 us -> 1.67 us  [the longest x1 1.35 us: body(): outgoing = tokens.reshape(group_size, token_count // group_size, 4 * width)]
    unnamed x1 -> x0, matrix products: 8.1 us -> none
  transfers between devices with their start and end apart: 3 -> 9, of which waited for: 2 -> 5; matrix products, arithmetic and copies ran while one was open for 31% -> 1% of each run, Pallas kernels for 0% -> 9%
where the time goes in v2:
time: 284 us
  waiting for transfers between devices  184 us (65%)
  starting transfers between devices  37.6 us (13%)
  Pallas kernels  31.5 us (11%)
  between operations  13.7 us (5%)
  local copies, waits for them, and re-layouts  12.5 us (4%)
    all_gather x1, waiting for transfers between devices, body(): out_own = lax.all_gather(out_rows, 'tensor', axis=0, tiled=True)  67.6 us
    all_gather x1, waiting for transfers between devices, body(): w_half = lax.all_gather(qkv_rows, 'tensor', axis=0, tiled=True)  59.3 us
    all_to_all x1, waiting for transfers between devices, body(): lax.all_to_all(outgoing, 'tensor', split_axis=0, concat_axis=0, tiled=True)  33.7 us
    pallas_call x2, Pallas kernels, half_attention(): pl.pallas_call(lambda *refs: attention_kernel(*refs, head_width=head_widt...  25.7 us
    all_to_all x2, waiting for transfers between devices, copy_for_each(): lax.all_to_all(jnp.broadcast_to(x[None], (size, *x.shape)), axis, 0, 0, t...  23 us
    all_to_all x2, starting transfers between devices, copy_for_each(): lax.all_to_all(jnp.broadcast_to(x[None], (size, *x.shape)), axis, 0, 0, t...  20.6 us
    ppermute x4, starting transfers between devices, partner_copy(): return lax.ppermute(x, 'pipe', [(p, p ^ 1) for p in range(size)])  9.73 us
    unnamed x24, local copies, waits for them, and re-layouts  8.24 us
  transfers between devices with their start and end apart: 9, of which 5 were waited for; matrix products, arithmetic and copies ran while one was open for 1% of the time, Pallas kernels for 9%

profile of v2, /device:TPU:4, one launch (start us, length us, event | category | flops | bytes accessed | tf_op | source)
XLA Modules:
  0.0 283.8 jit_solution(15386143454640362054)
XLA Ops:
  6.5 0.9 pad_maximum_fusion
  8.3 7.2 %all-to-all-start.1 = ((bf16[16,40,320]{2,1,0:T(8,128)(2,1)}), bf16[16,40,320]{2,1,0:T(8,128)(2,1)S(1)}, u32[]{:S(2)}, u32[]{:S(2)}) async-start(bf16[16,40,320]{2,1,0:T(8,128)(2,1)} %broadcast_in_dim.86), calls=%async_computation.1 | async-start | bytes 983040 | tf_op jit(solution)/shard_map/all_to_all | solution.py:18
  15.6 15.3 %all-to-all-done.1.refs_1_ = bf16[16,40,320]{2,1,0:T(8,128)(2,1)S(1)} async-done(((bf16[16,40,320]{2,1,0:T(8,128)(2,1)}), bf16[16,40,320]{2,1,0:T(8,128)(2,1)S(1)}, u32[]{:S(2)}, u32[]{:S(2)}) %all-to-all-start.1) | async-done | bytes 409632 | tf_op jit(solution)/shard_map/all_to_all | solution.py:18
  30.9 0.9 unpack_weights.1
  32.5 3.5 %collective-permute-start = (bf16[512,1280]{1,0:T(8,128)(2,1)S(1)}, bf16[512,1280]{1,0:T(8,128)(2,1)S(1)}, u32[]{:S(2)}, u32[]{:S(2)}) collective-permute-start(bf16[512,1280]{1,0:T(8,128)(2,1)S(1)} %copy-done.2), channel_id=1, source_target_pairs={{0,32},{32,0},{64,96},{96,64},{128,160},{160,128},{192,224},{224,1... | collective-permute-start | bytes 3932168 | tf_op jit(solution)/shard_map/ppermute | solution.py:23
  37.3 1.9 collective-permute-start.1
  40.0 13.4 %all-to-all-start = ((s32[32,1,8]{2,1,0:T(1,128)}), s32[32,1,8]{2,1,0:T(1,128)S(1)}, u32[]{:S(2)}, u32[]{:S(2)}) async-start(s32[32,1,8]{2,1,0:T(1,128)} %broadcast_in_dim.79), calls=%async_computation | async-start | bytes 32768 | tf_op jit(solution)/shard_map/all_to_all | solution.py:18
  53.4 7.7 %all-to-all-done = s32[32,1,8]{2,1,0:T(1,128)S(1)} async-done(((s32[32,1,8]{2,1,0:T(1,128)}), s32[32,1,8]{2,1,0:T(1,128)S(1)}, u32[]{:S(2)}, u32[]{:S(2)}) %all-to-all-start) | async-done | bytes 1056 | tf_op jit(solution)/shard_map/all_to_all | solution.py:18
  62.3 59.3 %all-gather.3.cloned.1.call-done.refs_2_ = bf16[1280,1920]{1,0:T(8,128)(2,1)} async-done(((bf16[40,1920]{1,0:T(8,128)(2,1)}), bf16[1280,1920]{1,0:T(8,128)(2,1)}) %all-gather.3.cloned.1.call-update) | async-done | bytes 4915216 | tf_op jit(solution)/shard_map/all_gather | solution.py:238
  121.6 2.4 copy-done
  124.0 12.8 %half_attention.3 = bf16[512,640]{1,0:T(8,128)(2,1)S(1)} custom-call(bf16[512,1280]{1,0:T(8,128)(2,1)S(1)} %collective-permute-done.refs_0_, f32[1,1280]{1,0:T(1,128)S(1)} %broadcast_in_dim.85.refs_1_, bf16[1280,1920]{1,0:T(8,128)(2,1)S(1)} %copy-done, s32[512,1]{1,0:T(8,128)S(1)} %copy.19.refs_3_, s32[4,128]{1,0:T(4,128)S(1)} %collective-permute-done.1), custom_call_target="tpu_custom_call" | custom-call | tf_op jit(solution)/shard_map/half_attention/pallas_call | solution.py:100
  136.9 0.8 copy-done.6
  137.7 67.6 %all-gather.5.cloned.1.call-done.w_own_ref = bf16[1280,640]{1,0:T(8,128)(2,1)} async-done(((bf16[40,640]{1,0:T(8,128)(2,1)}), bf16[1280,640]{1,0:T(8,128)(2,1)}) %all-gather.5.cloned.1.call-update) | async-done | bytes 1638416 | tf_op jit(solution)/shard_map/all_gather | solution.py:239
  205.3 1.9 collective-permute-start.3
  207.2 2.4 collective-permute-start.2
  209.8 2.4 copy-done.1
  212.2 12.8 %half_attention.2.own_ref = bf16[512,640]{1,0:T(8,128)(2,1)S(1)} custom-call(bf16[512,1280]{1,0:T(8,128)(2,1)S(1)} %copy-done.2, f32[1,1280]{1,0:T(1,128)S(1)} %broadcast_in_dim.85.refs_1_, bf16[1280,1920]{1,0:T(8,128)(2,1)S(1)} %copy-done.1, s32[512,1]{1,0:T(8,128)S(1)} %copy.18.refs_3_, s32[4,128]{1,0:T(4,128)S(1)} %get-tuple-element.25.refs_4_), custom_call_target="tpu_custom_call" | custom-call | tf_op jit(solution)/shard_map/half_attention/pallas_call | solution.py:100
  225.1 1.2 copy-done.4
  226.2 1.4 copy-done.5
  227.7 5.0 %merge_tokens.1 = bf16[128,5120]{1,0:T(8,128)(2,1)S(1)} custom-call(s32[1]{0:T(128)} %bitcast.3.refs_0_.core_ref, bf16[512,640]{1,0:T(8,128)(2,1)S(1)} %half_attention.2.own_ref, bf16[512,640]{1,0:T(8,128)(2,1)} %collective-permute-done.2.other_ref, bf16[1280,640]{1,0:T(8,128)(2,1)S(1)} %copy-done.3, bf16[1280,640]{1,0:T(8,128)(2,1)S(1)} %copy-done.5, ...), custom_call_target="tpu_custom_call" | custom-call | tf_op jit(solution)/shard_map/merge_tokens/pallas_call | solution.py:165
  232.7 1.3 reshape.52
  234.0 7.2 %all-to-all-start.2 = ((bf16[32,4,5120]{2,1,0:T(4,128)(2,1)}), bf16[32,4,5120]{2,1,0:T(4,128)(2,1)S(1)}, u32[]{:S(2)}, u32[]{:S(2)}) async-start(bf16[32,4,5120]{2,1,0:T(4,128)(2,1)} %reshape.52), calls=%async_computation.2 | async-start | bytes 2621440 | tf_op jit(solution)/shard_map/all_to_all | solution.py:269
  241.4 33.7 %all-to-all-done.2 = bf16[32,4,5120]{2,1,0:T(4,128)(2,1)S(1)} async-done(((bf16[32,4,5120]{2,1,0:T(4,128)(2,1)}), bf16[32,4,5120]{2,1,0:T(4,128)(2,1)S(1)}, u32[]{:S(2)}, u32[]{:S(2)}) %all-to-all-start.2) | async-done | bytes 1310752 | tf_op jit(solution)/shard_map/all_to_all | solution.py:269
  275.4 1.6 fusion
  (55 shorter events, 5.4 us)
Async XLA Ops:
  6.5 26.0 %copy-start.2 = (bf16[512,1280]{1,0:T(8,128)(2,1)S(1)}, bf16[512,1280]{1,0:T(8,128)(2,1)}, u32[]{:S(2)}) copy-start(bf16[512,1280]{1,0:T(8,128)(2,1)} %x_ref.1) | copy-start | bytes 3932164
  6.5 29.5 %copy-start.10 = (s32[4]{0:T(128)S(1)}, s32[4]{0:T(128)}, u32[]{:S(2)}) copy-start(s32[4]{0:T(128)} %param.14) | copy-start | bytes 52
  6.5 30.1 %copy-start.9 = (s32[512]{0:T(512)S(1)}, s32[512]{0:T(512)}, u32[]{:S(2)}) copy-start(s32[512]{0:T(512)} %param.13) | copy-start | bytes 6148
  6.5 32.7 %copy-start.11 = (s32[4]{0:T(128)S(1)}, s32[4]{0:T(128)}, u32[]{:S(2)}) copy-start(s32[4]{0:T(128)} %param.15) | copy-start | bytes 52
  6.5 46.9 %copy-start.7 = (f32[1280]{0:T(1024)S(1)}, f32[1280]{0:T(1024)}, u32[]{:S(2)}) copy-start(f32[1280]{0:T(1024)} %param.9) | copy-start | bytes 15364
  8.3 22.6 %all-to-all-start.1 = ((bf16[16,40,320]{2,1,0:T(8,128)(2,1)}), bf16[16,40,320]{2,1,0:T(8,128)(2,1)S(1)}, u32[]{:S(2)}, u32[]{:S(2)}) async-start(bf16[16,40,320]{2,1,0:T(8,128)(2,1)} %broadcast_in_dim.86), calls=%async_computation.1 | async-start | bytes 983040 | tf_op jit(solution)/shard_map/all_to_all | solution.py:18
  15.5 106.1 %all-gather.3.cloned.1.call-start = ((), (), s32[]{:S(2)}) async-start(), calls=%async_computation.3 | async-start | bytes 5068800 | tf_op jit(solution)/shard_map/all_gather | solution.py:238
  31.8 173.5 %all-gather.5.cloned.1.call-start = ((), (), s32[]{:S(2)}) async-start(), calls=%async_computation.4 | async-start | bytes 1689600 | tf_op jit(solution)/shard_map/all_gather | solution.py:239
  32.5 29.6 %collective-permute-start = (bf16[512,1280]{1,0:T(8,128)(2,1)S(1)}, bf16[512,1280]{1,0:T(8,128)(2,1)S(1)}, u32[]{:S(2)}, u32[]{:S(2)}) collective-permute-start(bf16[512,1280]{1,0:T(8,128)(2,1)S(1)} %copy-done.2), channel_id=1, source_target_pairs={{0,32},{32,0},{64,96},{96,64},{128,160},{160,128},{192,224},{224,1... | collective-permute-start | bytes 3932168 | tf_op jit(solution)/shard_map/ppermute | solution.py:23
  37.3 24.8 %collective-permute-start.1 = (s32[4,128]{1,0:T(4,128)S(1)}, s32[4,128]{1,0:T(4,128)S(1)}, u32[]{:S(2)}, u32[]{:S(2)}) collective-permute-start(s32[4,128]{1,0:T(4,128)S(1)} %get-tuple-element.25.refs_4_), channel_id=1, source_target_pairs={{0,32},{32,0},{64,96},{96,64},{128,160},{160,128},{192,224},{224,1... | collective-permute-start | bytes 6152 | tf_op jit(solution)/shard_map/ppermute | solution.py:23
  40.0 21.2 %all-to-all-start = ((s32[32,1,8]{2,1,0:T(1,128)}), s32[32,1,8]{2,1,0:T(1,128)S(1)}, u32[]{:S(2)}, u32[]{:S(2)}) async-start(s32[32,1,8]{2,1,0:T(1,128)} %broadcast_in_dim.79), calls=%async_computation | async-start | bytes 32768 | tf_op jit(solution)/shard_map/all_to_all | solution.py:18
  121.6 2.4 copy-start
  124.0 85.8 %copy-start.8 = (f32[1280]{0:T(1024)S(1)}, f32[1280]{0:T(1024)}, u32[]{:S(2)}) copy-start(f32[1280]{0:T(1024)} %param.12) | copy-start | bytes 15364
  136.9 0.8 copy-start.6
  205.3 19.8 %collective-permute-start.3 = (bf16[1280,640]{1,0:T(8,128)(2,1)}, bf16[1280,640]{1,0:T(8,128)(2,1)S(1)}, u32[]{:S(2)}, u32[]{:S(2)}) collective-permute-start(bf16[1280,640]{1,0:T(8,128)(2,1)} %all-gather.5.cloned.1.call-done.w_own_ref), channel_id=1, source_target_pairs={{0,32},{32,0},{64,96},{96,64},{128,160},{160,128},{192,224},{224,1... | collective-permute-start | bytes 4915208 | tf_op jit(solution)/shard_map/ppermute | solution.py:23
  207.2 17.8 %collective-permute-start.2 = (bf16[512,640]{1,0:T(8,128)(2,1)}, bf16[512,640]{1,0:T(8,128)(2,1)}, u32[]{:S(2)}, u32[]{:S(2)}) collective-permute-start(bf16[512,640]{1,0:T(8,128)(2,1)} %copy-done.6), channel_id=1, source_target_pairs={{0,32},{32,0},{64,96},{96,64},{128,160},{160,128},{192,224},{224,1... | collective-permute-start | bytes 1966088 | tf_op jit(solution)/shard_map/ppermute | solution.py:23
  209.8 2.4 copy-start.1
  212.2 14.1 %copy-start.3 = (bf16[1280,640]{1,0:T(8,128)(2,1)S(1)}, bf16[1280,640]{1,0:T(8,128)(2,1)}, u32[]{:S(2)}) copy-start(bf16[1280,640]{1,0:T(8,128)(2,1)} %all-gather.5.cloned.1.call-done.w_own_ref) | copy-start | bytes 4915204
  225.1 1.2 copy-start.4
  226.2 1.4 copy-start.5
  234.0 41.1 %all-to-all-start.2 = ((bf16[32,4,5120]{2,1,0:T(4,128)(2,1)}), bf16[32,4,5120]{2,1,0:T(4,128)(2,1)S(1)}, u32[]{:S(2)}, u32[]{:S(2)}) async-start(bf16[32,4,5120]{2,1,0:T(4,128)(2,1)} %reshape.52), calls=%async_computation.2 | async-start | bytes 2621440 | tf_op jit(solution)/shard_map/all_to_all | solution.py:269
Sparse Core Ops, SparseCore 0:
  31.9 89.6 all-gather.2
  124.8 80.4 all-gather.4

commit v3 on v2

v3 whole, which is shorter than its diff:
```python
import math

import jax
import jax.numpy as jnp
from jax import lax
from jax.experimental import pallas as pl
from jax.experimental.pallas import tpu as pltpu
from jax.sharding import PartitionSpec as P

HEADS = 16
UNIT = 128

epsilon = 1e-06


def copy_for_each(x, axis):
    size = lax.axis_size(axis)
    return lax.all_to_all(jnp.broadcast_to(x[None], (size, *x.shape)), axis, 0, 0, tiled=True)


def partner_copy(x):
    size = lax.axis_size("pipe")
    return lax.ppermute(x, "pipe", [(p, p ^ 1) for p in range(size)])


def attention_kernel(
    x_ref, gain_ref, w_ref, row_ref, col_ref, out_ref, normed_ref, wide_ref, heads_ref, *, head_width
):
    step = pl.program_id(0)
    columns = w_ref.shape[1]
    count, width = x_ref.shape
    head_count = width // head_width
    in_block = columns // head_width

    @pl.when(step == 0)
    def _():
        x = x_ref[...].astype(jnp.float32)
        scale = lax.rsqrt(jnp.mean(x * x, axis=-1, keepdims=True) + epsilon)
        normed_ref[...] = (x * scale * gain_ref[...]).astype(jnp.bfloat16)

    wide_ref[:, :columns] = lax.dot_general(
        normed_ref[...],
        w_ref[0],
        (((1,), (1,)), ((), ())),
        preferred_element_type=jnp.float32,
    ).astype(jnp.bfloat16).astype(jnp.float32)
    lane = lax.broadcasted_iota(jnp.int32, (1, 128), 1)
    for piece in range(in_block):
        part = step * in_block + piece
        offset = jnp.where(part < 2 * head_count, 0, (part - 2 * head_count) * head_width % 128)
        shift = (offset - piece * head_width + 256) % 256
        moved = pltpu.roll(wide_ref[...], shift, axis=1)
        end = offset + head_width
        heads_ref[part] = jnp.where(
            (lane >= offset) & (lane < end),
            moved[:, :128],
            jnp.where(lane < end - 128, moved[:, 128:], 0.0),
        ).astype(jnp.bfloat16)

    @pl.when(step == pl.num_programs(0) - 1)
    def _():
        def unit(index, carry):
            rows = pl.ds(pl.multiple_of(index * UNIT, UNIT), UNIT)
            row_id = row_ref[rows, :]
            live = row_id >= 0
            allowed = row_id == col_ref[pl.ds(index, 1), :]

            def group(number, carry):
                column = jnp.zeros((UNIT, 128), jnp.float32)
                for at in range(8):
                    head = number * 8 + at
                    scores = lax.dot_general(
                        heads_ref[head, rows, :],
                        heads_ref[head_count + head, rows, :],
                        (((1,), (1,)), ((), ())),
                        preferred_element_type=jnp.float32,
                    )
                    scores = jnp.where(allowed, scores, -1e30)
                    highest = jnp.max(scores, axis=-1, keepdims=True)
                    weights = jnp.exp2(
                        (scores - highest) * (1.0 / (math.sqrt(head_width) * math.log(2.0)))
                    )
                    weights = weights * (1.0 / jnp.sum(weights, axis=-1, keepdims=True))
                    mixed = jnp.dot(
                        weights.astype(jnp.bfloat16),
                        heads_ref[2 * head_count + head, rows, :],
                        preferred_element_type=jnp.float32,
                    )
                    first = at * head_width % 128
                    place = at * head_width // 128
                    column = jnp.where(lane >= first, mixed, column)
                    if first + head_width >= 128:
                        start = pl.multiple_of(number * 8 * head_width + place * 128, 128)
                        out_ref[rows, pl.ds(start, 128)] = jnp.where(live, column, 0.0).astype(
                            jnp.bfloat16
                        )
                        column = mixed
                return carry

            return lax.fori_loop(0, head_count // 8, group, carry)

        lax.fori_loop(0, count // UNIT, unit, 0)


def attention(x, gain, slabs, row_id, col_id):
    count, width = x.shape
    blocks, columns, _ = slabs.shape
    head_width = width // HEADS
    whole = lambda *shape: pl.BlockSpec(shape, lambda n: (0,) * len(shape))
    return pl.pallas_call(
        lambda *refs: attention_kernel(*refs, head_width=head_width),
        grid=(blocks,),
        in_specs=[
            whole(count, width),
            whole(1, width),
            pl.BlockSpec((1, columns, width), lambda n: (n, 0, 0)),
            whole(count, 1),
            whole(count // UNIT, UNIT),
        ],
        out_specs=whole(count, width),
        out_shape=jax.ShapeDtypeStruct((count, width), jnp.bfloat16),
        scratch_shapes=[
            pltpu.VMEM((count, width), jnp.bfloat16),
            pltpu.VMEM((count, 256), jnp.float32),
            pltpu.VMEM((3 * HEADS, count, 128), jnp.bfloat16),
        ],
        compiler_params=pltpu.CompilerParams(
            dimension_semantics=("arbitrary",), vmem_limit_bytes=32 << 20
        ),
        name="attention",
    )(x, gain, pltpu.with_memory_space_constraint(slabs, pltpu.HBM), row_id, col_id)


def merge_kernel(
    core_ref, context_ref, w_own_ref, w_other_ref, x_ref, gain_ref, out_ref, hidden_ref, merged_ref
):
    core = core_ref[0]
    count, width = context_ref.shape
    half = width // 2
    for w_ref, place in ((w_own_ref, core), (w_other_ref, 1 - core)):
        hidden_ref[place] = jnp.dot(
            context_ref[...], w_ref[...], preferred_element_type=jnp.float32
        )
    low = x_ref[:, :half].astype(jnp.float32) + hidden_ref[0]
    high = x_ref[:, half:].astype(jnp.float32) + hidden_ref[1]
    square = jnp.sum(low * low, axis=-1, keepdims=True) + jnp.sum(
        high * high, axis=-1, keepdims=True
    )
    scale = lax.rsqrt(square * (1.0 / width) + epsilon)
    merged_ref[:, :half] = (low * scale * gain_ref[:, :half]).astype(jnp.bfloat16)
    merged_ref[:, half:] = (high * scale * gain_ref[:, half:]).astype(jnp.bfloat16)
    tokens = out_ref.shape[0]
    units = count // UNIT
    to_row = lax.broadcasted_iota(jnp.int32, (tokens, count), 0)
    from_row = lax.broadcasted_iota(jnp.int32, (tokens, count), 1)
    first_row = (to_row % units) * UNIT + (to_row // units) * 4
    for member in range(4):
        choice = (from_row == first_row + member).astype(jnp.bfloat16)
        out_ref[:, member * width : (member + 1) * width] = jnp.dot(
            choice, merged_ref[...], preferred_element_type=jnp.float32
        ).astype(jnp.bfloat16)


def on_chip(x):
    return pltpu.with_memory_space_constraint(x, pltpu.VMEM)


def in_vmem(count):
    return [pl.BlockSpec(memory_space=pltpu.VMEM)] * count


def merge_tokens(core, context, w_own, w_other, x, gain):
    count, width = x.shape
    return pl.pallas_call(
        merge_kernel,
        in_specs=[pl.BlockSpec(memory_space=pltpu.SMEM)] + in_vmem(5),
        out_specs=pl.BlockSpec(memory_space=pltpu.VMEM),
        out_shape=jax.ShapeDtypeStruct((count // 4, 4 * width), jnp.bfloat16),
        scratch_shapes=[
            pltpu.VMEM((2, count, width // 2), jnp.float32),
            pltpu.VMEM((count, width), jnp.bfloat16),
        ],
        compiler_params=pltpu.CompilerParams(vmem_limit_bytes=28 << 20),
        name="merge_tokens",
    )(core, context, on_chip(w_own), on_chip(w_other), x, gain)


def destination_rows(units, samples):
    slots = units.shape[1]
    samples = samples.reshape(-1)
    flat = units.reshape(-1)
    order = jnp.arange(flat.shape[0], dtype=jnp.int32)
    ahead = (samples[:, None] < samples[None, :]) | (
        (samples[:, None] == samples[None, :]) & (order[:, None] < order[None, :])
    )
    starts = jnp.sum(jnp.where(ahead, flat[:, None], 0), axis=0).reshape(units.shape)
    slot = jnp.arange(slots, dtype=jnp.int32)
    offsets = jnp.sum(jnp.where(slot[:, None] < slot[None, :], units[:, :, None], 0), axis=1)
    unit = slot[None, None, :]
    inside = (unit >= offsets[:, :, None]) & (unit < (offsets + units)[:, :, None])
    row = jnp.sum(jnp.where(inside, (starts - offsets)[:, :, None] + unit, 0), axis=1)
    return jnp.where(jnp.any(inside, axis=1), row, -1)


def body(patches, attn_gain, w_qkv, w_out, merge_gain, window_ids, image_patches, image_sample):
    patch_count, width = patches.shape
    token_count = patch_count // 4
    group_size = lax.axis_size("tensor")
    core = (lax.axis_index("pipe") % 2).astype(jnp.int32).reshape(1)

    half = width // 2
    slots = image_patches.shape[0]
    row_count, qkv_part = w_qkv.shape

    info = jnp.concatenate([image_patches // UNIT, image_sample]).astype(jnp.bfloat16)
    info = jnp.broadcast_to(info[None], (row_count, 2 * slots))
    rows = copy_for_each(jnp.concatenate([w_qkv, info], axis=1), "tensor")
    slab = rows[:, :, :qkv_part].reshape(width, qkv_part).T
    slabs = lax.all_gather(slab, "pipe", axis=0, tiled=False)
    info = rows[:, 0, qkv_part:].astype(jnp.int32)
    dest_rows = destination_rows(info[:, :slots], info[:, slots:])

    slab, w_out = lax.optimization_barrier((slab, w_out))
    blocks = copy_for_each(w_out, "pipe")
    out_rows = jnp.moveaxis(blocks, 0, 1).reshape(row_count, 2, half)
    out_rows = lax.dynamic_index_in_dim(out_rows, core[0], axis=1, keepdims=False)
    out_own = copy_for_each(out_rows, "tensor").reshape(width, half)
    out_other = partner_copy(out_own)

    live = jnp.arange(patch_count, dtype=jnp.int32) < jnp.sum(image_patches)
    ids = jnp.where(live, window_ids, -1)
    ids, dest_rows, out_own = lax.optimization_barrier((ids, dest_rows, out_own))
    context = attention(
        patches,
        attn_gain[None, :],
        slabs,
        jnp.where(ids < 0, -2, ids)[:, None],
        ids.reshape(patch_count // UNIT, UNIT),
    )
    tokens = merge_tokens(core, context, out_own, out_other, patches, merge_gain[None, :])
    outgoing = tokens.reshape(group_size, token_count // group_size, 4 * width)
    received = lax.all_to_all(outgoing, "tensor", split_axis=0, concat_axis=0, tiled=True)
    placement = (
        jnp.arange(token_count, dtype=jnp.int32)[:, None] == dest_rows.reshape(1, token_count)
    ).astype(jnp.bfloat16)
    placed = jnp.dot(
        placement, received.reshape(token_count, 4 * width), preferred_element_type=jnp.float32
    )
    return placed.astype(jnp.bfloat16).reshape(1, token_count, 1, 4 * width)


def solution(mesh):
    return jax.shard_map(
        body,
        mesh=mesh,
        in_specs=(
            P(("pipe", "tensor"), None),
            P(),
            P("tensor", "pipe"),
            P("tensor", "pipe"),
            P(),
            P(("pipe", "tensor")),
            P(("pipe", "tensor")),
            P(("pipe", "tensor")),
        ),
        out_specs=P("pipe", None, "tensor", None),
        check_vma=False,
    )
```

time: 284 us -> 209 us (0.74)
  waiting for transfers between devices: 184 us -> 85.7 us
  blocking collectives: 0 us -> 32.9 us
  starting transfers between devices: 37.6 us -> 20.1 us
  Pallas kernels: 31.5 us -> 43.1 us
  local copies, waits for them, and re-layouts: 12.5 us -> 7.18 us
    all_gather x2 -> x1, waiting for transfers between devices: 127 us -> 0.02 us  [body(): slabs = lax.all_gather(slab, 'pipe', axis=0, tiled=False)]
    all_to_all x0 -> x1, blocking collectives: none -> 32.9 us  [copy_for_each(): lax.all_to_all(jnp.broadcast_to(x[None], (size, *x.shape)), axis, 0, 0, t...]
    all_to_all x2, waiting for transfers between devices: 23 us -> 51.6 us  [copy_for_each(): lax.all_to_all(jnp.broadcast_to(x[None], (size, *x.shape)), axis, 0, 0, t...]
    pallas_call x3 -> x1, Pallas kernels: 26.5 us -> 38 us  [attention(): pl.pallas_call(lambda *refs: attention_kernel(*refs, head_width=head_widt...]
    unnamed x24 -> x16, local copies, waits for them, and re-layouts: 8.24 us -> 0.12 us
    all_to_all x2, starting transfers between devices: 20.6 us -> 12.6 us  [copy_for_each(): lax.all_to_all(jnp.broadcast_to(x[None], (size, *x.shape)), axis, 0, 0, t...]
    ppermute x4 -> x1, starting transfers between devices: 9.73 us -> 2.01 us  [partner_copy(): return lax.ppermute(x, 'pipe', [(p, p ^ 1) for p in range(size)])]
  transfers between devices with their start and end apart: 9 -> 5, of which waited for: 5 -> 3; matrix products, arithmetic and copies ran while one was open for 1% -> 3% of each run, Pallas kernels for 9% -> 18%
where the time goes in v3:
time: 209 us; the launch traced here: 208 us
  waiting for transfers between devices  85.7 us (41%)
  Pallas kernels  43.1 us (21%)
  blocking collectives  32.9 us (16%)
  starting transfers between devices  20.1 us (10%)
  between operations  13.7 us (7%)
  local copies, waits for them, and re-layouts  7.18 us (3%)
  other arithmetic  3.69 us (2%)
    all_to_all x2, waiting for transfers between devices, copy_for_each(): lax.all_to_all(jnp.broadcast_to(x[None], (size, *x.shape)), axis, 0, 0, t...  51.6 us
    pallas_call x1, Pallas kernels, attention(): pl.pallas_call(lambda *refs: attention_kernel(*refs, head_width=head_widt...  38 us
    all_to_all x1, waiting for transfers between devices, body(): lax.all_to_all(outgoing, 'tensor', split_axis=0, concat_axis=0, tiled=True)  34.1 us
    all_to_all x1, blocking collectives, copy_for_each(): lax.all_to_all(jnp.broadcast_to(x[None], (size, *x.shape)), axis, 0, 0, t...  32.9 us
    all_to_all x2, starting transfers between devices, copy_for_each(): lax.all_to_all(jnp.broadcast_to(x[None], (size, *x.shape)), axis, 0, 0, t...  12.6 us
    all_to_all x1, starting transfers between devices, body(): lax.all_to_all(outgoing, 'tensor', split_axis=0, concat_axis=0, tiled=True)  5.43 us
    pallas_call x1, Pallas kernels, merge_tokens(): pl.pallas_call(merge_kernel, in_specs=[pl.BlockSpec(memory_space=pltpu.SM...  5.09 us
  transfers between devices with their start and end apart: 5, of which 3 were waited for; matrix products, arithmetic and copies ran while one was open for 3% of the time, Pallas kernels for 18%

profile of v3, /device:TPU:4, one launch (start us, length us, event | category | flops | bytes accessed | tf_op | source)
XLA Modules:
  0.0 207.9 jit_solution(27454748657252715)
XLA Ops:
  6.5 1.3 fusion.8
  7.8 0.7 convert.8
  8.6 0.7 pad_maximum_fusion
  9.4 32.9 %all_to_all.20 = bf16[32,40,248]{2,1,0:T(8,128)(2,1)S(1)} all-to-all(bf16[32,40,248]{2,1,0:T(8,128)(2,1)S(1)} %broadcast_in_dim.92), channel_id=1, replica_groups=mesh['pipe'=16,'tensor'=32] {'tensor'}, dimensions={0} | all-to-all | bytes 1269760 | tf_op jit(solution)/shard_map/all_to_all | solution.py:18
  42.3 1.1 copy.25
  43.4 0.7 broadcast_in_dim.99
  44.1 7.2 %all-to-all-start.1 = ((bf16[16,40,80]{2,1,0:T(8,128)(2,1)}), bf16[16,40,80]{2,1,0:T(8,128)(2,1)S(1)}, u32[]{:S(2)}, u32[]{:S(2)}) async-start(bf16[16,40,80]{2,1,0:T(8,128)(2,1)} %broadcast_in_dim.99), calls=%async_computation.1 | async-start | bytes 327680 | tf_op jit(solution)/shard_map/all_to_all | solution.py:18
  51.3 9.5 %all-to-all-done.1 = bf16[16,40,80]{2,1,0:T(8,128)(2,1)S(1)} async-done(((bf16[16,40,80]{2,1,0:T(8,128)(2,1)}), bf16[16,40,80]{2,1,0:T(8,128)(2,1)S(1)}, u32[]{:S(2)}, u32[]{:S(2)}) %all-to-all-start.1) | async-done | bytes 102432 | tf_op jit(solution)/shard_map/all_to_all | solution.py:18
  60.8 0.3 reshape.65
  61.2 1.3 broadcast_in_dim.101
  62.5 5.4 %all-to-all-start.2 = ((bf16[32,40,640]{2,1,0:T(8,128)(2,1)}), bf16[32,40,640]{2,1,0:T(8,128)(2,1)S(1)}, u32[]{:S(2)}, u32[]{:S(2)}) async-start(bf16[32,40,640]{2,1,0:T(8,128)(2,1)} %broadcast_in_dim.101), calls=%async_computation.2 | async-start | bytes 3276800 | tf_op jit(solution)/shard_map/all_to_all | solution.py:18
  68.0 42.1 %all-to-all-done.2 = bf16[32,40,640]{2,1,0:T(8,128)(2,1)S(1)} async-done(((bf16[32,40,640]{2,1,0:T(8,128)(2,1)}), bf16[32,40,640]{2,1,0:T(8,128)(2,1)S(1)}, u32[]{:S(2)}, u32[]{:S(2)}) %all-to-all-start.2) | async-done | bytes 1638432 | tf_op jit(solution)/shard_map/all_to_all | solution.py:18
  110.1 2.0 collective-permute-start
  112.2 0.6 fusion.5
  112.8 0.9 slice.16
  114.3 0.1 select_reduce_fusion
  114.7 0.1 copy.26.refs_3_
  114.9 38.0 %attention.1.context_ref = bf16[512,1280]{1,0:T(8,128)(2,1)S(1)} custom-call(bf16[512,1280]{1,0:T(8,128)(2,1)S(1)} %copy-done, f32[1,1280]{1,0:T(1,128)S(1)} %broadcast_in_dim.102.refs_1_, bf16[16,240,1280]{2,1,0:T(8,128)(2,1)} %bitcast.22, s32[512,1]{1,0:T(8,128)S(1)} %copy.26.refs_3_, s32[4,128]{1,0:T(4,128)S(1)} %bitcast.21), custom_call_target="tpu_custom_call" | custom-call | tf_op jit(solution)/shard_map/attention/pallas_call | solution.py:110
  152.9 5.1 %merge_tokens.1 = bf16[128,5120]{1,0:T(8,128)(2,1)S(1)} custom-call(s32[1]{0:T(128)} %bitcast.6.core_ref, bf16[512,1280]{1,0:T(8,128)(2,1)S(1)} %attention.1.context_ref, bf16[1280,640]{1,0:T(8,128)(2,1)S(1)} %bitcast.20, bf16[1280,640]{1,0:T(8,128)(2,1)} %collective-permute-done.w_other_ref, bf16[512,1280]{1,0:T(8,128)(2,1)S(1)} %copy-done.1, ...), custom_call_target="tpu_custom_call" | custom-call | tf_op jit(solution)/shard_map/merge_tokens/pallas_call | solution.py:174
  158.0 1.3 reshape.69
  159.4 5.4 %all-to-all-start.3 = ((bf16[32,4,5120]{2,1,0:T(4,128)(2,1)}), bf16[32,4,5120]{2,1,0:T(4,128)(2,1)S(1)}, u32[]{:S(2)}, u32[]{:S(2)}) async-start(bf16[32,4,5120]{2,1,0:T(4,128)(2,1)} %reshape.69), calls=%async_computation.3 | async-start | bytes 2621440 | tf_op jit(solution)/shard_map/all_to_all | solution.py:242
  165.0 34.1 %all-to-all-done.3 = bf16[32,4,5120]{2,1,0:T(4,128)(2,1)S(1)} async-done(((bf16[32,4,5120]{2,1,0:T(4,128)(2,1)}), bf16[32,4,5120]{2,1,0:T(4,128)(2,1)S(1)}, u32[]{:S(2)}, u32[]{:S(2)}) %all-to-all-start.3) | async-done | bytes 1310752 | tf_op jit(solution)/shard_map/all_to_all | solution.py:242
  199.1 0.3 reshape.70
  199.5 1.6 fusion
  (44 shorter events, 1.4 us)
Async XLA Ops:
  6.5 108.3 %all-gather.3.cloned.1.call-start = ((), (), s32[]{:S(2)}) async-start(), calls=%async_computation.4 | async-start | bytes 10444800 | tf_op jit(solution)/shard_map/all_gather | solution.py:219
  9.4 34.0 %copy-start.3 = (bf16[40,80]{1,0:T(8,128)(2,1)S(1)}, bf16[40,80]{1,0:T(8,128)(2,1)}, u32[]{:S(2)}) copy-start(bf16[40,80]{1,0:T(8,128)(2,1)} %param.11) | copy-start | bytes 19204
  42.3 18.5 %copy-start.2 = (bf16[32,40,248]{2,1,0:T(8,128)(2,1)}, bf16[32,40,248]{2,1,0:T(8,128)(2,1)S(1)}, u32[]{:S(2)}) copy-start(bf16[32,40,248]{2,1,0:T(8,128)(2,1)S(1)} %all_to_all.20) | copy-start | bytes 1904644
  44.1 16.7 %all-to-all-start.1 = ((bf16[16,40,80]{2,1,0:T(8,128)(2,1)}), bf16[16,40,80]{2,1,0:T(8,128)(2,1)S(1)}, u32[]{:S(2)}, u32[]{:S(2)}) async-start(bf16[16,40,80]{2,1,0:T(8,128)(2,1)} %broadcast_in_dim.99), calls=%async_computation.1 | async-start | bytes 327680 | tf_op jit(solution)/shard_map/all_to_all | solution.py:18
  62.5 5.5 %copy-start.4 = (f32[1280]{0:T(1024)S(1)}, f32[1280]{0:T(1024)}, u32[]{:S(2)}) copy-start(f32[1280]{0:T(1024)} %param.9) | copy-start | bytes 15364
  62.5 5.5 %copy-start.5 = (f32[1280]{0:T(1024)S(1)}, f32[1280]{0:T(1024)}, u32[]{:S(2)}) copy-start(f32[1280]{0:T(1024)} %param.12) | copy-start | bytes 15364
  62.5 49.6 %copy-start.6 = (s32[512]{0:T(512)S(1)}, s32[512]{0:T(512)}, u32[]{:S(2)}) copy-start(s32[512]{0:T(512)} %param.13) | copy-start | bytes 6148
  62.5 52.4 %copy-start = (bf16[512,1280]{1,0:T(8,128)(2,1)S(1)}, bf16[512,1280]{1,0:T(8,128)(2,1)}, u32[]{:S(2)}) copy-start(bf16[512,1280]{1,0:T(8,128)(2,1)} %x_ref.1) | copy-start | bytes 3932164
  62.5 47.6 %all-to-all-start.2 = ((bf16[32,40,640]{2,1,0:T(8,128)(2,1)}), bf16[32,40,640]{2,1,0:T(8,128)(2,1)S(1)}, u32[]{:S(2)}, u32[]{:S(2)}) async-start(bf16[32,40,640]{2,1,0:T(8,128)(2,1)} %broadcast_in_dim.101), calls=%async_computation.2 | async-start | bytes 3276800 | tf_op jit(solution)/shard_map/all_to_all | solution.py:18
  110.1 42.8 %collective-permute-start = (bf16[1280,640]{1,0:T(8,128)(2,1)S(1)}, bf16[1280,640]{1,0:T(8,128)(2,1)}, u32[]{:S(2)}, u32[]{:S(2)}) collective-permute-start(bf16[1280,640]{1,0:T(8,128)(2,1)S(1)} %bitcast.19), channel_id=1, source_target_pairs={{0,32},{32,0},{64,96},{96,64},{128,160},{160,128},{192,224},{224,1... | collective-permute-start | bytes 4915208 | tf_op jit(solution)/shard_map/ppermute | solution.py:23
  114.9 38.0 %copy-start.1 = (bf16[512,1280]{1,0:T(8,128)(2,1)S(1)}, bf16[512,1280]{1,0:T(8,128)(2,1)}, u32[]{:S(2)}) copy-start(bf16[512,1280]{1,0:T(8,128)(2,1)} %x_ref.1) | copy-start | bytes 3932164
  159.4 39.8 %all-to-all-start.3 = ((bf16[32,4,5120]{2,1,0:T(4,128)(2,1)}), bf16[32,4,5120]{2,1,0:T(4,128)(2,1)S(1)}, u32[]{:S(2)}, u32[]{:S(2)}) async-start(bf16[32,4,5120]{2,1,0:T(4,128)(2,1)} %reshape.69), calls=%async_computation.3 | async-start | bytes 2621440 | tf_op jit(solution)/shard_map/all_to_all | solution.py:242
Sparse Core Ops, SparseCore 0:
  43.5 63.3 all-gather.2

commit v4 on v3

--- a/solution.py
+++ b/solution.py
@@ -24,111 +24,80 @@
 
 
 def attention_kernel(
-    x_ref, gain_ref, w_ref, row_ref, col_ref, out_ref, normed_ref, wide_ref, heads_ref, *, head_width
+    x_ref, gain_ref, w_ref, key_ref, query_ref, out_ref, normed_ref, qkv_ref, context_ref, *, head_width
 ):
     step = pl.program_id(0)
-    columns = w_ref.shape[1]
+    chunk = w_ref.shape[0]
     count, width = x_ref.shape
     head_count = width // head_width
-    in_block = columns // head_width
+    chunks = 3 * width // chunk
 
     @pl.when(step == 0)
     def _():
         x = x_ref[...].astype(jnp.float32)
         scale = lax.rsqrt(jnp.mean(x * x, axis=-1, keepdims=True) + epsilon)
-        normed_ref[...] = (x * scale * gain_ref[...]).astype(jnp.bfloat16)
-
-    wide_ref[:, :columns] = lax.dot_general(
-        normed_ref[...],
-        w_ref[0],
-        (((1,), (1,)), ((), ())),
-        preferred_element_type=jnp.float32,
-    ).astype(jnp.bfloat16).astype(jnp.float32)
-    lane = lax.broadcasted_iota(jnp.int32, (1, 128), 1)
-    for piece in range(in_block):
-        part = step * in_block + piece
-        offset = jnp.where(part < 2 * head_count, 0, (part - 2 * head_count) * head_width % 128)
-        shift = (offset - piece * head_width + 256) % 256
-        moved = pltpu.roll(wide_ref[...], shift, axis=1)
-        end = offset + head_width
-        heads_ref[part] = jnp.where(
-            (lane >= offset) & (lane < end),
-            moved[:, :128],
-            jnp.where(lane < end - 128, moved[:, 128:], 0.0),
+        normed_ref[...] = (x * scale * gain_ref[...]).astype(jnp.bfloat16).T
+
+    @pl.when(step < chunks)
+    def _():
+        qkv_ref[pl.ds(pl.multiple_of(step * chunk, chunk), chunk), :] = jnp.dot(
+            w_ref[...], normed_ref[...], preferred_element_type=jnp.float32
         ).astype(jnp.bfloat16)
 
-    @pl.when(step == pl.num_programs(0) - 1)
+    @pl.when(step >= chunks)
     def _():
-        def unit(index, carry):
-            rows = pl.ds(pl.multiple_of(index * UNIT, UNIT), UNIT)
-            row_id = row_ref[rows, :]
-            live = row_id >= 0
-            allowed = row_id == col_ref[pl.ds(index, 1), :]
-
-            def group(number, carry):
-                column = jnp.zeros((UNIT, 128), jnp.float32)
-                for at in range(8):
-                    head = number * 8 + at
-                    scores = lax.dot_general(
-                        heads_ref[head, rows, :],
-                        heads_ref[head_count + head, rows, :],
-                        (((1,), (1,)), ((), ())),
-                        preferred_element_type=jnp.float32,
-                    )
-                    scores = jnp.where(allowed, scores, -1e30)
-                    highest = jnp.max(scores, axis=-1, keepdims=True)
-                    weights = jnp.exp2(
-                        (scores - highest) * (1.0 / (math.sqrt(head_width) * math.log(2.0)))
-                    )
-                    weights = weights * (1.0 / jnp.sum(weights, axis=-1, keepdims=True))
-                    mixed = jnp.dot(
-                        weights.astype(jnp.bfloat16),
-                        heads_ref[2 * head_count + head, rows, :],
-                        preferred_element_type=jnp.float32,
-                    )
-                    first = at * head_width % 128
-                    place = at * head_width // 128
-                    column = jnp.where(lane >= first, mixed, column)
-                    if first + head_width >= 128:
-                        start = pl.multiple_of(number * 8 * head_width + place * 128, 128)
-                        out_ref[rows, pl.ds(start, 128)] = jnp.where(live, column, 0.0).astype(
-                            jnp.bfloat16
-                        )
-                        column = mixed
-                return carry
-
-            return lax.fori_loop(0, head_count // 8, group, carry)
-
-        lax.fori_loop(0, count // UNIT, unit, 0)
-
-
-def attention(x, gain, slabs, row_id, col_id):
+        unit = step - chunks
+        patches = pl.ds(pl.multiple_of(unit * UNIT, UNIT), UNIT)
+        query_id = query_ref[pl.ds(unit, 1), :]
+        allowed = key_ref[patches, :] == query_id
+        for head in range(head_count):
+            query, key, value = (
+                qkv_ref[part * width + head * head_width : part * width + (head + 1) * head_width, patches]
+                for part in range(3)
+            )
+            scores = lax.dot_general(
+                key, query, (((0,), (0,)), ((), ())), preferred_element_type=jnp.float32
+            )
+            scores = jnp.where(allowed, scores, -1e30)
+            highest = jnp.max(scores, axis=0, keepdims=True)
+            weights = jnp.exp2(
+                (scores - highest) * (1.0 / (math.sqrt(head_width) * math.log(2.0)))
+            )
+            total = jnp.sum(weights, axis=0, keepdims=True)
+            weights = weights * jnp.where(query_id >= 0, 1.0 / total, 0.0)
+            context_ref[head * head_width : (head + 1) * head_width, :] = jnp.dot(
+                value, weights.astype(jnp.bfloat16), preferred_element_type=jnp.float32
+            ).astype(jnp.bfloat16)
+        out_ref[...] = context_ref[...].T
+
+
+def attention(x, gain, w, key_id, query_id):
     count, width = x.shape
-    blocks, columns, _ = slabs.shape
-    head_width = width // HEADS
+    chunk = 3 * width // 4
+    units = count // UNIT
     whole = lambda *shape: pl.BlockSpec(shape, lambda n: (0,) * len(shape))
     return pl.pallas_call(
-        lambda *refs: attention_kernel(*refs, head_width=head_width),
-        grid=(blocks,),
+        lambda *refs: attention_kernel(*refs, head_width=width // HEADS),
+        grid=(4 + units,),
         in_specs=[
             whole(count, width),
             whole(1, width),
-            pl.BlockSpec((1, columns, width), lambda n: (n, 0, 0)),
+            pl.BlockSpec((chunk, width), lambda n: (jnp.minimum(n, 3), 0)),
             whole(count, 1),
-            whole(count // UNIT, UNIT),
+            whole(units, UNIT),
         ],
-        out_specs=whole(count, width),
+        out_specs=pl.BlockSpec((UNIT, width), lambda n: (jnp.maximum(n - 4, 0), 0)),
         out_shape=jax.ShapeDtypeStruct((count, width), jnp.bfloat16),
         scratch_shapes=[
-            pltpu.VMEM((count, width), jnp.bfloat16),
-            pltpu.VMEM((count, 256), jnp.float32),
-            pltpu.VMEM((3 * HEADS, count, 128), jnp.bfloat16),
+            pltpu.VMEM((width, count), jnp.bfloat16),
+            pltpu.VMEM((3 * width, count), jnp.bfloat16),
+            pltpu.VMEM((width, UNIT), jnp.bfloat16),
         ],
         compiler_params=pltpu.CompilerParams(
             dimension_semantics=("arbitrary",), vmem_limit_bytes=32 << 20
         ),
         name="attention",
-    )(x, gain, pltpu.with_memory_space_constraint(slabs, pltpu.HBM), row_id, col_id)
+    )(x, gain, pltpu.with_memory_space_constraint(w, pltpu.HBM), key_id, query_id)
 
 
 def merge_kernel(
@@ -216,11 +185,10 @@
     info = jnp.broadcast_to(info[None], (row_count, 2 * slots))
     rows = copy_for_each(jnp.concatenate([w_qkv, info], axis=1), "tensor")
     slab = rows[:, :, :qkv_part].reshape(width, qkv_part).T
-    slabs = lax.all_gather(slab, "pipe", axis=0, tiled=False)
+    w_all = lax.all_gather(slab, "pipe", axis=0, tiled=True)
     info = rows[:, 0, qkv_part:].astype(jnp.int32)
     dest_rows = destination_rows(info[:, :slots], info[:, slots:])
 
-    slab, w_out = lax.optimization_barrier((slab, w_out))
     blocks = copy_for_each(w_out, "pipe")
     out_rows = jnp.moveaxis(blocks, 0, 1).reshape(row_count, 2, half)
     out_rows = lax.dynamic_index_in_dim(out_rows, core[0], axis=1, keepdims=False)
@@ -229,13 +197,13 @@
 
     live = jnp.arange(patch_count, dtype=jnp.int32) < jnp.sum(image_patches)
     ids = jnp.where(live, window_ids, -1)
-    ids, dest_rows, out_own = lax.optimization_barrier((ids, dest_rows, out_own))
+    ids, dest_rows = lax.optimization_barrier((ids, dest_rows))
     context = attention(
         patches,
         attn_gain[None, :],
-        slabs,
-        jnp.where(ids < 0, -2, ids)[:, None],
-        ids.reshape(patch_count // UNIT, UNIT),
+        w_all,
+        ids[:, None],
+        jnp.where(ids < 0, -2, ids).reshape(patch_count // UNIT, UNIT),
     )
     tokens = merge_tokens(core, context, out_own, out_other, patches, merge_gain[None, :])
     outgoing = tokens.reshape(group_size, token_count // group_size, 4 * width)

time: 209 us -> 187 us (0.89)
  the two profiles are of different devices: /device:TPU:4 before, /device:TPU:2 now
where the time goes in v4:
time: 187 us; the launch traced here: 186 us
  waiting for transfers between devices  85.9 us (46%)
  blocking collectives  32.9 us (18%)
  Pallas kernels  21.5 us (11%)
  starting transfers between devices  19.9 us (11%)
  between operations  13.7 us (7%)
  local copies, waits for them, and re-layouts  7.18 us (4%)
  other arithmetic  3.69 us (2%)
    all_to_all x2, waiting for transfers between devices, copy_for_each(): lax.all_to_all(jnp.broadcast_to(x[None], (size, *x.shape)), axis, 0, 0, t...  51.7 us
    all_to_all x1, waiting for transfers between devices, body(): lax.all_to_all(outgoing, 'tensor', split_axis=0, concat_axis=0, tiled=True)  34.2 us
    all_to_all x1, blocking collectives, copy_for_each(): lax.all_to_all(jnp.broadcast_to(x[None], (size, *x.shape)), axis, 0, 0, t...  32.9 us
    pallas_call x1, Pallas kernels, attention(): pl.pallas_call(lambda *refs: attention_kernel(*refs, head_width=width //...  16.4 us
    all_to_all x2, starting transfers between devices, copy_for_each(): lax.all_to_all(jnp.broadcast_to(x[None], (size, *x.shape)), axis, 0, 0, t...  12.6 us
    all_to_all x1, starting transfers between devices, body(): lax.all_to_all(outgoing, 'tensor', split_axis=0, concat_axis=0, tiled=True)  5.21 us
    pallas_call x1, Pallas kernels, merge_tokens(): pl.pallas_call(merge_kernel, in_specs=[pl.BlockSpec(memory_space=pltpu.SM...  5.09 us
  transfers between devices with their start and end apart: 5, of which 3 were waited for; matrix products, arithmetic and copies ran while one was open for 3% of the time, Pallas kernels for 9%

profile of v4, /device:TPU:2, one launch (start us, length us, event | category | flops | bytes accessed | tf_op | source)
XLA Modules:
  0.0 186.2 jit_solution(8423885226494765887)
XLA Ops:
  6.5 0.7 convert.8
  7.2 1.3 fusion.9
  8.6 0.7 pad_maximum_fusion
  9.4 32.9 %all_to_all.20 = bf16[32,40,248]{2,1,0:T(8,128)(2,1)S(1)} all-to-all(bf16[32,40,248]{2,1,0:T(8,128)(2,1)S(1)} %broadcast_in_dim.92), channel_id=1, replica_groups=mesh['pipe'=16,'tensor'=32] {'tensor'}, dimensions={0} | all-to-all | bytes 1269760 | tf_op jit(solution)/shard_map/all_to_all | solution.py:18
  42.3 1.1 copy.25
  43.4 0.7 broadcast_in_dim.102
  44.1 7.2 %all-to-all-start.1 = ((bf16[16,40,80]{2,1,0:T(8,128)(2,1)}), bf16[16,40,80]{2,1,0:T(8,128)(2,1)S(1)}, u32[]{:S(2)}, u32[]{:S(2)}) async-start(bf16[16,40,80]{2,1,0:T(8,128)(2,1)} %broadcast_in_dim.102), calls=%async_computation.1 | async-start | bytes 327680 | tf_op jit(solution)/shard_map/all_to_all | solution.py:18
  51.3 9.5 %all-to-all-done.1 = bf16[16,40,80]{2,1,0:T(8,128)(2,1)S(1)} async-done(((bf16[16,40,80]{2,1,0:T(8,128)(2,1)}), bf16[16,40,80]{2,1,0:T(8,128)(2,1)S(1)}, u32[]{:S(2)}, u32[]{:S(2)}) %all-to-all-start.1) | async-done | bytes 102432 | tf_op jit(solution)/shard_map/all_to_all | solution.py:18
  60.8 0.3 reshape.67
  61.2 1.3 broadcast_in_dim.104
  62.6 5.4 %all-to-all-start.2 = ((bf16[32,40,640]{2,1,0:T(8,128)(2,1)}), bf16[32,40,640]{2,1,0:T(8,128)(2,1)S(1)}, u32[]{:S(2)}, u32[]{:S(2)}) async-start(bf16[32,40,640]{2,1,0:T(8,128)(2,1)} %broadcast_in_dim.104), calls=%async_computation.2 | async-start | bytes 3276800 | tf_op jit(solution)/shard_map/all_to_all | solution.py:18
  68.0 42.3 %all-to-all-done.2 = bf16[32,40,640]{2,1,0:T(8,128)(2,1)S(1)} async-done(((bf16[32,40,640]{2,1,0:T(8,128)(2,1)}), bf16[32,40,640]{2,1,0:T(8,128)(2,1)S(1)}, u32[]{:S(2)}, u32[]{:S(2)}) %all-to-all-start.2) | async-done | bytes 1638432 | tf_op jit(solution)/shard_map/all_to_all | solution.py:18
  110.3 2.0 %collective-permute-start = (bf16[1280,640]{1,0:T(8,128)(2,1)S(1)}, bf16[1280,640]{1,0:T(8,128)(2,1)}, u32[]{:S(2)}, u32[]{:S(2)}) collective-permute-start(bf16[1280,640]{1,0:T(8,128)(2,1)S(1)} %bitcast.18), channel_id=1, source_target_pairs={{0,32},{32,0},{64,96},{96,64},{128,160},{160,128},{192,224},{224,1... | collective-permute-start | bytes 4915208 | tf_op jit(solution)/shard_map/ppermute | solution.py:23
  112.4 0.6 fusion.6
  113.0 0.9 slice.16
  114.5 0.1 select_reduce_fusion
  114.9 0.1 copy.26.refs_3_
  115.1 16.4 %attention.1.context_ref = bf16[512,1280]{1,0:T(8,128)(2,1)S(1)} custom-call(bf16[512,1280]{1,0:T(8,128)(2,1)S(1)} %copy-done, f32[1,1280]{1,0:T(1,128)S(1)} %broadcast_in_dim.99.refs_1_, bf16[3840,1280]{1,0:T(8,128)(2,1)} %all-gather.2.cloned.1.call-done.refs_2_, s32[512,1]{1,0:T(8,128)S(1)} %copy.26.refs_3_, s32[4,128]{1,0:T(4,128)S(1)} %fusion.5.refs_4_), custom_call_target="tpu_custom_call" | custom-call | tf_op jit(solution)/shard_map/attention/pallas_call | solution.py:79
  131.5 5.1 %merge_tokens.1 = bf16[128,5120]{1,0:T(8,128)(2,1)S(1)} custom-call(s32[1]{0:T(128)} %bitcast.2.core_ref, bf16[512,1280]{1,0:T(8,128)(2,1)S(1)} %attention.1.context_ref, bf16[1280,640]{1,0:T(8,128)(2,1)S(1)} %bitcast.19, bf16[1280,640]{1,0:T(8,128)(2,1)} %collective-permute-done.w_other_ref, bf16[512,1280]{1,0:T(8,128)(2,1)S(1)} %copy-done.1, ...), custom_call_target="tpu_custom_call" | custom-call | tf_op jit(solution)/shard_map/merge_tokens/pallas_call | solution.py:143
  136.6 1.3 reshape.69
  137.9 5.2 %all-to-all-start.3 = ((bf16[32,4,5120]{2,1,0:T(4,128)(2,1)}), bf16[32,4,5120]{2,1,0:T(4,128)(2,1)S(1)}, u32[]{:S(2)}, u32[]{:S(2)}) async-start(bf16[32,4,5120]{2,1,0:T(4,128)(2,1)} %reshape.69), calls=%async_computation.3 | async-start | bytes 2621440 | tf_op jit(solution)/shard_map/all_to_all | solution.py:210
  143.3 34.2 %all-to-all-done.3 = bf16[32,4,5120]{2,1,0:T(4,128)(2,1)S(1)} async-done(((bf16[32,4,5120]{2,1,0:T(4,128)(2,1)}), bf16[32,4,5120]{2,1,0:T(4,128)(2,1)S(1)}, u32[]{:S(2)}, u32[]{:S(2)}) %all-to-all-start.3) | async-done | bytes 1310752 | tf_op jit(solution)/shard_map/all_to_all | solution.py:210
  177.5 0.3 reshape.70
  177.8 1.6 fusion
  (44 shorter events, 1.4 us)
Async XLA Ops:
  6.5 108.5 %all-gather.2.cloned.1.call-start = ((), (), s32[]{:S(2)}) async-start(), calls=%async_computation.4 | async-start | bytes 10444800 | tf_op jit(solution)/shard_map/all_gather | solution.py:188
  9.4 34.0 %copy-start.3 = (bf16[40,80]{1,0:T(8,128)(2,1)S(1)}, bf16[40,80]{1,0:T(8,128)(2,1)}, u32[]{:S(2)}) copy-start(bf16[40,80]{1,0:T(8,128)(2,1)} %param.11) | copy-start | bytes 19204
  42.3 18.5 %copy-start.2 = (bf16[32,40,248]{2,1,0:T(8,128)(2,1)}, bf16[32,40,248]{2,1,0:T(8,128)(2,1)S(1)}, u32[]{:S(2)}) copy-start(bf16[32,40,248]{2,1,0:T(8,128)(2,1)S(1)} %all_to_all.20) | copy-start | bytes 1904644
  44.1 16.7 %all-to-all-start.1 = ((bf16[16,40,80]{2,1,0:T(8,128)(2,1)}), bf16[16,40,80]{2,1,0:T(8,128)(2,1)S(1)}, u32[]{:S(2)}, u32[]{:S(2)}) async-start(bf16[16,40,80]{2,1,0:T(8,128)(2,1)} %broadcast_in_dim.102), calls=%async_computation.1 | async-start | bytes 327680 | tf_op jit(solution)/shard_map/all_to_all | solution.py:18
  62.5 5.4 %copy-start.4 = (f32[1280]{0:T(1024)S(1)}, f32[1280]{0:T(1024)}, u32[]{:S(2)}) copy-start(f32[1280]{0:T(1024)} %param.9) | copy-start | bytes 15364
  62.5 5.5 %copy-start.5 = (f32[1280]{0:T(1024)S(1)}, f32[1280]{0:T(1024)}, u32[]{:S(2)}) copy-start(f32[1280]{0:T(1024)} %param.12) | copy-start | bytes 15364
  62.5 49.8 %copy-start.6 = (s32[512]{0:T(512)S(1)}, s32[512]{0:T(512)}, u32[]{:S(2)}) copy-start(s32[512]{0:T(512)} %param.13) | copy-start | bytes 6148
  62.5 52.5 %copy-start = (bf16[512,1280]{1,0:T(8,128)(2,1)S(1)}, bf16[512,1280]{1,0:T(8,128)(2,1)}, u32[]{:S(2)}) copy-start(bf16[512,1280]{1,0:T(8,128)(2,1)} %x_ref.1) | copy-start | bytes 3932164
  62.6 47.8 %all-to-all-start.2 = ((bf16[32,40,640]{2,1,0:T(8,128)(2,1)}), bf16[32,40,640]{2,1,0:T(8,128)(2,1)S(1)}, u32[]{:S(2)}, u32[]{:S(2)}) async-start(bf16[32,40,640]{2,1,0:T(8,128)(2,1)} %broadcast_in_dim.104), calls=%async_computation.2 | async-start | bytes 3276800 | tf_op jit(solution)/shard_map/all_to_all | solution.py:18
  110.3 21.2 %collective-permute-start = (bf16[1280,640]{1,0:T(8,128)(2,1)S(1)}, bf16[1280,640]{1,0:T(8,128)(2,1)}, u32[]{:S(2)}, u32[]{:S(2)}) collective-permute-start(bf16[1280,640]{1,0:T(8,128)(2,1)S(1)} %bitcast.18), channel_id=1, source_target_pairs={{0,32},{32,0},{64,96},{96,64},{128,160},{160,128},{192,224},{224,1... | collective-permute-start | bytes 4915208 | tf_op jit(solution)/shard_map/ppermute | solution.py:23
  115.1 16.4 %copy-start.1 = (bf16[512,1280]{1,0:T(8,128)(2,1)S(1)}, bf16[512,1280]{1,0:T(8,128)(2,1)}, u32[]{:S(2)}) copy-start(bf16[512,1280]{1,0:T(8,128)(2,1)} %x_ref.1) | copy-start | bytes 3932164
  137.9 39.6 %all-to-all-start.3 = ((bf16[32,4,5120]{2,1,0:T(4,128)(2,1)}), bf16[32,4,5120]{2,1,0:T(4,128)(2,1)S(1)}, u32[]{:S(2)}, u32[]{:S(2)}) async-start(bf16[32,4,5120]{2,1,0:T(4,128)(2,1)} %reshape.69), calls=%async_computation.3 | async-start | bytes 2621440 | tf_op jit(solution)/shard_map/all_to_all | solution.py:210
Sparse Core Ops, SparseCore 0:
  43.5 63.3 all-gather.1

commit v5 on v4

--- a/solution.py
+++ b/solution.py
@@ -23,81 +23,169 @@
     return lax.ppermute(x, "pipe", [(p, p ^ 1) for p in range(size)])
 
 
-def attention_kernel(
-    x_ref, gain_ref, w_ref, key_ref, query_ref, out_ref, normed_ref, qkv_ref, context_ref, *, head_width
-):
-    step = pl.program_id(0)
-    chunk = w_ref.shape[0]
-    count, width = x_ref.shape
-    head_count = width // head_width
-    chunks = 3 * width // chunk
-
-    @pl.when(step == 0)
-    def _():
-        x = x_ref[...].astype(jnp.float32)
-        scale = lax.rsqrt(jnp.mean(x * x, axis=-1, keepdims=True) + epsilon)
-        normed_ref[...] = (x * scale * gain_ref[...]).astype(jnp.bfloat16).T
-
-    @pl.when(step < chunks)
-    def _():
-        qkv_ref[pl.ds(pl.multiple_of(step * chunk, chunk), chunk), :] = jnp.dot(
-            w_ref[...], normed_ref[...], preferred_element_type=jnp.float32
+def chip_copy(x, chips):
+    size = lax.axis_size("pipe")
+    return lax.ppermute(x, "pipe", [(p, (p + 2 * chips) % size) for p in range(size)])
+
+
+def ring_project(slab, normed, w_out, core, early):
+    rows = slab.shape[0]
+    size = lax.axis_size("pipe")
+    place = lax.axis_index("pipe").astype(jnp.int32)
+    together = lax.optimization_barrier
+
+    def firsts(pieces):
+        owners = [(place + owner, offset) for owner, offset in pieces]
+        owners += [((place ^ 1) + owner, offset) for owner, offset in pieces]
+        return jnp.stack([((owner + size) % size) * rows + offset for owner, offset in owners])
+
+    cut = rows * 2 // 3
+    near = [(0, 0)], [(-2, 0), (2, 0)], [(-4, 0), (4, 0)], [(-6, 0), (6, 0)], [(8, 0), (8, cut)]
+    a1, b1 = chip_copy(slab, 1), chip_copy(slab, -1)
+    blocks = copy_for_each(w_out, "pipe")
+    other = partner_copy(slab)
+    a1, b1, other, normed, blocks = together((a1, b1, other, normed, blocks))
+
+    a2, b2 = chip_copy(a1, 1), chip_copy(b1, -1)
+    pa1, pb1 = partner_copy(a1), partner_copy(b1)
+    half = blocks.shape[0] * blocks.shape[2] // 2
+    out_rows = jnp.moveaxis(blocks, 0, 1).reshape(blocks.shape[1], 2, half)
+    out_rows = lax.dynamic_index_in_dim(out_rows, core[0], axis=1, keepdims=False)
+    out_own = copy_for_each(out_rows, "tensor")
+    buffer = project(normed, [slab, other], firsts(near[0]), None)
+    a2, b2, pa1, pb1, buffer, early = together((a2, b2, pa1, pb1, buffer, early))
+
+    a3, b3 = chip_copy(a2, 1), chip_copy(b2, -1)
+    pa2, pb2 = partner_copy(a2), partner_copy(b2)
+    buffer = project(normed, [a1, b1, pa1, pb1], firsts(near[1]), buffer)
+    a3, b3, pa2, pb2, buffer = together((a3, b3, pa2, pb2, buffer))
+
+    a4, b4 = chip_copy(a3[:cut], 1), chip_copy(b3[cut:], -1)
+    pa3, pb3 = partner_copy(a3), partner_copy(b3)
+    buffer = project(normed, [a2, b2, pa2, pb2], firsts(near[2]), buffer)
+    a4, b4, pa3, pb3, buffer = together((a4, b4, pa3, pb3, buffer))
+
+    pa4, pb4 = partner_copy(a4), partner_copy(b4)
+    buffer = project(normed, [a3, b3, pa3, pb3], firsts(near[3]), buffer)
+    pa4, pb4, buffer, out_own = together((pa4, pb4, buffer, out_own))
+    buffer = project(normed, [a4, b4, pa4, pb4], firsts(near[4]), buffer)
+    return buffer, out_own.reshape(-1, half), early
+
+
+def on_chip(x):
+    return pltpu.with_memory_space_constraint(x, pltpu.VMEM)
+
+
+def in_hbm(x):
+    return pltpu.with_memory_space_constraint(x, pltpu.HBM)
+
+
+def in_vmem(count):
+    return [pl.BlockSpec(memory_space=pltpu.VMEM)] * count
+
+
+def normalize_kernel(x_ref, gain_ref, out_ref):
+    x = x_ref[...].astype(jnp.float32)
+    scale = lax.rsqrt(jnp.mean(x * x, axis=-1, keepdims=True) + epsilon)
+    out_ref[...] = (x * scale * gain_ref[...]).astype(jnp.bfloat16).T
+
+
+def normalize_rows(x, gain):
+    return pl.pallas_call(
+        normalize_kernel,
+        in_specs=in_vmem(2),
+        out_specs=pl.BlockSpec(memory_space=pltpu.VMEM),
+        out_shape=jax.ShapeDtypeStruct((x.shape[1], x.shape[0]), jnp.bfloat16),
+        compiler_params=pltpu.CompilerParams(vmem_limit_bytes=16 << 20),
+        name="normalize_rows",
+    )(x, gain)
+
+
+def project_kernel(first_ref, normed_ref, *refs, pieces, aliased):
+    slab_refs = refs[:pieces]
+    out_ref, part_ref, sems = refs[pieces + aliased :]
+    copies = []
+    at = 0
+    for piece, slab_ref in enumerate(slab_refs):
+        rows = slab_ref.shape[0]
+        part_ref[at : at + rows, :] = jnp.dot(
+            slab_ref[...], normed_ref[...], preferred_element_type=jnp.float32
         ).astype(jnp.bfloat16)
-
-    @pl.when(step >= chunks)
-    def _():
-        unit = step - chunks
-        patches = pl.ds(pl.multiple_of(unit * UNIT, UNIT), UNIT)
-        query_id = query_ref[pl.ds(unit, 1), :]
-        allowed = key_ref[patches, :] == query_id
-        for head in range(head_count):
-            query, key, value = (
-                qkv_ref[part * width + head * head_width : part * width + (head + 1) * head_width, patches]
-                for part in range(3)
+        first = pl.multiple_of(first_ref[piece], 80)
+        copies.append(
+            pltpu.make_async_copy(
+                part_ref.at[at : at + rows, :], out_ref.at[pl.ds(first, rows), :], sems.at[piece]
             )
-            scores = lax.dot_general(
-                key, query, (((0,), (0,)), ((), ())), preferred_element_type=jnp.float32
-            )
-            scores = jnp.where(allowed, scores, -1e30)
-            highest = jnp.max(scores, axis=0, keepdims=True)
-            weights = jnp.exp2(
-                (scores - highest) * (1.0 / (math.sqrt(head_width) * math.log(2.0)))
-            )
-            total = jnp.sum(weights, axis=0, keepdims=True)
-            weights = weights * jnp.where(query_id >= 0, 1.0 / total, 0.0)
-            context_ref[head * head_width : (head + 1) * head_width, :] = jnp.dot(
-                value, weights.astype(jnp.bfloat16), preferred_element_type=jnp.float32
-            ).astype(jnp.bfloat16)
-        out_ref[...] = context_ref[...].T
-
-
-def attention(x, gain, w, key_id, query_id):
-    count, width = x.shape
-    chunk = 3 * width // 4
+        )
+        copies[-1].start()
+        at += rows
+    for copy in copies:
+        copy.wait()
+
+
+def project(normed, slabs, firsts, buffer):
+    width, count = normed.shape
+    aliased = buffer is not None
+    rows = sum(slab.shape[0] for slab in slabs)
+    return pl.pallas_call(
+        lambda *refs: project_kernel(*refs, pieces=len(slabs), aliased=aliased),
+        in_specs=[pl.BlockSpec(memory_space=pltpu.SMEM)]
+        + in_vmem(1 + len(slabs))
+        + [pl.BlockSpec(memory_space=pltpu.HBM)] * aliased,
+        out_specs=pl.BlockSpec(memory_space=pltpu.HBM),
+        out_shape=pltpu.HBM((3 * width, count), jnp.bfloat16),
+        scratch_shapes=[
+            pltpu.VMEM((rows, count), jnp.bfloat16),
+            pltpu.SemaphoreType.DMA((len(slabs),)),
+        ],
+        input_output_aliases={2 + len(slabs): 0} if aliased else {},
+        compiler_params=pltpu.CompilerParams(vmem_limit_bytes=16 << 20),
+        name="project",
+    )(firsts, normed, *slabs, *([in_hbm(buffer)] if aliased else []))
+
+
+def attention_kernel(qkv_ref, key_ref, query_ref, out_ref, context_ref, *, head_width):
+    width = out_ref.shape[1]
+    query_id = query_ref[pl.ds(pl.program_id(0), 1), :]
+    allowed = key_ref[...] == query_id
+    for head in range(width // head_width):
+        query, key, value = (
+            qkv_ref[part * width + head * head_width : part * width + (head + 1) * head_width, :]
+            for part in range(3)
+        )
+        scores = lax.dot_general(
+            key, query, (((0,), (0,)), ((), ())), preferred_element_type=jnp.float32
+        )
+        scores = jnp.where(allowed, scores, -1e30)
+        highest = jnp.max(scores, axis=0, keepdims=True)
+        weights = jnp.exp2((scores - highest) * (1.0 / (math.sqrt(head_width) * math.log(2.0))))
+        total = jnp.sum(weights, axis=0, keepdims=True)
+        weights = weights * jnp.where(query_id >= 0, 1.0 / total, 0.0)
+        context_ref[head * head_width : (head + 1) * head_width, :] = jnp.dot(
+            value, weights.astype(jnp.bfloat16), preferred_element_type=jnp.float32
+        ).astype(jnp.bfloat16)
+    out_ref[...] = context_ref[...].T
+
+
+def attention(qkv, key_id, query_id):
+    width, count = qkv.shape[0] // 3, qkv.shape[1]
     units = count // UNIT
-    whole = lambda *shape: pl.BlockSpec(shape, lambda n: (0,) * len(shape))
     return pl.pallas_call(
         lambda *refs: attention_kernel(*refs, head_width=width // HEADS),
-        grid=(4 + units,),
+        grid=(units,),
         in_specs=[
-            whole(count, width),
-            whole(1, width),
-            pl.BlockSpec((chunk, width), lambda n: (jnp.minimum(n, 3), 0)),
-            whole(count, 1),
-            whole(units, UNIT),
+            pl.BlockSpec((3 * width, UNIT), lambda n: (0, n)),
+            pl.BlockSpec((UNIT, 1), lambda n: (n, 0)),
+            pl.BlockSpec((units, UNIT), lambda n: (0, 0)),
         ],
-        out_specs=pl.BlockSpec((UNIT, width), lambda n: (jnp.maximum(n - 4, 0), 0)),
+        out_specs=pl.BlockSpec((UNIT, width), lambda n: (n, 0)),
         out_shape=jax.ShapeDtypeStruct((count, width), jnp.bfloat16),
-        scratch_shapes=[
-            pltpu.VMEM((width, count), jnp.bfloat16),
-            pltpu.VMEM((3 * width, count), jnp.bfloat16),
-            pltpu.VMEM((width, UNIT), jnp.bfloat16),
-        ],
+        scratch_shapes=[pltpu.VMEM((width, UNIT), jnp.bfloat16)],
         compiler_params=pltpu.CompilerParams(
-            dimension_semantics=("arbitrary",), vmem_limit_bytes=32 << 20
+            dimension_semantics=("arbitrary",), vmem_limit_bytes=16 << 20
         ),
         name="attention",
-    )(x, gain, pltpu.with_memory_space_constraint(w, pltpu.HBM), key_id, query_id)
+    )(in_hbm(qkv), key_id, query_id)
 
 
 def merge_kernel(
@@ -130,14 +218,6 @@
         ).astype(jnp.bfloat16)
 
 
-def on_chip(x):
-    return pltpu.with_memory_space_constraint(x, pltpu.VMEM)
-
-
-def in_vmem(count):
-    return [pl.BlockSpec(memory_space=pltpu.VMEM)] * count
-
-
 def merge_tokens(core, context, w_own, w_other, x, gain):
     count, width = x.shape
     return pl.pallas_call(
@@ -177,7 +257,6 @@
     group_size = lax.axis_size("tensor")
     core = (lax.axis_index("pipe") % 2).astype(jnp.int32).reshape(1)
 
-    half = width // 2
     slots = image_patches.shape[0]
     row_count, qkv_part = w_qkv.shape
 
@@ -185,26 +264,19 @@
     info = jnp.broadcast_to(info[None], (row_count, 2 * slots))
     rows = copy_for_each(jnp.concatenate([w_qkv, info], axis=1), "tensor")
     slab = rows[:, :, :qkv_part].reshape(width, qkv_part).T
-    w_all = lax.all_gather(slab, "pipe", axis=0, tiled=True)
     info = rows[:, 0, qkv_part:].astype(jnp.int32)
     dest_rows = destination_rows(info[:, :slots], info[:, slots:])
 
-    blocks = copy_for_each(w_out, "pipe")
-    out_rows = jnp.moveaxis(blocks, 0, 1).reshape(row_count, 2, half)
-    out_rows = lax.dynamic_index_in_dim(out_rows, core[0], axis=1, keepdims=False)
-    out_own = copy_for_each(out_rows, "tensor").reshape(width, half)
+    slab, w_out = lax.optimization_barrier((slab, w_out))
+    normed = normalize_rows(patches, attn_gain[None, :])
+    live = jnp.arange(patch_count, dtype=jnp.int32) < jnp.sum(image_patches)
+    key_id = jnp.where(live, window_ids, -1)[:, None]
+    query_id = jnp.where(live, window_ids, -2).reshape(patch_count // UNIT, UNIT)
+    qkv, out_own, (key_id, query_id, dest_rows) = ring_project(
+        slab, normed, w_out, core, (key_id, query_id, dest_rows)
+    )
     out_other = partner_copy(out_own)
-
-    live = jnp.arange(patch_count, dtype=jnp.int32) < jnp.sum(image_patches)
-    ids = jnp.where(live, window_ids, -1)
-    ids, dest_rows = lax.optimization_barrier((ids, dest_rows))
-    context = attention(
-        patches,
-        attn_gain[None, :],
-        w_all,
-        ids[:, None],
-        jnp.where(ids < 0, -2, ids).reshape(patch_count // UNIT, UNIT),
-    )
+    context = attention(qkv, key_id, query_id)
     tokens = merge_tokens(core, context, out_own, out_other, patches, merge_gain[None, :])
     outgoing = tokens.reshape(group_size, token_count // group_size, 4 * width)
     received = lax.all_to_all(outgoing, "tensor", split_axis=0, concat_axis=0, tiled=True)

time: 187 us -> 218 us (1.17)
  the two profiles are of different devices: /device:TPU:2 before, /device:TPU:4 now
where the time goes in v5:
time: 218 us; the launch traced here: 217 us
  starting transfers between devices  72 us (33%)
  waiting for transfers between devices  62.1 us (28%)
  blocking collectives  33 us (15%)
  Pallas kernels  31.7 us (15%)
  local copies, waits for them, and re-layouts  11.8 us (5%)
  other arithmetic  4.18 us (2%)
    all_to_all x1, waiting for transfers between devices, body(): lax.all_to_all(outgoing, 'tensor', split_axis=0, concat_axis=0, tiled=True)  34.1 us
    all_to_all x1, blocking collectives, copy_for_each(): lax.all_to_all(jnp.broadcast_to(x[None], (size, *x.shape)), axis, 0, 0, t...  33 us
    ppermute x8, starting transfers between devices, chip_copy(): lax.ppermute(x, 'pipe', [(p, (p + 2 * chips) % size) for p in range(size)])  28.9 us
    ppermute x10, starting transfers between devices, partner_copy(): return lax.ppermute(x, 'pipe', [(p, p ^ 1) for p in range(size)])  20.6 us
    ppermute x8, waiting for transfers between devices, chip_copy(): lax.ppermute(x, 'pipe', [(p, (p + 2 * chips) % size) for p in range(size)])  19.5 us
    pallas_call x5, Pallas kernels, project(): pl.pallas_call(lambda *refs: project_kernel(*refs, pieces=len(slabs), ali...  16.9 us
    all_to_all x2, starting transfers between devices, copy_for_each(): lax.all_to_all(jnp.broadcast_to(x[None], (size, *x.shape)), axis, 0, 0, t...  12.8 us
    all_to_all x1, starting transfers between devices, body(): lax.all_to_all(outgoing, 'tensor', split_axis=0, concat_axis=0, tiled=True)  9.78 us
  transfers between devices with their start and end apart: 21, of which 8 were waited for; matrix products, arithmetic and copies ran while one was open for 3% of the time, Pallas kernels for 12%

profile of v5, /device:TPU:4, one launch (start us, length us, event | category | flops | bytes accessed | tf_op | source)
XLA Modules:
  0.0 217.1 jit_solution(4385264614666779784)
XLA Ops:
  2.9 33.0 %all_to_all.20 = bf16[32,40,248]{2,1,0:T(8,128)(2,1)S(1)} all-to-all(bf16[32,40,248]{2,1,0:T(8,128)(2,1)S(1)} %broadcast_in_dim.89), channel_id=1, replica_groups=mesh['pipe'=16,'tensor'=32] {'tensor'}, dimensions={0} | all-to-all | bytes 1269760 | tf_op jit(solution)/shard_map/all_to_all | solution.py:18
  36.2 3.5 %collective-permute-start = (bf16[240,1280]{1,0:T(8,128)(2,1)S(1)}, bf16[240,1280]{1,0:T(8,128)(2,1)}, u32[]{:S(2)}, u32[]{:S(2)}) collective-permute-start(bf16[240,1280]{1,0:T(8,128)(2,1)S(1)} %bitcast.38), channel_id=1, source_target_pairs={{0,64},{32,96},{64,128},{96,160},{128,192},{160,224},{192,256},{22... | collective-permute-start | bytes 1843208 | tf_op jit(solution)/shard_map/ppermute | solution.py:28
  39.7 3.8 %collective-permute-start.1 = (bf16[240,1280]{1,0:T(8,128)(2,1)S(1)}, bf16[240,1280]{1,0:T(8,128)(2,1)}, u32[]{:S(2)}, u32[]{:S(2)}) collective-permute-start(bf16[240,1280]{1,0:T(8,128)(2,1)S(1)} %bitcast.39), channel_id=1, source_target_pairs={{0,448},{32,480},{64,0},{96,32},{128,64},{160,96},{192,128},{224,1... | collective-permute-start | bytes 1843208 | tf_op jit(solution)/shard_map/ppermute | solution.py:28
  46.1 7.1 %all-to-all-start.1 = ((bf16[16,40,80]{2,1,0:T(8,128)(2,1)}), bf16[16,40,80]{2,1,0:T(8,128)(2,1)S(1)}, u32[]{:S(2)}, u32[]{:S(2)}) async-start(bf16[16,40,80]{2,1,0:T(8,128)(2,1)} %broadcast_in_dim.91), calls=%async_computation.1 | async-start | bytes 327680 | tf_op jit(solution)/shard_map/all_to_all | solution.py:18
  54.0 8.4 %all-to-all-done.1 = bf16[16,40,80]{2,1,0:T(8,128)(2,1)S(1)} async-done(((bf16[16,40,80]{2,1,0:T(8,128)(2,1)}), bf16[16,40,80]{2,1,0:T(8,128)(2,1)S(1)}, u32[]{:S(2)}, u32[]{:S(2)}) %all-to-all-start.1) | async-done | bytes 102432 | tf_op jit(solution)/shard_map/all_to_all | solution.py:18
  64.2 5.7 %all-to-all-start.2 = ((bf16[32,40,640]{2,1,0:T(8,128)(2,1)}), bf16[32,40,640]{2,1,0:T(8,128)(2,1)S(1)}, u32[]{:S(2)}, u32[]{:S(2)}) async-start(bf16[32,40,640]{2,1,0:T(8,128)(2,1)} %broadcast_in_dim.103), calls=%async_computation.2 | async-start | bytes 3276800 | tf_op jit(solution)/shard_map/all_to_all | solution.py:18
  71.8 4.4 %collective-permute-start.3 = (bf16[240,1280]{1,0:T(8,128)(2,1)}, bf16[240,1280]{1,0:T(8,128)(2,1)}, u32[]{:S(2)}, u32[]{:S(2)}) collective-permute-start(bf16[240,1280]{1,0:T(8,128)(2,1)} %collective-permute-done.refs_2_), channel_id=1, source_target_pairs={{0,64},{32,96},{64,128},{96,160},{128,192},{160,224},{192,256},{22... | collective-permute-start | bytes 1843208 | tf_op jit(solution)/shard_map/ppermute | solution.py:28
  78.1 2.7 %collective-permute-start.4 = (bf16[240,1280]{1,0:T(8,128)(2,1)}, bf16[240,1280]{1,0:T(8,128)(2,1)}, u32[]{:S(2)}, u32[]{:S(2)}) collective-permute-start(bf16[240,1280]{1,0:T(8,128)(2,1)} %collective-permute-done.1.refs_3_), channel_id=1, source_target_pairs={{0,448},{32,480},{64,0},{96,32},{128,64},{160,96},{192,128},{224,1... | collective-permute-start | bytes 1843208 | tf_op jit(solution)/shard_map/ppermute | solution.py:28
  84.8 2.6 %project.5.refs_6_ = bf16[3840,512]{1,0:T(8,128)(2,1)} custom-call(s32[2]{0:T(128)S(1)} %pad_add_fusion.refs_0_, bf16[1280,512]{1,0:T(8,128)(2,1)S(1)} %normalize_rows.1.refs_1_, bf16[240,1280]{1,0:T(8,128)(2,1)S(1)} %bitcast.41, bf16[240,1280]{1,0:T(8,128)(2,1)} %collective-permute-done.2.refs_3_), custom_call_target="tpu_custom_call" | custom-call | tf_op jit(solution)/shard_map/project/pallas_call | solution.py:130
  87.4 3.8 %collective-permute-done.3.refs_2_ = bf16[240,1280]{1,0:T(8,128)(2,1)} collective-permute-done((bf16[240,1280]{1,0:T(8,128)(2,1)}, bf16[240,1280]{1,0:T(8,128)(2,1)}, u32[]{:S(2)}, u32[]{:S(2)}) %collective-permute-start.3) | collective-permute-done | bytes 614432 | tf_op jit(solution)/shard_map/ppermute | solution.py:28
  91.1 5.4 %collective-permute-done.4.refs_3_ = bf16[240,1280]{1,0:T(8,128)(2,1)} collective-permute-done((bf16[240,1280]{1,0:T(8,128)(2,1)}, bf16[240,1280]{1,0:T(8,128)(2,1)}, u32[]{:S(2)}, u32[]{:S(2)}) %collective-permute-start.4) | collective-permute-done | bytes 614432 | tf_op jit(solution)/shard_map/ppermute | solution.py:28
  98.5 2.6 %collective-permute-start.7 = (bf16[240,1280]{1,0:T(8,128)(2,1)}, bf16[240,1280]{1,0:T(8,128)(2,1)}, u32[]{:S(2)}, u32[]{:S(2)}) collective-permute-start(bf16[240,1280]{1,0:T(8,128)(2,1)} %collective-permute-done.3.refs_2_), channel_id=1, source_target_pairs={{0,64},{32,96},{64,128},{96,160},{128,192},{160,224},{192,256},{22... | collective-permute-start | bytes 1843208 | tf_op jit(solution)/shard_map/ppermute | solution.py:28
  101.1 4.5 %collective-permute-start.8 = (bf16[240,1280]{1,0:T(8,128)(2,1)}, bf16[240,1280]{1,0:T(8,128)(2,1)}, u32[]{:S(2)}, u32[]{:S(2)}) collective-permute-start(bf16[240,1280]{1,0:T(8,128)(2,1)} %collective-permute-done.4.refs_3_), channel_id=1, source_target_pairs={{0,448},{32,480},{64,0},{96,32},{128,64},{160,96},{192,128},{224,1... | collective-permute-start | bytes 1843208 | tf_op jit(solution)/shard_map/ppermute | solution.py:28
  107.6 3.8 %project.6.refs_6_ = bf16[3840,512]{1,0:T(8,128)(2,1)} custom-call(s32[4]{0:T(128)S(1)} %pad_add_fusion.2.refs_0_, bf16[1280,512]{1,0:T(8,128)(2,1)S(1)} %normalize_rows.1.refs_1_, bf16[240,1280]{1,0:T(8,128)(2,1)} %collective-permute-done.refs_2_, bf16[240,1280]{1,0:T(8,128)(2,1)} %collective-permute-done.1.refs_3_, ...), custom_call_target="tpu_custom_call", output_to_operand_aliasing={{}: (6, {})} | custom-call | tf_op jit(solution)/shard_map/project/pallas_call | solution.py:130
  111.4 6.7 %collective-permute-done.7.refs_2_ = bf16[240,1280]{1,0:T(8,128)(2,1)} collective-permute-done((bf16[240,1280]{1,0:T(8,128)(2,1)}, bf16[240,1280]{1,0:T(8,128)(2,1)}, u32[]{:S(2)}, u32[]{:S(2)}) %collective-permute-start.7) | collective-permute-done | bytes 614432 | tf_op jit(solution)/shard_map/ppermute | solution.py:28
  125.5 2.5 %collective-permute-start.11 = (bf16[160,1280]{1,0:T(8,128)(2,1)}, bf16[160,1280]{1,0:T(8,128)(2,1)S(1)}, u32[]{:S(2)}, u32[]{:S(2)}) collective-permute-start(bf16[160,1280]{1,0:T(8,128)(2,1)} %slice.22), channel_id=1, source_target_pairs={{0,64},{32,96},{64,128},{96,160},{128,192},{160,224},{192,256},{22... | collective-permute-start | bytes 1228808 | tf_op jit(solution)/shard_map/ppermute | solution.py:28
  129.6 5.0 %collective-permute-start.12 = (bf16[80,1280]{1,0:T(8,128)(2,1)}, bf16[80,1280]{1,0:T(8,128)(2,1)}, u32[]{:S(2)}, u32[]{:S(2)}) collective-permute-start(bf16[80,1280]{1,0:T(8,128)(2,1)} %slice.23), channel_id=1, source_target_pairs={{0,448},{32,480},{64,0},{96,32},{128,64},{160,96},{192,128},{224,1... | collective-permute-start | bytes 614408 | tf_op jit(solution)/shard_map/ppermute | solution.py:28
  134.7 3.8 %project.7.refs_6_ = bf16[3840,512]{1,0:T(8,128)(2,1)} custom-call(s32[4]{0:T(128)S(1)} %pad_add_fusion.3.refs_0_, bf16[1280,512]{1,0:T(8,128)(2,1)S(1)} %normalize_rows.1.refs_1_, bf16[240,1280]{1,0:T(8,128)(2,1)} %collective-permute-done.3.refs_2_, bf16[240,1280]{1,0:T(8,128)(2,1)} %collective-permute-done.4.refs_3_, ...), custom_call_target="tpu_custom_call", output_to_operand_aliasing={{}: (6, {})} | custom-call | tf_op jit(solution)/shard_map/project/pallas_call | solution.py:130
  145.4 3.9 %project.8.refs_6_ = bf16[3840,512]{1,0:T(8,128)(2,1)} custom-call(s32[4]{0:T(128)S(1)} %pad_add_fusion.4.refs_0_, bf16[1280,512]{1,0:T(8,128)(2,1)S(1)} %normalize_rows.1.refs_1_, bf16[240,1280]{1,0:T(8,128)(2,1)} %collective-permute-done.7.refs_2_, bf16[240,1280]{1,0:T(8,128)(2,1)} %collective-permute-done.8.refs_3_, ...), custom_call_target="tpu_custom_call", output_to_operand_aliasing={{}: (6, {})} | custom-call | tf_op jit(solution)/shard_map/project/pallas_call | solution.py:130
  152.7 2.8 %project.9.refs_0_ = bf16[3840,512]{1,0:T(8,128)(2,1)} custom-call(s32[4]{0:T(128)S(1)} %pad_add_fusion.1.refs_0_, bf16[1280,512]{1,0:T(8,128)(2,1)S(1)} %normalize_rows.1.refs_1_, bf16[160,1280]{1,0:T(8,128)(2,1)S(1)} %copy-done.5, bf16[80,1280]{1,0:T(8,128)(2,1)} %collective-permute-done.12.refs_3_, ...), custom_call_target="tpu_custom_call", output_to_operand_aliasing={{}: (6, {})} | custom-call | tf_op jit(solution)/shard_map/project/pallas_call | solution.py:130
  155.6 9.0 %attention.1.context_ref = bf16[512,1280]{1,0:T(8,128)(2,1)S(1)} custom-call(bf16[3840,512]{1,0:T(8,128)(2,1)} %project.9.refs_0_, s32[512,1]{1,0:T(8,128)S(1)} %copy.31.refs_1_, s32[4,128]{1,0:T(4,128)S(1)} %get-tuple-element.61.refs_2_), custom_call_target="tpu_custom_call" | custom-call | tf_op jit(solution)/shard_map/attention/pallas_call | solution.py:173
  164.7 5.1 %merge_tokens.1 = bf16[128,5120]{1,0:T(8,128)(2,1)S(1)} custom-call(s32[1]{0:T(128)} %bitcast.8.core_ref, bf16[512,1280]{1,0:T(8,128)(2,1)S(1)} %attention.1.context_ref, bf16[1280,640]{1,0:T(8,128)(2,1)S(1)} %bitcast.37, bf16[1280,640]{1,0:T(8,128)(2,1)} %collective-permute-done.17.w_other_ref, bf16[512,1280]{1,0:T(8,128)(2,1)S(1)} %copy-done.1, ...), custom_call_target="tpu_custom_call" | custom-call | tf_op jit(solution)/shard_map/merge_tokens/pallas_call | solution.py:223
  171.1 9.8 %all-to-all-start.3 = ((bf16[32,4,5120]{2,1,0:T(4,128)(2,1)}), bf16[32,4,5120]{2,1,0:T(4,128)(2,1)S(1)}, u32[]{:S(2)}, u32[]{:S(2)}) async-start(bf16[32,4,5120]{2,1,0:T(4,128)(2,1)} %reshape.69), calls=%async_computation.3 | async-start | bytes 2621440 | tf_op jit(solution)/shard_map/all_to_all | solution.py:282
  181.1 34.1 %all-to-all-done.3 = bf16[32,4,5120]{2,1,0:T(4,128)(2,1)S(1)} async-done(((bf16[32,4,5120]{2,1,0:T(4,128)(2,1)}), bf16[32,4,5120]{2,1,0:T(4,128)(2,1)S(1)}, u32[]{:S(2)}, u32[]{:S(2)}) %all-to-all-start.3) | async-done | bytes 1310752 | tf_op jit(solution)/shard_map/all_to_all | solution.py:282
  (95 shorter events, 42.3 us)
Async XLA Ops:
  2.9 42.5 %copy-start.7 = (bf16[40,80]{1,0:T(8,128)(2,1)S(1)}, bf16[40,80]{1,0:T(8,128)(2,1)}, u32[]{:S(2)}) copy-start(bf16[40,80]{1,0:T(8,128)(2,1)} %param.11) | copy-start | bytes 19204
  2.9 50.4 %copy-start.8 = (f32[1280]{0:T(1024)S(1)}, f32[1280]{0:T(1024)}, u32[]{:S(2)}) copy-start(f32[1280]{0:T(1024)} %param.9) | copy-start | bytes 15364
  2.9 50.4 %copy-start = (bf16[512,1280]{1,0:T(8,128)(2,1)S(1)}, bf16[512,1280]{1,0:T(8,128)(2,1)}, u32[]{:S(2)}) copy-start(bf16[512,1280]{1,0:T(8,128)(2,1)} %x_ref.3) | copy-start | bytes 3932164
  36.2 26.2 %collective-permute-start = (bf16[240,1280]{1,0:T(8,128)(2,1)S(1)}, bf16[240,1280]{1,0:T(8,128)(2,1)}, u32[]{:S(2)}, u32[]{:S(2)}) collective-permute-start(bf16[240,1280]{1,0:T(8,128)(2,1)S(1)} %bitcast.38), channel_id=1, source_target_pairs={{0,64},{32,96},{64,128},{96,160},{128,192},{160,224},{192,256},{22... | collective-permute-start | bytes 1843208 | tf_op jit(solution)/shard_map/ppermute | solution.py:28
  39.7 22.7 %collective-permute-start.1 = (bf16[240,1280]{1,0:T(8,128)(2,1)S(1)}, bf16[240,1280]{1,0:T(8,128)(2,1)}, u32[]{:S(2)}, u32[]{:S(2)}) collective-permute-start(bf16[240,1280]{1,0:T(8,128)(2,1)S(1)} %bitcast.39), channel_id=1, source_target_pairs={{0,448},{32,480},{64,0},{96,32},{128,64},{160,96},{192,128},{224,1... | collective-permute-start | bytes 1843208 | tf_op jit(solution)/shard_map/ppermute | solution.py:28
  43.5 18.9 %collective-permute-start.2 = (bf16[240,1280]{1,0:T(8,128)(2,1)S(1)}, bf16[240,1280]{1,0:T(8,128)(2,1)}, u32[]{:S(2)}, u32[]{:S(2)}) collective-permute-start(bf16[240,1280]{1,0:T(8,128)(2,1)S(1)} %bitcast.40), channel_id=1, source_target_pairs={{0,32},{32,0},{64,96},{96,64},{128,160},{160,128},{192,224},{224,1... | collective-permute-start | bytes 1843208 | tf_op jit(solution)/shard_map/ppermute | solution.py:23
  46.1 16.3 %all-to-all-start.1 = ((bf16[16,40,80]{2,1,0:T(8,128)(2,1)}), bf16[16,40,80]{2,1,0:T(8,128)(2,1)S(1)}, u32[]{:S(2)}, u32[]{:S(2)}) async-start(bf16[16,40,80]{2,1,0:T(8,128)(2,1)} %broadcast_in_dim.91), calls=%async_computation.1 | async-start | bytes 327680 | tf_op jit(solution)/shard_map/all_to_all | solution.py:18
  64.2 85.1 %all-to-all-start.2 = ((bf16[32,40,640]{2,1,0:T(8,128)(2,1)}), bf16[32,40,640]{2,1,0:T(8,128)(2,1)S(1)}, u32[]{:S(2)}, u32[]{:S(2)}) async-start(bf16[32,40,640]{2,1,0:T(8,128)(2,1)} %broadcast_in_dim.103), calls=%async_computation.2 | async-start | bytes 3276800 | tf_op jit(solution)/shard_map/all_to_all | solution.py:18
  71.8 19.4 %collective-permute-start.3 = (bf16[240,1280]{1,0:T(8,128)(2,1)}, bf16[240,1280]{1,0:T(8,128)(2,1)}, u32[]{:S(2)}, u32[]{:S(2)}) collective-permute-start(bf16[240,1280]{1,0:T(8,128)(2,1)} %collective-permute-done.refs_2_), channel_id=1, source_target_pairs={{0,64},{32,96},{64,128},{96,160},{128,192},{160,224},{192,256},{22... | collective-permute-start | bytes 1843208 | tf_op jit(solution)/shard_map/ppermute | solution.py:28
  76.2 20.4 %collective-permute-start.5 = (bf16[240,1280]{1,0:T(8,128)(2,1)}, bf16[240,1280]{1,0:T(8,128)(2,1)}, u32[]{:S(2)}, u32[]{:S(2)}) collective-permute-start(bf16[240,1280]{1,0:T(8,128)(2,1)} %collective-permute-done.refs_2_), channel_id=1, source_target_pairs={{0,32},{32,0},{64,96},{96,64},{128,160},{160,128},{192,224},{224,1... | collective-permute-start | bytes 1843208 | tf_op jit(solution)/shard_map/ppermute | solution.py:23
  78.1 18.5 %collective-permute-start.4 = (bf16[240,1280]{1,0:T(8,128)(2,1)}, bf16[240,1280]{1,0:T(8,128)(2,1)}, u32[]{:S(2)}, u32[]{:S(2)}) collective-permute-start(bf16[240,1280]{1,0:T(8,128)(2,1)} %collective-permute-done.1.refs_3_), channel_id=1, source_target_pairs={{0,448},{32,480},{64,0},{96,32},{128,64},{160,96},{192,128},{224,1... | collective-permute-start | bytes 1843208 | tf_op jit(solution)/shard_map/ppermute | solution.py:28
  80.8 15.8 %collective-permute-start.6 = (bf16[240,1280]{1,0:T(8,128)(2,1)}, bf16[240,1280]{1,0:T(8,128)(2,1)}, u32[]{:S(2)}, u32[]{:S(2)}) collective-permute-start(bf16[240,1280]{1,0:T(8,128)(2,1)} %collective-permute-done.1.refs_3_), channel_id=1, source_target_pairs={{0,32},{32,0},{64,96},{96,64},{128,160},{160,128},{192,224},{224,1... | collective-permute-start | bytes 1843208 | tf_op jit(solution)/shard_map/ppermute | solution.py:23
  96.6 14.9 %collective-permute-start.10 = (bf16[240,1280]{1,0:T(8,128)(2,1)}, bf16[240,1280]{1,0:T(8,128)(2,1)}, u32[]{:S(2)}, u32[]{:S(2)}) collective-permute-start(bf16[240,1280]{1,0:T(8,128)(2,1)} %collective-permute-done.4.refs_3_), channel_id=1, source_target_pairs={{0,32},{32,0},{64,96},{96,64},{128,160},{160,128},{192,224},{224,1... | collective-permute-start | bytes 1843208 | tf_op jit(solution)/shard_map/ppermute | solution.py:23
  98.5 19.7 %collective-permute-start.7 = (bf16[240,1280]{1,0:T(8,128)(2,1)}, bf16[240,1280]{1,0:T(8,128)(2,1)}, u32[]{:S(2)}, u32[]{:S(2)}) collective-permute-start(bf16[240,1280]{1,0:T(8,128)(2,1)} %collective-permute-done.3.refs_2_), channel_id=1, source_target_pairs={{0,64},{32,96},{64,128},{96,160},{128,192},{160,224},{192,256},{22... | collective-permute-start | bytes 1843208 | tf_op jit(solution)/shard_map/ppermute | solution.py:28
  101.1 18.3 %collective-permute-start.8 = (bf16[240,1280]{1,0:T(8,128)(2,1)}, bf16[240,1280]{1,0:T(8,128)(2,1)}, u32[]{:S(2)}, u32[]{:S(2)}) collective-permute-start(bf16[240,1280]{1,0:T(8,128)(2,1)} %collective-permute-done.4.refs_3_), channel_id=1, source_target_pairs={{0,448},{32,480},{64,0},{96,32},{128,64},{160,96},{192,128},{224,1... | collective-permute-start | bytes 1843208 | tf_op jit(solution)/shard_map/ppermute | solution.py:28
  105.6 13.8 %collective-permute-start.9 = (bf16[240,1280]{1,0:T(8,128)(2,1)}, bf16[240,1280]{1,0:T(8,128)(2,1)}, u32[]{:S(2)}, u32[]{:S(2)}) collective-permute-start(bf16[240,1280]{1,0:T(8,128)(2,1)} %collective-permute-done.3.refs_2_), channel_id=1, source_target_pairs={{0,32},{32,0},{64,96},{96,64},{128,160},{160,128},{192,224},{224,1... | collective-permute-start | bytes 1843208 | tf_op jit(solution)/shard_map/ppermute | solution.py:23
  119.4 21.6 %collective-permute-start.13 = (bf16[240,1280]{1,0:T(8,128)(2,1)}, bf16[240,1280]{1,0:T(8,128)(2,1)}, u32[]{:S(2)}, u32[]{:S(2)}) collective-permute-start(bf16[240,1280]{1,0:T(8,128)(2,1)} %collective-permute-done.7.refs_2_), channel_id=1, source_target_pairs={{0,32},{32,0},{64,96},{96,64},{128,160},{160,128},{192,224},{224,1... | collective-permute-start | bytes 1843208 | tf_op jit(solution)/shard_map/ppermute | solution.py:23
  121.3 19.6 %collective-permute-start.14 = (bf16[240,1280]{1,0:T(8,128)(2,1)}, bf16[240,1280]{1,0:T(8,128)(2,1)}, u32[]{:S(2)}, u32[]{:S(2)}) collective-permute-start(bf16[240,1280]{1,0:T(8,128)(2,1)} %collective-permute-done.8.refs_3_), channel_id=1, source_target_pairs={{0,32},{32,0},{64,96},{96,64},{128,160},{160,128},{192,224},{224,1... | collective-permute-start | bytes 1843208 | tf_op jit(solution)/shard_map/ppermute | solution.py:23
  125.5 15.4 %collective-permute-start.11 = (bf16[160,1280]{1,0:T(8,128)(2,1)}, bf16[160,1280]{1,0:T(8,128)(2,1)S(1)}, u32[]{:S(2)}, u32[]{:S(2)}) collective-permute-start(bf16[160,1280]{1,0:T(8,128)(2,1)} %slice.22), channel_id=1, source_target_pairs={{0,64},{32,96},{64,128},{96,160},{128,192},{160,224},{192,256},{22... | collective-permute-start | bytes 1228808 | tf_op jit(solution)/shard_map/ppermute | solution.py:28
  129.6 9.8 %collective-permute-start.12 = (bf16[80,1280]{1,0:T(8,128)(2,1)}, bf16[80,1280]{1,0:T(8,128)(2,1)}, u32[]{:S(2)}, u32[]{:S(2)}) collective-permute-start(bf16[80,1280]{1,0:T(8,128)(2,1)} %slice.23), channel_id=1, source_target_pairs={{0,448},{32,480},{64,0},{96,32},{128,64},{160,96},{192,128},{224,1... | collective-permute-start | bytes 614408 | tf_op jit(solution)/shard_map/ppermute | solution.py:28
  140.9 8.4 %collective-permute-start.15 = (bf16[160,1280]{1,0:T(8,128)(2,1)S(1)}, bf16[160,1280]{1,0:T(8,128)(2,1)}, u32[]{:S(2)}, u32[]{:S(2)}) collective-permute-start(bf16[160,1280]{1,0:T(8,128)(2,1)S(1)} %collective-permute-done.11.refs_2_), channel_id=1, source_target_pairs={{0,32},{32,0},{64,96},{96,64},{128,160},{160,128},{192,224},{224,1... | collective-permute-start | bytes 1228808 | tf_op jit(solution)/shard_map/ppermute | solution.py:23
  142.8 6.4 %collective-permute-start.16 = (bf16[80,1280]{1,0:T(8,128)(2,1)}, bf16[80,1280]{1,0:T(8,128)(2,1)}, u32[]{:S(2)}, u32[]{:S(2)}) collective-permute-start(bf16[80,1280]{1,0:T(8,128)(2,1)} %collective-permute-done.12.refs_3_), channel_id=1, source_target_pairs={{0,32},{32,0},{64,96},{96,64},{128,160},{160,128},{192,224},{224,1... | collective-permute-start | bytes 614408 | tf_op jit(solution)/shard_map/ppermute | solution.py:23
  149.3 15.3 %collective-permute-start.17 = (bf16[1280,640]{1,0:T(8,128)(2,1)S(1)}, bf16[1280,640]{1,0:T(8,128)(2,1)}, u32[]{:S(2)}, u32[]{:S(2)}) collective-permute-start(bf16[1280,640]{1,0:T(8,128)(2,1)S(1)} %bitcast.36), channel_id=1, source_target_pairs={{0,32},{32,0},{64,96},{96,64},{128,160},{160,128},{192,224},{224,1... | collective-permute-start | bytes 4915208 | tf_op jit(solution)/shard_map/ppermute | solution.py:23
  171.1 44.1 %all-to-all-start.3 = ((bf16[32,4,5120]{2,1,0:T(4,128)(2,1)}), bf16[32,4,5120]{2,1,0:T(4,128)(2,1)S(1)}, u32[]{:S(2)}, u32[]{:S(2)}) async-start(bf16[32,4,5120]{2,1,0:T(4,128)(2,1)} %reshape.69), calls=%async_computation.3 | async-start | bytes 2621440 | tf_op jit(solution)/shard_map/all_to_all | solution.py:282
  (8 other events, 66.5 us)

commit v6 on v5

--- a/solution.py
+++ b/solution.py
@@ -28,48 +28,41 @@
     return lax.ppermute(x, "pipe", [(p, (p + 2 * chips) % size) for p in range(size)])
 
 
-def ring_project(slab, normed, w_out, core, early):
+def ring_project(slab, patches, gain, w_out, core, early):
     rows = slab.shape[0]
     size = lax.axis_size("pipe")
     place = lax.axis_index("pipe").astype(jnp.int32)
     together = lax.optimization_barrier
-
-    def firsts(pieces):
-        owners = [(place + owner, offset) for owner, offset in pieces]
-        owners += [((place ^ 1) + owner, offset) for owner, offset in pieces]
-        return jnp.stack([((owner + size) % size) * rows + offset for owner, offset in owners])
-
-    cut = rows * 2 // 3
-    near = [(0, 0)], [(-2, 0), (2, 0)], [(-4, 0), (4, 0)], [(-6, 0), (6, 0)], [(8, 0), (8, cut)]
+    other = partner_copy(patches)
+    normed = normalize_rows(patches, other, gain)
+
     a1, b1 = chip_copy(slab, 1), chip_copy(slab, -1)
     blocks = copy_for_each(w_out, "pipe")
-    other = partner_copy(slab)
-    a1, b1, other, normed, blocks = together((a1, b1, other, normed, blocks))
+    a1, b1, normed, blocks, early = together((a1, b1, normed, blocks, early))
 
     a2, b2 = chip_copy(a1, 1), chip_copy(b1, -1)
-    pa1, pb1 = partner_copy(a1), partner_copy(b1)
     half = blocks.shape[0] * blocks.shape[2] // 2
     out_rows = jnp.moveaxis(blocks, 0, 1).reshape(blocks.shape[1], 2, half)
     out_rows = lax.dynamic_index_in_dim(out_rows, core[0], axis=1, keepdims=False)
     out_own = copy_for_each(out_rows, "tensor")
-    buffer = project(normed, [slab, other], firsts(near[0]), None)
-    a2, b2, pa1, pb1, buffer, early = together((a2, b2, pa1, pb1, buffer, early))
+    a2, b2 = together((a2, b2))
 
     a3, b3 = chip_copy(a2, 1), chip_copy(b2, -1)
-    pa2, pb2 = partner_copy(a2), partner_copy(b2)
-    buffer = project(normed, [a1, b1, pa1, pb1], firsts(near[1]), buffer)
-    a3, b3, pa2, pb2, buffer = together((a3, b3, pa2, pb2, buffer))
-
-    a4, b4 = chip_copy(a3[:cut], 1), chip_copy(b3[cut:], -1)
-    pa3, pb3 = partner_copy(a3), partner_copy(b3)
-    buffer = project(normed, [a2, b2, pa2, pb2], firsts(near[2]), buffer)
-    a4, b4, pa3, pb3, buffer = together((a4, b4, pa3, pb3, buffer))
-
-    pa4, pb4 = partner_copy(a4), partner_copy(b4)
-    buffer = project(normed, [a3, b3, pa3, pb3], firsts(near[3]), buffer)
-    pa4, pb4, buffer, out_own = together((pa4, pb4, buffer, out_own))
-    buffer = project(normed, [a4, b4, pa4, pb4], firsts(near[4]), buffer)
-    return buffer, out_own.reshape(-1, half), early
+    own1, sent1 = project(normed, [slab, a1, b1, a2, b2])
+    a3, b3, own1, sent1 = together((a3, b3, own1, sent1))
+
+    a4 = chip_copy(a3, 1)
+    got1 = partner_copy(sent1)
+    own2, sent2 = project(normed, [a3, b3])
+    a4, own2, sent2 = together((a4, own2, sent2))
+
+    own3, sent3 = project(normed, [a4])
+    got2, got3 = partner_copy(sent2), partner_copy(sent3)
+    got3, out_own = together((got3, out_own))
+    owners = [0, -2, 2, -4, 4, -6, 6, 8]
+    owners = [place + owner for owner in owners] + [(place ^ 1) + owner for owner in owners]
+    firsts = jnp.stack([(owner + size) % size * rows for owner in owners])
+    return (firsts, own1, own2, own3, got1, got2, got3), out_own.reshape(-1, half), early
 
 
 def on_chip(x):
@@ -84,73 +77,81 @@
     return [pl.BlockSpec(memory_space=pltpu.VMEM)] * count
 
 
-def normalize_kernel(x_ref, gain_ref, out_ref):
-    x = x_ref[...].astype(jnp.float32)
-    scale = lax.rsqrt(jnp.mean(x * x, axis=-1, keepdims=True) + epsilon)
-    out_ref[...] = (x * scale * gain_ref[...]).astype(jnp.bfloat16).T
-
-
-def normalize_rows(x, gain):
+def normalize_kernel(x_ref, other_ref, gain_ref, out_ref):
+    count = x_ref.shape[0]
+    for at, ref in enumerate((x_ref, other_ref)):
+        x = ref[...].astype(jnp.float32)
+        scale = lax.rsqrt(jnp.mean(x * x, axis=-1, keepdims=True) + epsilon)
+        normed = (x * scale * gain_ref[...]).astype(jnp.bfloat16)
+        out_ref[:, at * count : (at + 1) * count] = normed.T
+
+
+def normalize_rows(x, other, gain):
     return pl.pallas_call(
         normalize_kernel,
-        in_specs=in_vmem(2),
+        in_specs=in_vmem(3),
         out_specs=pl.BlockSpec(memory_space=pltpu.VMEM),
-        out_shape=jax.ShapeDtypeStruct((x.shape[1], x.shape[0]), jnp.bfloat16),
-        compiler_params=pltpu.CompilerParams(vmem_limit_bytes=16 << 20),
+        out_shape=jax.ShapeDtypeStruct((x.shape[1], 2 * x.shape[0]), jnp.bfloat16),
+        compiler_params=pltpu.CompilerParams(vmem_limit_bytes=20 << 20),
         name="normalize_rows",
-    )(x, gain)
-
-
-def project_kernel(first_ref, normed_ref, *refs, pieces, aliased):
-    slab_refs = refs[:pieces]
-    out_ref, part_ref, sems = refs[pieces + aliased :]
-    copies = []
-    at = 0
-    for piece, slab_ref in enumerate(slab_refs):
-        rows = slab_ref.shape[0]
-        part_ref[at : at + rows, :] = jnp.dot(
+    )(x, other, gain)
+
+
+def project_kernel(normed_ref, *refs):
+    *slab_refs, own_ref, sent_ref = refs
+    count = own_ref.shape[1]
+    rows = slab_refs[0].shape[0]
+    for at, slab_ref in enumerate(slab_refs):
+        part = jnp.dot(
             slab_ref[...], normed_ref[...], preferred_element_type=jnp.float32
         ).astype(jnp.bfloat16)
-        first = pl.multiple_of(first_ref[piece], 80)
-        copies.append(
-            pltpu.make_async_copy(
-                part_ref.at[at : at + rows, :], out_ref.at[pl.ds(first, rows), :], sems.at[piece]
-            )
-        )
-        copies[-1].start()
-        at += rows
-    for copy in copies:
-        copy.wait()
-
-
-def project(normed, slabs, firsts, buffer):
-    width, count = normed.shape
-    aliased = buffer is not None
-    rows = sum(slab.shape[0] for slab in slabs)
+        own_ref[at * rows : (at + 1) * rows, :] = part[:, :count]
+        sent_ref[at * rows : (at + 1) * rows, :] = part[:, count:]
+
+
+def project(normed, slabs):
+    count = normed.shape[1] // 2
+    shape = jax.ShapeDtypeStruct((len(slabs) * slabs[0].shape[0], count), jnp.bfloat16)
     return pl.pallas_call(
-        lambda *refs: project_kernel(*refs, pieces=len(slabs), aliased=aliased),
-        in_specs=[pl.BlockSpec(memory_space=pltpu.SMEM)]
-        + in_vmem(1 + len(slabs))
-        + [pl.BlockSpec(memory_space=pltpu.HBM)] * aliased,
-        out_specs=pl.BlockSpec(memory_space=pltpu.HBM),
-        out_shape=pltpu.HBM((3 * width, count), jnp.bfloat16),
-        scratch_shapes=[
-            pltpu.VMEM((rows, count), jnp.bfloat16),
-            pltpu.SemaphoreType.DMA((len(slabs),)),
-        ],
-        input_output_aliases={2 + len(slabs): 0} if aliased else {},
-        compiler_params=pltpu.CompilerParams(vmem_limit_bytes=16 << 20),
+        project_kernel,
+        in_specs=in_vmem(1 + len(slabs)),
+        out_specs=in_vmem(2),
+        out_shape=[shape, shape],
+        compiler_params=pltpu.CompilerParams(vmem_limit_bytes=20 << 20),
         name="project",
-    )(firsts, normed, *slabs, *([in_hbm(buffer)] if aliased else []))
-
-
-def attention_kernel(qkv_ref, key_ref, query_ref, out_ref, context_ref, *, head_width):
+    )(normed, *slabs)
+
+
+def attention_kernel(first_ref, *refs, pieces, head_width, rows):
+    piece_refs = refs[:pieces]
+    key_ref, query_ref, out_ref, qkv_ref, context_ref, sems = refs[pieces:]
     width = out_ref.shape[1]
-    query_id = query_ref[pl.ds(pl.program_id(0), 1), :]
+
+    @pl.when(pl.program_id(0) == 0)
+    def _():
+        copies = []
+        for piece_ref in piece_refs:
+            for at in range(0, piece_ref.shape[0], rows):
+                number = len(copies)
+                first = pl.multiple_of(first_ref[number], rows)
+                copies.append(
+                    pltpu.make_async_copy(
+                        piece_ref.at[at : at + rows, :],
+                        qkv_ref.at[pl.ds(first, rows), :],
+                        sems.at[number],
+                    )
+                )
+                copies[-1].start()
+        for copy in copies:
+            copy.wait()
+
+    unit = pl.program_id(0)
+    patches = pl.ds(pl.multiple_of(unit * UNIT, UNIT), UNIT)
+    query_id = query_ref[pl.ds(unit, 1), :]
     allowed = key_ref[...] == query_id
     for head in range(width // head_width):
         query, key, value = (
-            qkv_ref[part * width + head * head_width : part * width + (head + 1) * head_width, :]
+            qkv_ref[part * width + head * head_width : part * width + (head + 1) * head_width, patches]
             for part in range(3)
         )
         scores = lax.dot_general(
@@ -167,25 +168,34 @@
     out_ref[...] = context_ref[...].T
 
 
-def attention(qkv, key_id, query_id):
-    width, count = qkv.shape[0] // 3, qkv.shape[1]
-    units = count // UNIT
+def attention(pieces, rows, key_id, query_id):
+    firsts, *pieces = pieces
+    units, count = query_id.shape[0], pieces[0].shape[1]
+    total = sum(piece.shape[0] for piece in pieces)
+    width = total // 3
     return pl.pallas_call(
-        lambda *refs: attention_kernel(*refs, head_width=width // HEADS),
+        lambda *refs: attention_kernel(
+            *refs, pieces=len(pieces), head_width=width // HEADS, rows=rows
+        ),
         grid=(units,),
-        in_specs=[
-            pl.BlockSpec((3 * width, UNIT), lambda n: (0, n)),
+        in_specs=[pl.BlockSpec(memory_space=pltpu.SMEM)]
+        + [pl.BlockSpec(memory_space=pltpu.HBM)] * len(pieces)
+        + [
             pl.BlockSpec((UNIT, 1), lambda n: (n, 0)),
             pl.BlockSpec((units, UNIT), lambda n: (0, 0)),
         ],
         out_specs=pl.BlockSpec((UNIT, width), lambda n: (n, 0)),
         out_shape=jax.ShapeDtypeStruct((count, width), jnp.bfloat16),
-        scratch_shapes=[pltpu.VMEM((width, UNIT), jnp.bfloat16)],
+        scratch_shapes=[
+            pltpu.VMEM((total, count), jnp.bfloat16),
+            pltpu.VMEM((width, UNIT), jnp.bfloat16),
+            pltpu.SemaphoreType.DMA((total // rows,)),
+        ],
         compiler_params=pltpu.CompilerParams(
-            dimension_semantics=("arbitrary",), vmem_limit_bytes=16 << 20
+            dimension_semantics=("arbitrary",), vmem_limit_bytes=20 << 20
         ),
         name="attention",
-    )(in_hbm(qkv), key_id, query_id)
+    )(firsts, *(in_hbm(piece) for piece in pieces), key_id, query_id)
 
 
 def merge_kernel(
@@ -268,15 +278,14 @@
     dest_rows = destination_rows(info[:, :slots], info[:, slots:])
 
     slab, w_out = lax.optimization_barrier((slab, w_out))
-    normed = normalize_rows(patches, attn_gain[None, :])
     live = jnp.arange(patch_count, dtype=jnp.int32) < jnp.sum(image_patches)
     key_id = jnp.where(live, window_ids, -1)[:, None]
     query_id = jnp.where(live, window_ids, -2).reshape(patch_count // UNIT, UNIT)
-    qkv, out_own, (key_id, query_id, dest_rows) = ring_project(
-        slab, normed, w_out, core, (key_id, query_id, dest_rows)
+    pieces, out_own, (key_id, query_id, dest_rows) = ring_project(
+        slab, patches, attn_gain[None, :], w_out, core, (key_id, query_id, dest_rows)
     )
     out_other = partner_copy(out_own)
-    context = attention(qkv, key_id, query_id)
+    context = attention(pieces, qkv_part, key_id, query_id)
     tokens = merge_tokens(core, context, out_own, out_other, patches, merge_gain[None, :])
     outgoing = tokens.reshape(group_size, token_count // group_size, 4 * width)
     received = lax.all_to_all(outgoing, "tensor", split_axis=0, concat_axis=0, tiled=True)

time: 218 us -> 209 us (0.959)
  blocking collectives: 33 us -> 0 us
  waiting for transfers between devices: 62.1 us -> 93.4 us
  Pallas kernels: 31.7 us -> 23.9 us
  local copies, waits for them, and re-layouts: 11.8 us -> 15.1 us
  starting transfers between devices: 72 us -> 69.5 us
    all_to_all x1 -> x0, blocking collectives: 33 us -> none  [copy_for_each(): lax.all_to_all(jnp.broadcast_to(x[None], (size, *x.shape)), axis, 0, 0, t...]
    ppermute x8 -> x7, waiting for transfers between devices: 19.5 us -> 35.1 us  [chip_copy(): lax.ppermute(x, 'pipe', [(p, (p + 2 * chips) % size) for p in range(size)])]
    all_to_all x2 -> x3, waiting for transfers between devices: 8.43 us -> 21.8 us  [copy_for_each(): lax.all_to_all(jnp.broadcast_to(x[None], (size, *x.shape)), axis, 0, 0, t...]
    all_to_all x2 -> x3, starting transfers between devices: 12.8 us -> 25.7 us  [copy_for_each(): lax.all_to_all(jnp.broadcast_to(x[None], (size, *x.shape)), axis, 0, 0, t...]
    ppermute x10 -> x5, starting transfers between devices: 20.6 us -> 10.4 us  [partner_copy(): return lax.ppermute(x, 'pipe', [(p, p ^ 1) for p in range(size)])]
    pallas_call x7 -> x5, Pallas kernels: 26.6 us -> 18.8 us  [the longest x1 10.7 us: attention(): pl.pallas_call(lambda *refs: attention_kernel(*refs, pieces=len(pieces),...]
    ppermute x8 -> x7, starting transfers between devices: 28.9 us -> 23.7 us  [chip_copy(): lax.ppermute(x, 'pipe', [(p, (p + 2 * chips) % size) for p in range(size)])]
    slice x2 -> x0, local copies, waits for them, and re-layouts: 3.4 us -> none  [ring_project(): a4, b4 = (chip_copy(a3[:cut], 1), chip_copy(b3[cut:], -1))]
  transfers between devices with their start and end apart: 21 -> 16, of which waited for: 8 -> 10; matrix products, arithmetic and copies ran while one was open for 3% -> 2% of each run, Pallas kernels for 12% -> 9%
where the time goes in v6:
time: 209 us; the launch traced here: 208 us
  waiting for transfers between devices  93.4 us (45%)
  starting transfers between devices  69.5 us (33%)
  Pallas kernels  23.9 us (11%)
  local copies, waits for them, and re-layouts  15.1 us (7%)
  other arithmetic  3.9 us (2%)
    ppermute x7, waiting for transfers between devices, chip_copy(): lax.ppermute(x, 'pipe', [(p, (p + 2 * chips) % size) for p in range(size)])  35.1 us
    all_to_all x1, waiting for transfers between devices, body(): lax.all_to_all(outgoing, 'tensor', split_axis=0, concat_axis=0, tiled=True)  33.8 us
    all_to_all x3, starting transfers between devices, copy_for_each(): lax.all_to_all(jnp.broadcast_to(x[None], (size, *x.shape)), axis, 0, 0, t...  25.7 us
    ppermute x7, starting transfers between devices, chip_copy(): lax.ppermute(x, 'pipe', [(p, (p + 2 * chips) % size) for p in range(size)])  23.7 us
    all_to_all x3, waiting for transfers between devices, copy_for_each(): lax.all_to_all(jnp.broadcast_to(x[None], (size, *x.shape)), axis, 0, 0, t...  21.8 us
    pallas_call x1, Pallas kernels, attention(): pl.pallas_call(lambda *refs: attention_kernel(*refs, pieces=len(pieces),...  10.7 us
    ppermute x5, starting transfers between devices, partner_copy(): return lax.ppermute(x, 'pipe', [(p, p ^ 1) for p in range(size)])  10.4 us
    all_to_all x1, starting transfers between devices, body(): lax.all_to_all(outgoing, 'tensor', split_axis=0, concat_axis=0, tiled=True)  9.77 us
  transfers between devices with their start and end apart: 16, of which 10 were waited for; matrix products, arithmetic and copies ran while one was open for 2% of the time, Pallas kernels for 9%

profile of v6, /device:TPU:4, one launch (start us, length us, event | category | flops | bytes accessed | tf_op | source)
XLA Modules:
  0.0 208.1 jit_solution(10211159559659416515)
XLA Ops:
  3.8 13.6 %all-to-all-start = ((bf16[32,40,248]{2,1,0:T(8,128)(2,1)}), bf16[32,40,248]{2,1,0:T(8,128)(2,1)}, u32[]{:S(2)}, u32[]{:S(2)}) async-start(bf16[32,40,248]{2,1,0:T(8,128)(2,1)} %broadcast_in_dim.89), calls=%async_computation | async-start | bytes 1310720 | tf_op jit(solution)/shard_map/all_to_all | solution.py:18
  17.5 1.9 collective-permute-start.2
  20.2 17.0 %all-to-all-done = bf16[32,40,248]{2,1,0:T(8,128)(2,1)} async-done(((bf16[32,40,248]{2,1,0:T(8,128)(2,1)}), bf16[32,40,248]{2,1,0:T(8,128)(2,1)}, u32[]{:S(2)}, u32[]{:S(2)}) %all-to-all-start) | async-done | bytes 634912 | tf_op jit(solution)/shard_map/all_to_all | solution.py:18
  38.5 5.4 %collective-permute-start.1 = (bf16[240,1280]{1,0:T(8,128)(2,1)S(1)}, bf16[240,1280]{1,0:T(8,128)(2,1)}, u32[]{:S(2)}, u32[]{:S(2)}) collective-permute-start(bf16[240,1280]{1,0:T(8,128)(2,1)S(1)} %bitcast.34), channel_id=1, source_target_pairs={{0,448},{32,480},{64,0},{96,32},{128,64},{160,96},{192,128},{224,1... | collective-permute-start | bytes 1843208 | tf_op jit(solution)/shard_map/ppermute | solution.py:28
  43.9 1.9 collective-permute-start
  48.3 5.8 %all-to-all-start.1 = ((bf16[16,40,80]{2,1,0:T(8,128)(2,1)}), bf16[16,40,80]{2,1,0:T(8,128)(2,1)S(1)}, u32[]{:S(2)}, u32[]{:S(2)}) async-start(bf16[16,40,80]{2,1,0:T(8,128)(2,1)} %broadcast_in_dim.91), calls=%async_computation.1 | async-start | bytes 327680 | tf_op jit(solution)/shard_map/all_to_all | solution.py:18
  59.1 4.8 %all-to-all-done.1 = bf16[16,40,80]{2,1,0:T(8,128)(2,1)S(1)} async-done(((bf16[16,40,80]{2,1,0:T(8,128)(2,1)}), bf16[16,40,80]{2,1,0:T(8,128)(2,1)S(1)}, u32[]{:S(2)}, u32[]{:S(2)}) %all-to-all-start.1) | async-done | bytes 102432 | tf_op jit(solution)/shard_map/all_to_all | solution.py:18
  67.3 6.4 %all-to-all-start.2 = ((bf16[32,40,640]{2,1,0:T(8,128)(2,1)}), bf16[32,40,640]{2,1,0:T(8,128)(2,1)}, u32[]{:S(2)}, u32[]{:S(2)}) async-start(bf16[32,40,640]{2,1,0:T(8,128)(2,1)} %broadcast_in_dim.103), calls=%async_computation.2 | async-start | bytes 3276800 | tf_op jit(solution)/shard_map/all_to_all | solution.py:18
  73.6 2.7 %collective-permute-start.3 = (bf16[240,1280]{1,0:T(8,128)(2,1)}, bf16[240,1280]{1,0:T(8,128)(2,1)S(1)}, u32[]{:S(2)}, u32[]{:S(2)}) collective-permute-start(bf16[240,1280]{1,0:T(8,128)(2,1)} %collective-permute-done.refs_1_), channel_id=1, source_target_pairs={{0,64},{32,96},{64,128},{96,160},{128,192},{160,224},{192,256},{22... | collective-permute-start | bytes 1843208 | tf_op jit(solution)/shard_map/ppermute | solution.py:28
  76.4 4.3 %collective-permute-start.4 = (bf16[240,1280]{1,0:T(8,128)(2,1)}, bf16[240,1280]{1,0:T(8,128)(2,1)S(1)}, u32[]{:S(2)}, u32[]{:S(2)}) collective-permute-start(bf16[240,1280]{1,0:T(8,128)(2,1)} %collective-permute-done.1.refs_2_), channel_id=1, source_target_pairs={{0,448},{32,480},{64,0},{96,32},{128,64},{160,96},{192,128},{224,1... | collective-permute-start | bytes 1843208 | tf_op jit(solution)/shard_map/ppermute | solution.py:28
  80.7 12.0 %collective-permute-done.3.refs_3_ = bf16[240,1280]{1,0:T(8,128)(2,1)S(1)} collective-permute-done((bf16[240,1280]{1,0:T(8,128)(2,1)}, bf16[240,1280]{1,0:T(8,128)(2,1)S(1)}, u32[]{:S(2)}, u32[]{:S(2)}) %collective-permute-start.3) | collective-permute-done | bytes 614432 | tf_op jit(solution)/shard_map/ppermute | solution.py:28
  94.0 3.1 %collective-permute-start.5 = (bf16[240,1280]{1,0:T(8,128)(2,1)S(1)}, bf16[240,1280]{1,0:T(8,128)(2,1)S(1)}, u32[]{:S(2)}, u32[]{:S(2)}) collective-permute-start(bf16[240,1280]{1,0:T(8,128)(2,1)S(1)} %collective-permute-done.3.refs_3_), channel_id=1, source_target_pairs={{0,64},{32,96},{64,128},{96,160},{128,192},{160,224},{192,256},{22... | collective-permute-start | bytes 1843208 | tf_op jit(solution)/shard_map/ppermute | solution.py:28
  97.1 4.3 %collective-permute-start.6 = (bf16[240,1280]{1,0:T(8,128)(2,1)S(1)}, bf16[240,1280]{1,0:T(8,128)(2,1)S(1)}, u32[]{:S(2)}, u32[]{:S(2)}) collective-permute-start(bf16[240,1280]{1,0:T(8,128)(2,1)S(1)} %collective-permute-done.4.refs_4_), channel_id=1, source_target_pairs={{0,448},{32,480},{64,0},{96,32},{128,64},{160,96},{192,128},{224,1... | collective-permute-start | bytes 1843208 | tf_op jit(solution)/shard_map/ppermute | solution.py:28
  101.4 4.6 %project.3 = (bf16[1200,512]{1,0:T(8,128)(2,1)S(1)}, bf16[1200,512]{1,0:T(8,128)(2,1)S(1)}) custom-call(bf16[1280,1024]{1,0:T(8,128)(2,1)S(1)} %normalize_rows.1.normed_ref, bf16[240,1280]{1,0:T(8,128)(2,1)S(1)} %bitcast.36, bf16[240,1280]{1,0:T(8,128)(2,1)} %collective-permute-done.refs_1_, bf16[240,1280]{1,0:T(8,128)(2,1)} %collective-permute-done.1.refs_2_, ...), custom_call_target="tpu_custom_call" | custom-call | tf_op jit(solution)/shard_map/project/pallas_call | solution.py:115
  106.0 6.4 %collective-permute-done.5.refs_0_ = bf16[240,1280]{1,0:T(8,128)(2,1)S(1)} collective-permute-done((bf16[240,1280]{1,0:T(8,128)(2,1)S(1)}, bf16[240,1280]{1,0:T(8,128)(2,1)S(1)}, u32[]{:S(2)}, u32[]{:S(2)}) %collective-permute-start.5) | collective-permute-done | bytes 614432 | tf_op jit(solution)/shard_map/ppermute | solution.py:28
  117.0 14.3 %collective-permute-done.7.refs_0_ = bf16[240,1280]{1,0:T(8,128)(2,1)S(1)} collective-permute-done((bf16[240,1280]{1,0:T(8,128)(2,1)S(1)}, bf16[240,1280]{1,0:T(8,128)(2,1)S(1)}, u32[]{:S(2)}, u32[]{:S(2)}) %collective-permute-start.7) | collective-permute-done | bytes 614432 | tf_op jit(solution)/shard_map/ppermute | solution.py:28
  132.8 1.9 collective-permute-start.10
  136.2 2.0 collective-permute-start.11
  138.2 2.3 %collective-permute-start.8 = (bf16[1200,512]{1,0:T(8,128)(2,1)}, bf16[1200,512]{1,0:T(8,128)(2,1)}, u32[]{:S(2)}, u32[]{:S(2)}) collective-permute-start(bf16[1200,512]{1,0:T(8,128)(2,1)} %copy-done.8), channel_id=1, source_target_pairs={{0,32},{32,0},{64,96},{96,64},{128,160},{160,128},{192,224},{224,1... | collective-permute-start | bytes 3686408 | tf_op jit(solution)/shard_map/ppermute | solution.py:23
  140.5 2.2 %collective-permute-start.9 = (bf16[480,512]{1,0:T(8,128)(2,1)}, bf16[480,512]{1,0:T(8,128)(2,1)S(1)}, u32[]{:S(2)}, u32[]{:S(2)}) collective-permute-start(bf16[480,512]{1,0:T(8,128)(2,1)} %copy-done.9), channel_id=1, source_target_pairs={{0,32},{32,0},{64,96},{96,64},{128,160},{160,128},{192,224},{224,1... | collective-permute-start | bytes 1474568 | tf_op jit(solution)/shard_map/ppermute | solution.py:23
  145.3 10.7 %attention.1.context_ref = bf16[512,1280]{1,0:T(8,128)(2,1)S(1)} custom-call(s32[16]{0:T(128)S(1)} %stack.67.refs_0_, bf16[1200,512]{1,0:T(8,128)(2,1)} %copy-done.5, bf16[480,512]{1,0:T(8,128)(2,1)} %copy-done.6, bf16[240,512]{1,0:T(8,128)(2,1)} %copy-done.7, bf16[1200,512]{1,0:T(8,128)(2,1)} %collective-permute-done.8.refs_4_, ...), custom_call_target="tpu_custom_call" | custom-call | tf_op jit(solution)/shard_map/attention/pallas_call | solution.py:176
  156.0 5.1 %merge_tokens.1 = bf16[128,5120]{1,0:T(8,128)(2,1)S(1)} custom-call(s32[1]{0:T(128)} %bitcast.6.core_ref, bf16[512,1280]{1,0:T(8,128)(2,1)S(1)} %attention.1.context_ref, bf16[1280,640]{1,0:T(8,128)(2,1)} %bitcast.24.w_own_ref, bf16[1280,640]{1,0:T(8,128)(2,1)S(1)} %collective-permute-done.11.w_other_ref, bf16[512,1280]{1,0:T(8,128)(2,1)S(1)} %copy-done.2, ...), custom_call_target="tpu_custom_call" | custom-call | tf_op jit(solution)/shard_map/merge_tokens/pallas_call | solution.py:233
  162.5 9.8 %all-to-all-start.3 = ((bf16[32,4,5120]{2,1,0:T(4,128)(2,1)}), bf16[32,4,5120]{2,1,0:T(4,128)(2,1)S(1)}, u32[]{:S(2)}, u32[]{:S(2)}) async-start(bf16[32,4,5120]{2,1,0:T(4,128)(2,1)} %reshape.69), calls=%async_computation.3 | async-start | bytes 2621440 | tf_op jit(solution)/shard_map/all_to_all | solution.py:291
  172.5 33.8 %all-to-all-done.3 = bf16[32,4,5120]{2,1,0:T(4,128)(2,1)S(1)} async-done(((bf16[32,4,5120]{2,1,0:T(4,128)(2,1)}), bf16[32,4,5120]{2,1,0:T(4,128)(2,1)S(1)}, u32[]{:S(2)}, u32[]{:S(2)}) %all-to-all-start.3) | async-done | bytes 1310752 | tf_op jit(solution)/shard_map/all_to_all | solution.py:291
  (86 shorter events, 31.2 us)
Async XLA Ops:
  0.0 17.5 %copy-start = (bf16[512,1280]{1,0:T(8,128)(2,1)S(1)}, bf16[512,1280]{1,0:T(8,128)(2,1)}, u32[]{:S(2)}) copy-start(bf16[512,1280]{1,0:T(8,128)(2,1)} %x_ref.3) | copy-start | bytes 3932164
  0.0 19.4 %copy-start.13 = (f32[1280]{0:T(1024)S(1)}, f32[1280]{0:T(1024)}, u32[]{:S(2)}) copy-start(f32[1280]{0:T(1024)} %param.9) | copy-start | bytes 15364
  0.0 19.4 %copy-start.15 = (s32[512]{0:T(512)S(1)}, s32[512]{0:T(512)}, u32[]{:S(2)}) copy-start(s32[512]{0:T(512)} %param.13) | copy-start | bytes 6148
  3.8 43.8 %copy-start.12 = (bf16[40,80]{1,0:T(8,128)(2,1)S(1)}, bf16[40,80]{1,0:T(8,128)(2,1)}, u32[]{:S(2)}) copy-start(bf16[40,80]{1,0:T(8,128)(2,1)} %param.11) | copy-start | bytes 19204
  3.8 33.3 %all-to-all-start = ((bf16[32,40,248]{2,1,0:T(8,128)(2,1)}), bf16[32,40,248]{2,1,0:T(8,128)(2,1)}, u32[]{:S(2)}, u32[]{:S(2)}) async-start(bf16[32,40,248]{2,1,0:T(8,128)(2,1)} %broadcast_in_dim.89), calls=%async_computation | async-start | bytes 1310720 | tf_op jit(solution)/shard_map/all_to_all | solution.py:18
  17.5 36.7 %collective-permute-start.2 = (bf16[512,1280]{1,0:T(8,128)(2,1)S(1)}, bf16[512,1280]{1,0:T(8,128)(2,1)S(1)}, u32[]{:S(2)}, u32[]{:S(2)}) collective-permute-start(bf16[512,1280]{1,0:T(8,128)(2,1)S(1)} %copy-done), channel_id=1, source_target_pairs={{0,32},{32,0},{64,96},{96,64},{128,160},{160,128},{192,224},{224,1... | collective-permute-start | bytes 3932168 | tf_op jit(solution)/shard_map/ppermute | solution.py:23
  38.5 25.5 %collective-permute-start.1 = (bf16[240,1280]{1,0:T(8,128)(2,1)S(1)}, bf16[240,1280]{1,0:T(8,128)(2,1)}, u32[]{:S(2)}, u32[]{:S(2)}) collective-permute-start(bf16[240,1280]{1,0:T(8,128)(2,1)S(1)} %bitcast.34), channel_id=1, source_target_pairs={{0,448},{32,480},{64,0},{96,32},{128,64},{160,96},{192,128},{224,1... | collective-permute-start | bytes 1843208 | tf_op jit(solution)/shard_map/ppermute | solution.py:28
  43.9 20.1 %collective-permute-start = (bf16[240,1280]{1,0:T(8,128)(2,1)S(1)}, bf16[240,1280]{1,0:T(8,128)(2,1)}, u32[]{:S(2)}, u32[]{:S(2)}) collective-permute-start(bf16[240,1280]{1,0:T(8,128)(2,1)S(1)} %bitcast.35), channel_id=1, source_target_pairs={{0,64},{32,96},{64,128},{96,160},{128,192},{160,224},{192,256},{22... | collective-permute-start | bytes 1843208 | tf_op jit(solution)/shard_map/ppermute | solution.py:28
  48.3 15.6 %all-to-all-start.1 = ((bf16[16,40,80]{2,1,0:T(8,128)(2,1)}), bf16[16,40,80]{2,1,0:T(8,128)(2,1)S(1)}, u32[]{:S(2)}, u32[]{:S(2)}) async-start(bf16[16,40,80]{2,1,0:T(8,128)(2,1)} %broadcast_in_dim.91), calls=%async_computation.1 | async-start | bytes 327680 | tf_op jit(solution)/shard_map/all_to_all | solution.py:18
  67.3 68.9 %all-to-all-start.2 = ((bf16[32,40,640]{2,1,0:T(8,128)(2,1)}), bf16[32,40,640]{2,1,0:T(8,128)(2,1)}, u32[]{:S(2)}, u32[]{:S(2)}) async-start(bf16[32,40,640]{2,1,0:T(8,128)(2,1)} %broadcast_in_dim.103), calls=%async_computation.2 | async-start | bytes 3276800 | tf_op jit(solution)/shard_map/all_to_all | solution.py:18
  73.6 19.0 %collective-permute-start.3 = (bf16[240,1280]{1,0:T(8,128)(2,1)}, bf16[240,1280]{1,0:T(8,128)(2,1)S(1)}, u32[]{:S(2)}, u32[]{:S(2)}) collective-permute-start(bf16[240,1280]{1,0:T(8,128)(2,1)} %collective-permute-done.refs_1_), channel_id=1, source_target_pairs={{0,64},{32,96},{64,128},{96,160},{128,192},{160,224},{192,256},{22... | collective-permute-start | bytes 1843208 | tf_op jit(solution)/shard_map/ppermute | solution.py:28
  76.4 17.6 %collective-permute-start.4 = (bf16[240,1280]{1,0:T(8,128)(2,1)}, bf16[240,1280]{1,0:T(8,128)(2,1)S(1)}, u32[]{:S(2)}, u32[]{:S(2)}) collective-permute-start(bf16[240,1280]{1,0:T(8,128)(2,1)} %collective-permute-done.1.refs_2_), channel_id=1, source_target_pairs={{0,448},{32,480},{64,0},{96,32},{128,64},{160,96},{192,128},{224,1... | collective-permute-start | bytes 1843208 | tf_op jit(solution)/shard_map/ppermute | solution.py:28
  94.0 18.4 %collective-permute-start.5 = (bf16[240,1280]{1,0:T(8,128)(2,1)S(1)}, bf16[240,1280]{1,0:T(8,128)(2,1)S(1)}, u32[]{:S(2)}, u32[]{:S(2)}) collective-permute-start(bf16[240,1280]{1,0:T(8,128)(2,1)S(1)} %collective-permute-done.3.refs_3_), channel_id=1, source_target_pairs={{0,64},{32,96},{64,128},{96,160},{128,192},{160,224},{192,256},{22... | collective-permute-start | bytes 1843208 | tf_op jit(solution)/shard_map/ppermute | solution.py:28
  97.1 16.5 %collective-permute-start.6 = (bf16[240,1280]{1,0:T(8,128)(2,1)S(1)}, bf16[240,1280]{1,0:T(8,128)(2,1)S(1)}, u32[]{:S(2)}, u32[]{:S(2)}) collective-permute-start(bf16[240,1280]{1,0:T(8,128)(2,1)S(1)} %collective-permute-done.4.refs_4_), channel_id=1, source_target_pairs={{0,448},{32,480},{64,0},{96,32},{128,64},{160,96},{192,128},{224,1... | collective-permute-start | bytes 1843208 | tf_op jit(solution)/shard_map/ppermute | solution.py:28
  106.0 26.8 %copy-start.8 = (bf16[1200,512]{1,0:T(8,128)(2,1)}, bf16[1200,512]{1,0:T(8,128)(2,1)S(1)}, u32[]{:S(2)}) copy-start(bf16[1200,512]{1,0:T(8,128)(2,1)S(1)} %get-tuple-element.49) | copy-start | bytes 3686404
  113.6 17.7 %collective-permute-start.7 = (bf16[240,1280]{1,0:T(8,128)(2,1)S(1)}, bf16[240,1280]{1,0:T(8,128)(2,1)S(1)}, u32[]{:S(2)}, u32[]{:S(2)}) collective-permute-start(bf16[240,1280]{1,0:T(8,128)(2,1)S(1)} %collective-permute-done.5.refs_0_), channel_id=1, source_target_pairs={{0,64},{32,96},{64,128},{96,160},{128,192},{160,224},{192,256},{22... | collective-permute-start | bytes 1843208 | tf_op jit(solution)/shard_map/ppermute | solution.py:28
  117.0 15.1 %copy-start.6 = (bf16[480,512]{1,0:T(8,128)(2,1)}, bf16[480,512]{1,0:T(8,128)(2,1)S(1)}, u32[]{:S(2)}) copy-start(bf16[480,512]{1,0:T(8,128)(2,1)S(1)} %get-tuple-element.46.refs_2_) | copy-start | bytes 1474564
  117.0 15.1 %copy-start.9 = (bf16[480,512]{1,0:T(8,128)(2,1)}, bf16[480,512]{1,0:T(8,128)(2,1)S(1)}, u32[]{:S(2)}) copy-start(bf16[480,512]{1,0:T(8,128)(2,1)S(1)} %get-tuple-element.50) | copy-start | bytes 1474564
  131.3 11.8 %copy-start.14 = (f32[1280]{0:T(1024)S(1)}, f32[1280]{0:T(1024)}, u32[]{:S(2)}) copy-start(f32[1280]{0:T(1024)} %param.12) | copy-start | bytes 15364
  132.8 3.4 %collective-permute-start.10 = (bf16[240,512]{1,0:T(8,128)(2,1)S(1)}, bf16[240,512]{1,0:T(8,128)(2,1)S(1)}, u32[]{:S(2)}, u32[]{:S(2)}) collective-permute-start(bf16[240,512]{1,0:T(8,128)(2,1)S(1)} %get-tuple-element.51), channel_id=1, source_target_pairs={{0,32},{32,0},{64,96},{96,64},{128,160},{160,128},{192,224},{224,1... | collective-permute-start | bytes 737288 | tf_op jit(solution)/shard_map/ppermute | solution.py:23
  136.2 19.8 %collective-permute-start.11 = (bf16[1280,640]{1,0:T(8,128)(2,1)}, bf16[1280,640]{1,0:T(8,128)(2,1)S(1)}, u32[]{:S(2)}, u32[]{:S(2)}) collective-permute-start(bf16[1280,640]{1,0:T(8,128)(2,1)} %bitcast.24.w_own_ref), channel_id=1, source_target_pairs={{0,32},{32,0},{64,96},{96,64},{128,160},{160,128},{192,224},{224,1... | collective-permute-start | bytes 4915208 | tf_op jit(solution)/shard_map/ppermute | solution.py:23
  138.2 6.3 %collective-permute-start.8 = (bf16[1200,512]{1,0:T(8,128)(2,1)}, bf16[1200,512]{1,0:T(8,128)(2,1)}, u32[]{:S(2)}, u32[]{:S(2)}) collective-permute-start(bf16[1200,512]{1,0:T(8,128)(2,1)} %copy-done.8), channel_id=1, source_target_pairs={{0,32},{32,0},{64,96},{96,64},{128,160},{160,128},{192,224},{224,1... | collective-permute-start | bytes 3686408 | tf_op jit(solution)/shard_map/ppermute | solution.py:23
  140.5 4.0 %collective-permute-start.9 = (bf16[480,512]{1,0:T(8,128)(2,1)}, bf16[480,512]{1,0:T(8,128)(2,1)S(1)}, u32[]{:S(2)}, u32[]{:S(2)}) collective-permute-start(bf16[480,512]{1,0:T(8,128)(2,1)} %copy-done.9), channel_id=1, source_target_pairs={{0,32},{32,0},{64,96},{96,64},{128,160},{160,128},{192,224},{224,1... | collective-permute-start | bytes 1474568 | tf_op jit(solution)/shard_map/ppermute | solution.py:23
  162.5 43.8 %all-to-all-start.3 = ((bf16[32,4,5120]{2,1,0:T(4,128)(2,1)}), bf16[32,4,5120]{2,1,0:T(4,128)(2,1)S(1)}, u32[]{:S(2)}, u32[]{:S(2)}) async-start(bf16[32,4,5120]{2,1,0:T(4,128)(2,1)} %reshape.69), calls=%async_computation.3 | async-start | bytes 2621440 | tf_op jit(solution)/shard_map/all_to_all | solution.py:291
  (8 other events, 35.2 us)

commit v7 on v5

--- a/solution.py
+++ b/solution.py
@@ -23,65 +23,46 @@
     return lax.ppermute(x, "pipe", [(p, p ^ 1) for p in range(size)])
 
 
-def chip_copy(x, chips):
-    size = lax.axis_size("pipe")
-    return lax.ppermute(x, "pipe", [(p, (p + 2 * chips) % size) for p in range(size)])
-
-
-def ring_project(slab, normed, w_out, core, early):
-    rows = slab.shape[0]
-    size = lax.axis_size("pipe")
-    place = lax.axis_index("pipe").astype(jnp.int32)
-    together = lax.optimization_barrier
-
-    def firsts(pieces):
-        owners = [(place + owner, offset) for owner, offset in pieces]
-        owners += [((place ^ 1) + owner, offset) for owner, offset in pieces]
-        return jnp.stack([((owner + size) % size) * rows + offset for owner, offset in owners])
-
-    cut = rows * 2 // 3
-    near = [(0, 0)], [(-2, 0), (2, 0)], [(-4, 0), (4, 0)], [(-6, 0), (6, 0)], [(8, 0), (8, cut)]
-    a1, b1 = chip_copy(slab, 1), chip_copy(slab, -1)
-    blocks = copy_for_each(w_out, "pipe")
-    other = partner_copy(slab)
-    a1, b1, other, normed, blocks = together((a1, b1, other, normed, blocks))
-
-    a2, b2 = chip_copy(a1, 1), chip_copy(b1, -1)
-    pa1, pb1 = partner_copy(a1), partner_copy(b1)
-    half = blocks.shape[0] * blocks.shape[2] // 2
-    out_rows = jnp.moveaxis(blocks, 0, 1).reshape(blocks.shape[1], 2, half)
-    out_rows = lax.dynamic_index_in_dim(out_rows, core[0], axis=1, keepdims=False)
-    out_own = copy_for_each(out_rows, "tensor")
-    buffer = project(normed, [slab, other], firsts(near[0]), None)
-    a2, b2, pa1, pb1, buffer, early = together((a2, b2, pa1, pb1, buffer, early))
-
-    a3, b3 = chip_copy(a2, 1), chip_copy(b2, -1)
-    pa2, pb2 = partner_copy(a2), partner_copy(b2)
-    buffer = project(normed, [a1, b1, pa1, pb1], firsts(near[1]), buffer)
-    a3, b3, pa2, pb2, buffer = together((a3, b3, pa2, pb2, buffer))
-
-    a4, b4 = chip_copy(a3[:cut], 1), chip_copy(b3[cut:], -1)
-    pa3, pb3 = partner_copy(a3), partner_copy(b3)
-    buffer = project(normed, [a2, b2, pa2, pb2], firsts(near[2]), buffer)
-    a4, b4, pa3, pb3, buffer = together((a4, b4, pa3, pb3, buffer))
-
-    pa4, pb4 = partner_copy(a4), partner_copy(b4)
-    buffer = project(normed, [a3, b3, pa3, pb3], firsts(near[3]), buffer)
-    pa4, pb4, buffer, out_own = together((pa4, pb4, buffer, out_own))
-    buffer = project(normed, [a4, b4, pa4, pb4], firsts(near[4]), buffer)
-    return buffer, out_own.reshape(-1, half), early
-
-
-def on_chip(x):
-    return pltpu.with_memory_space_constraint(x, pltpu.VMEM)
-
-
 def in_hbm(x):
     return pltpu.with_memory_space_constraint(x, pltpu.HBM)
 
 
 def in_vmem(count):
     return [pl.BlockSpec(memory_space=pltpu.VMEM)] * count
+
+
+def payload_kernel(patches_ref, sample_ref, w_ref, out_ref, wide_ref):
+    copies, rows, lanes = out_ref.shape
+    columns = w_ref.shape[1]
+    slots = patches_ref.shape[0]
+    last = lanes - 128
+    wide_ref[:, :columns] = w_ref[...].astype(jnp.float32)
+    lane = lax.broadcasted_iota(jnp.int32, (rows, 128), 1) + last
+    tail = jnp.where(lane < columns, wide_ref[:, last:], 0.0)
+    for slot in range(slots):
+        units = (patches_ref[slot] // UNIT).astype(jnp.float32)
+        tail = jnp.where(lane == columns + slot, units, tail)
+        sample = sample_ref[slot].astype(jnp.float32)
+        tail = jnp.where(lane == columns + slots + slot, sample, tail)
+    head = wide_ref[:, :last].astype(jnp.bfloat16)
+    tail = tail.astype(jnp.bfloat16)
+    for copy in range(copies):
+        out_ref[copy, :, :last] = head
+        out_ref[copy, :, last:] = tail
+
+
+def payload_copies(image_patches, image_sample, w, copies):
+    rows, columns = w.shape
+    lanes = -(-(columns + 2 * image_patches.shape[0]) // 128) * 128
+    return pl.pallas_call(
+        payload_kernel,
+        in_specs=[pl.BlockSpec(memory_space=pltpu.SMEM)] * 2 + in_vmem(1),
+        out_specs=pl.BlockSpec(memory_space=pltpu.VMEM),
+        out_shape=jax.ShapeDtypeStruct((copies, rows, lanes), jnp.bfloat16),
+        scratch_shapes=[pltpu.VMEM((rows, lanes), jnp.float32)],
+        compiler_params=pltpu.CompilerParams(vmem_limit_bytes=8 << 20),
+        name="payload_copies",
+    )(image_patches, image_sample, w)
 
 
 def normalize_kernel(x_ref, gain_ref, out_ref):
@@ -101,47 +82,29 @@
     )(x, gain)
 
 
-def project_kernel(first_ref, normed_ref, *refs, pieces, aliased):
-    slab_refs = refs[:pieces]
-    out_ref, part_ref, sems = refs[pieces + aliased :]
-    copies = []
-    at = 0
-    for piece, slab_ref in enumerate(slab_refs):
-        rows = slab_ref.shape[0]
-        part_ref[at : at + rows, :] = jnp.dot(
-            slab_ref[...], normed_ref[...], preferred_element_type=jnp.float32
-        ).astype(jnp.bfloat16)
-        first = pl.multiple_of(first_ref[piece], 80)
-        copies.append(
-            pltpu.make_async_copy(
-                part_ref.at[at : at + rows, :], out_ref.at[pl.ds(first, rows), :], sems.at[piece]
-            )
-        )
-        copies[-1].start()
-        at += rows
-    for copy in copies:
-        copy.wait()
-
-
-def project(normed, slabs, firsts, buffer):
+def project_kernel(w_ref, normed_ref, out_ref):
+    out_ref[...] = jnp.dot(
+        w_ref[...], normed_ref[...], preferred_element_type=jnp.float32
+    ).astype(jnp.bfloat16)
+
+
+def project(w, normed):
     width, count = normed.shape
-    aliased = buffer is not None
-    rows = sum(slab.shape[0] for slab in slabs)
-    return pl.pallas_call(
-        lambda *refs: project_kernel(*refs, pieces=len(slabs), aliased=aliased),
-        in_specs=[pl.BlockSpec(memory_space=pltpu.SMEM)]
-        + in_vmem(1 + len(slabs))
-        + [pl.BlockSpec(memory_space=pltpu.HBM)] * aliased,
-        out_specs=pl.BlockSpec(memory_space=pltpu.HBM),
+    chunk = 3 * width // 4
+    return pl.pallas_call(
+        project_kernel,
+        grid=(4,),
+        in_specs=[
+            pl.BlockSpec((chunk, width), lambda n: (n, 0)),
+            pl.BlockSpec((width, count), lambda n: (0, 0)),
+        ],
+        out_specs=pl.BlockSpec((chunk, count), lambda n: (n, 0)),
         out_shape=pltpu.HBM((3 * width, count), jnp.bfloat16),
-        scratch_shapes=[
-            pltpu.VMEM((rows, count), jnp.bfloat16),
-            pltpu.SemaphoreType.DMA((len(slabs),)),
-        ],
-        input_output_aliases={2 + len(slabs): 0} if aliased else {},
-        compiler_params=pltpu.CompilerParams(vmem_limit_bytes=16 << 20),
+        compiler_params=pltpu.CompilerParams(
+            dimension_semantics=("arbitrary",), vmem_limit_bytes=20 << 20
+        ),
         name="project",
-    )(firsts, normed, *slabs, *([in_hbm(buffer)] if aliased else []))
+    )(in_hbm(w), normed)
 
 
 def attention_kernel(qkv_ref, key_ref, query_ref, out_ref, context_ref, *, head_width):
@@ -231,7 +194,7 @@
         ],
         compiler_params=pltpu.CompilerParams(vmem_limit_bytes=28 << 20),
         name="merge_tokens",
-    )(core, context, on_chip(w_own), on_chip(w_other), x, gain)
+    )(core, context, w_own, in_hbm(w_other), x, gain)
 
 
 def destination_rows(units, samples):
@@ -257,27 +220,35 @@
     group_size = lax.axis_size("tensor")
     core = (lax.axis_index("pipe") % 2).astype(jnp.int32).reshape(1)
 
+    half = width // 2
     slots = image_patches.shape[0]
     row_count, qkv_part = w_qkv.shape
 
-    info = jnp.concatenate([image_patches // UNIT, image_sample]).astype(jnp.bfloat16)
-    info = jnp.broadcast_to(info[None], (row_count, 2 * slots))
-    rows = copy_for_each(jnp.concatenate([w_qkv, info], axis=1), "tensor")
+    together = lax.optimization_barrier
+    payload = payload_copies(image_patches, image_sample, w_qkv, group_size)
+    rows = lax.all_to_all(payload, "tensor", 0, 0, tiled=True)
     slab = rows[:, :, :qkv_part].reshape(width, qkv_part).T
-    info = rows[:, 0, qkv_part:].astype(jnp.int32)
-    dest_rows = destination_rows(info[:, :slots], info[:, slots:])
-
-    slab, w_out = lax.optimization_barrier((slab, w_out))
+    w_all = lax.all_gather(slab, "pipe", axis=0, tiled=True)
+    info = rows[:, 0, qkv_part : qkv_part + 2 * slots].astype(jnp.int32)
+
+    slab, w_out, patches = together((slab, w_out, patches))
     normed = normalize_rows(patches, attn_gain[None, :])
     live = jnp.arange(patch_count, dtype=jnp.int32) < jnp.sum(image_patches)
     key_id = jnp.where(live, window_ids, -1)[:, None]
     query_id = jnp.where(live, window_ids, -2).reshape(patch_count // UNIT, UNIT)
-    qkv, out_own, (key_id, query_id, dest_rows) = ring_project(
-        slab, normed, w_out, core, (key_id, query_id, dest_rows)
-    )
+    blocks = copy_for_each(w_out, "pipe")
+    blocks, normed, key_id, query_id = together((blocks, normed, key_id, query_id))
+    out_rows = jnp.moveaxis(blocks, 0, 1).reshape(row_count, 2, half)
+    out_rows = lax.dynamic_index_in_dim(out_rows, core[0], axis=1, keepdims=False)
+    out_own = copy_for_each(out_rows, "tensor")
+    qkv = project(w_all, normed)
+    qkv, out_own = together((qkv, out_own))
+    out_own = out_own.reshape(width, half)
     out_other = partner_copy(out_own)
     context = attention(qkv, key_id, query_id)
     tokens = merge_tokens(core, context, out_own, out_other, patches, merge_gain[None, :])
+    tokens, info = together((tokens, info))
+    dest_rows = destination_rows(info[:, :slots], info[:, slots:])
     outgoing = tokens.reshape(group_size, token_count // group_size, 4 * width)
     received = lax.all_to_all(outgoing, "tensor", split_axis=0, concat_axis=0, tiled=True)
     placement = (

time: 218 us -> 187 us (0.86)
  starting transfers between devices: 72 us -> 22.4 us
  waiting for transfers between devices: 62.1 us -> 80.5 us
  between operations: 0.78 us -> 13.7 us
  Pallas kernels: 31.7 us -> 24.7 us
  local copies, waits for them, and re-layouts: 11.8 us -> 8.2 us
    all_gather x0 -> x1, waiting for transfers between devices: none -> 39 us  [body(): w_all = lax.all_gather(slab, 'pipe', axis=0, tiled=True)]
    ppermute x8 -> x0, starting transfers between devices: 28.9 us -> none  [chip_copy(): lax.ppermute(x, 'pipe', [(p, (p + 2 * chips) % size) for p in range(size)])]
    ppermute x8 -> x0, waiting for transfers between devices: 19.5 us -> none  [chip_copy(): lax.ppermute(x, 'pipe', [(p, (p + 2 * chips) % size) for p in range(size)])]
    ppermute x10 -> x1, starting transfers between devices: 20.6 us -> 2.14 us  [partner_copy(): return lax.ppermute(x, 'pipe', [(p, p ^ 1) for p in range(size)])]
    pallas_call x5 -> x2, Pallas kernels: 16.9 us -> 9.85 us  [the longest x1 9.22 us: project(): pl.pallas_call(project_kernel, grid=(4,), in_specs=[pl.BlockSpec((chunk,...]
    slice x3 -> x0, local copies, waits for them, and re-layouts: 4.33 us -> none  [the longest x2 3.4 us: ring_project(): a4, b4 = (chip_copy(a3[:cut], 1), chip_copy(b3[cut:], -1))]
  transfers between devices with their start and end apart: 21 -> 5, of which waited for: 8 -> 3; matrix products, arithmetic and copies ran while one was open for 3% -> 3% of each run, Pallas kernels for 12% -> 10%
where the time goes in v7:
time: 187 us
  waiting for transfers between devices  80.5 us (43%)
  blocking collectives  33 us (18%)
  Pallas kernels  24.7 us (13%)
  starting transfers between devices  22.4 us (12%)
  between operations  13.7 us (7%)
  local copies, waits for them, and re-layouts  8.2 us (4%)
  other arithmetic  2.57 us (1%)
    all_gather x1, waiting for transfers between devices, body(): w_all = lax.all_gather(slab, 'pipe', axis=0, tiled=True)  39 us
    all_to_all x1, blocking collectives, body(): rows = lax.all_to_all(payload, 'tensor', 0, 0, tiled=True)  33 us
    all_to_all x1, waiting for transfers between devices, body(): lax.all_to_all(outgoing, 'tensor', split_axis=0, concat_axis=0, tiled=True)  32.9 us
    all_to_all x2, starting transfers between devices, copy_for_each(): lax.all_to_all(jnp.broadcast_to(x[None], (size, *x.shape)), axis, 0, 0, t...  12.2 us
    pallas_call x1, Pallas kernels, project(): pl.pallas_call(project_kernel, grid=(4,), in_specs=[pl.BlockSpec((chunk,...  9.22 us
    pallas_call x1, Pallas kernels, attention(): pl.pallas_call(lambda *refs: attention_kernel(*refs, head_width=width //...  9.04 us
    all_to_all x2, waiting for transfers between devices, copy_for_each(): lax.all_to_all(jnp.broadcast_to(x[None], (size, *x.shape)), axis, 0, 0, t...  8.57 us
    all_to_all x1, starting transfers between devices, body(): lax.all_to_all(outgoing, 'tensor', split_axis=0, concat_axis=0, tiled=True)  8.12 us
  transfers between devices with their start and end apart: 5, of which 3 were waited for; matrix products, arithmetic and copies ran while one was open for 3% of the time, Pallas kernels for 10%

profile of v7, /device:TPU:4, one launch (start us, length us, event | category | flops | bytes accessed | tf_op | source)
XLA Modules:
  0.0 186.6 jit_solution(16487316363706917990)
XLA Ops:
  6.5 0.7 copy-done.2
  7.3 0.7 copy-done.3
  7.9 0.7 copy-done.4
  8.6 0.6 payload_copies.1
  9.3 33.0 %all_to_all.20 = bf16[32,40,256]{2,1,0:T(8,128)(2,1)S(1)} all-to-all(bf16[32,40,256]{2,1,0:T(8,128)(2,1)S(1)} %payload_copies.1), channel_id=1, replica_groups=mesh['pipe'=16,'tensor'=32] {'tensor'}, dimensions={0} | all-to-all | bytes 1310720 | tf_op jit(solution)/shard_map/all_to_all | solution.py:229
  42.3 1.1 copy.25
  43.4 0.7 reduce_sum.36
  44.0 0.7 broadcast_in_dim.77
  44.7 7.2 %all-to-all-start.1 = ((bf16[16,40,80]{2,1,0:T(8,128)(2,1)}), bf16[16,40,80]{2,1,0:T(8,128)(2,1)S(1)}, u32[]{:S(2)}, u32[]{:S(2)}) async-start(bf16[16,40,80]{2,1,0:T(8,128)(2,1)} %broadcast_in_dim.77), calls=%async_computation.1 | async-start | bytes 327680 | tf_op jit(solution)/shard_map/all_to_all | solution.py:18
  52.0 0.6 select_bitcast_fusion
  52.6 0.7 normalize_rows.1.normed_ref
  53.3 8.6 %all-to-all-done.1 = bf16[16,40,80]{2,1,0:T(8,128)(2,1)S(1)} async-done(((bf16[16,40,80]{2,1,0:T(8,128)(2,1)}), bf16[16,40,80]{2,1,0:T(8,128)(2,1)S(1)}, u32[]{:S(2)}, u32[]{:S(2)}) %all-to-all-start.1) | async-done | bytes 102432 | tf_op jit(solution)/shard_map/all_to_all | solution.py:18
  62.3 1.3 broadcast_in_dim.83
  63.6 5.0 %all-to-all-start.2 = ((bf16[32,40,640]{2,1,0:T(8,128)(2,1)}), bf16[32,40,640]{2,1,0:T(8,128)(2,1)S(1)}, u32[]{:S(2)}, u32[]{:S(2)}) async-start(bf16[32,40,640]{2,1,0:T(8,128)(2,1)} %broadcast_in_dim.83), calls=%async_computation.2 | async-start | bytes 3276800 | tf_op jit(solution)/shard_map/all_to_all | solution.py:18
  68.6 39.0 %all-gather.2.cloned.1.call-done.w_ref = bf16[3840,1280]{1,0:T(8,128)(2,1)} async-done(((bf16[240,1280]{1,0:T(8,128)(2,1)}), bf16[3840,1280]{1,0:T(8,128)(2,1)}) %all-gather.2.cloned.1.call-update) | async-done | bytes 9830416 | tf_op jit(solution)/shard_map/all_gather | solution.py:231
  107.6 9.2 %project.1.refs_0_ = bf16[3840,512]{1,0:T(8,128)(2,1)} custom-call(bf16[3840,1280]{1,0:T(8,128)(2,1)} %all-gather.2.cloned.1.call-done.w_ref, bf16[1280,512]{1,0:T(8,128)(2,1)S(1)} %normalize_rows.1.normed_ref), custom_call_target="tpu_custom_call" | custom-call | tf_op jit(solution)/shard_map/project/pallas_call | solution.py:94
  116.8 2.1 %collective-permute-start = (bf16[1280,640]{1,0:T(8,128)(2,1)S(1)}, bf16[1280,640]{1,0:T(8,128)(2,1)}, u32[]{:S(2)}, u32[]{:S(2)}) collective-permute-start(bf16[1280,640]{1,0:T(8,128)(2,1)S(1)} %bitcast.17), channel_id=1, source_target_pairs={{0,32},{32,0},{64,96},{96,64},{128,160},{160,128},{192,224},{224,1... | collective-permute-start | bytes 4915208 | tf_op jit(solution)/shard_map/ppermute | solution.py:23
  119.0 0.9 slice_convert_fusion
  120.1 9.0 %attention.1.context_ref = bf16[512,1280]{1,0:T(8,128)(2,1)S(1)} custom-call(bf16[3840,512]{1,0:T(8,128)(2,1)} %project.1.refs_0_, s32[512,1]{1,0:T(8,128)S(1)} %copy.27.refs_1_, s32[4,128]{1,0:T(4,128)S(1)} %get-tuple-element.21.refs_2_), custom_call_target="tpu_custom_call" | custom-call | tf_op jit(solution)/shard_map/attention/pallas_call | solution.py:136
  129.1 5.1 %merge_tokens.1 = bf16[128,5120]{1,0:T(8,128)(2,1)S(1)} custom-call(s32[1]{0:T(128)} %bitcast.core_ref, bf16[512,1280]{1,0:T(8,128)(2,1)S(1)} %attention.1.context_ref, bf16[1280,640]{1,0:T(8,128)(2,1)S(1)} %bitcast.18, bf16[1280,640]{1,0:T(8,128)(2,1)} %collective-permute-done.w_other_ref, bf16[512,1280]{1,0:T(8,128)(2,1)S(1)} %copy-done.1, ...), custom_call_target="tpu_custom_call" | custom-call | tf_op jit(solution)/shard_map/merge_tokens/pallas_call | solution.py:186
  134.2 1.3 reshape.63
  135.6 8.1 %all-to-all-start.3 = ((bf16[32,4,5120]{2,1,0:T(4,128)(2,1)}), bf16[32,4,5120]{2,1,0:T(4,128)(2,1)S(1)}, u32[]{:S(2)}, u32[]{:S(2)}) async-start(bf16[32,4,5120]{2,1,0:T(4,128)(2,1)} %reshape.63), calls=%async_computation.3 | async-start | bytes 2621440 | tf_op jit(solution)/shard_map/all_to_all | solution.py:253
  144.9 32.9 %all-to-all-done.3 = bf16[32,4,5120]{2,1,0:T(4,128)(2,1)S(1)} async-done(((bf16[32,4,5120]{2,1,0:T(4,128)(2,1)}), bf16[32,4,5120]{2,1,0:T(4,128)(2,1)S(1)}, u32[]{:S(2)}, u32[]{:S(2)}) %all-to-all-start.3) | async-done | bytes 1310752 | tf_op jit(solution)/shard_map/all_to_all | solution.py:253
  178.1 1.6 fusion
  (48 shorter events, 2.1 us)
Async XLA Ops:
  6.5 101.0 %all-gather.2.cloned.1.call-start = ((), (), s32[]{:S(2)}) async-start(), calls=%async_computation.4 | async-start | bytes 10444800 | tf_op jit(solution)/shard_map/all_gather | solution.py:231
  6.5 0.7 copy-start.2
  7.3 0.7 copy-start.3
  7.9 0.7 copy-start.4
  9.2 34.2 %copy-start.5 = (s32[4]{0:T(128)S(1)}, s32[4]{0:T(128)}, u32[]{:S(2)}) copy-start(s32[4]{0:T(128)} %patches_ref.1) | copy-start | bytes 52
  9.2 34.8 %copy-start.8 = (f32[1280]{0:T(1024)S(1)}, f32[1280]{0:T(1024)}, u32[]{:S(2)}) copy-start(f32[1280]{0:T(1024)} %param.9) | copy-start | bytes 15364
  9.2 34.8 %copy-start.7 = (bf16[40,80]{1,0:T(8,128)(2,1)S(1)}, bf16[40,80]{1,0:T(8,128)(2,1)}, u32[]{:S(2)}) copy-start(bf16[40,80]{1,0:T(8,128)(2,1)} %param.11) | copy-start | bytes 19204
  42.3 1.1 copy-start.6
  42.3 9.7 %copy-start.10 = (s32[512]{0:T(512)S(1)}, s32[512]{0:T(512)}, u32[]{:S(2)}) copy-start(s32[512]{0:T(512)} %param.13) | copy-start | bytes 6148
  42.3 10.3 %copy-start = (bf16[512,1280]{1,0:T(8,128)(2,1)S(1)}, bf16[512,1280]{1,0:T(8,128)(2,1)}, u32[]{:S(2)}) copy-start(bf16[512,1280]{1,0:T(8,128)(2,1)} %x_ref.1) | copy-start | bytes 3932164
  44.7 17.1 %all-to-all-start.1 = ((bf16[16,40,80]{2,1,0:T(8,128)(2,1)}), bf16[16,40,80]{2,1,0:T(8,128)(2,1)S(1)}, u32[]{:S(2)}, u32[]{:S(2)}) async-start(bf16[16,40,80]{2,1,0:T(8,128)(2,1)} %broadcast_in_dim.77), calls=%async_computation.1 | async-start | bytes 327680 | tf_op jit(solution)/shard_map/all_to_all | solution.py:18
  63.6 53.2 %all-to-all-start.2 = ((bf16[32,40,640]{2,1,0:T(8,128)(2,1)}), bf16[32,40,640]{2,1,0:T(8,128)(2,1)S(1)}, u32[]{:S(2)}, u32[]{:S(2)}) async-start(bf16[32,40,640]{2,1,0:T(8,128)(2,1)} %broadcast_in_dim.83), calls=%async_computation.2 | async-start | bytes 3276800 | tf_op jit(solution)/shard_map/all_to_all | solution.py:18
  68.6 50.4 %copy-start.9 = (f32[1280]{0:T(1024)S(1)}, f32[1280]{0:T(1024)}, u32[]{:S(2)}) copy-start(f32[1280]{0:T(1024)} %param.12) | copy-start | bytes 15364
  116.8 12.3 %collective-permute-start = (bf16[1280,640]{1,0:T(8,128)(2,1)S(1)}, bf16[1280,640]{1,0:T(8,128)(2,1)}, u32[]{:S(2)}, u32[]{:S(2)}) collective-permute-start(bf16[1280,640]{1,0:T(8,128)(2,1)S(1)} %bitcast.17), channel_id=1, source_target_pairs={{0,32},{32,0},{64,96},{96,64},{128,160},{160,128},{192,224},{224,1... | collective-permute-start | bytes 4915208 | tf_op jit(solution)/shard_map/ppermute | solution.py:23
  120.1 9.1 %copy-start.1 = (bf16[512,1280]{1,0:T(8,128)(2,1)S(1)}, bf16[512,1280]{1,0:T(8,128)(2,1)}, u32[]{:S(2)}) copy-start(bf16[512,1280]{1,0:T(8,128)(2,1)} %x_ref.1) | copy-start | bytes 3932164
  135.6 42.2 %all-to-all-start.3 = ((bf16[32,4,5120]{2,1,0:T(4,128)(2,1)}), bf16[32,4,5120]{2,1,0:T(4,128)(2,1)S(1)}, u32[]{:S(2)}, u32[]{:S(2)}) async-start(bf16[32,4,5120]{2,1,0:T(4,128)(2,1)} %reshape.63), calls=%async_computation.3 | async-start | bytes 2621440 | tf_op jit(solution)/shard_map/all_to_all | solution.py:253
Sparse Core Ops, SparseCore 0:
  43.5 64.0 all-gather.1

commit v8 on v7

--- a/solution.py
+++ b/solution.py
@@ -62,7 +62,7 @@
         scratch_shapes=[pltpu.VMEM((rows, lanes), jnp.float32)],
         compiler_params=pltpu.CompilerParams(vmem_limit_bytes=8 << 20),
         name="payload_copies",
-    )(image_patches, image_sample, w)
+    )(in_hbm(image_patches), in_hbm(image_sample), in_hbm(w))
 
 
 def normalize_kernel(x_ref, gain_ref, out_ref):
@@ -82,73 +82,79 @@
     )(x, gain)
 
 
-def project_kernel(w_ref, normed_ref, out_ref):
-    out_ref[...] = jnp.dot(
-        w_ref[...], normed_ref[...], preferred_element_type=jnp.float32
-    ).astype(jnp.bfloat16)
-
-
-def project(w, normed):
+def attention_kernel(
+    normed_ref, w_ref, key_ref, query_ref, out_ref, qkv_ref, context_ref, *, head_width
+):
+    step = pl.program_id(0)
+    chunk, width = w_ref.shape
+    chunks = 3 * width // chunk
+
+    @pl.when(step < chunks)
+    def _():
+        qkv_ref[pl.ds(pl.multiple_of(step * chunk, chunk), chunk), :] = jnp.dot(
+            w_ref[...], normed_ref[...], preferred_element_type=jnp.float32
+        ).astype(jnp.bfloat16)
+
+    @pl.when(step >= chunks)
+    def _():
+        unit = step - chunks
+        patches = pl.ds(pl.multiple_of(unit * UNIT, UNIT), UNIT)
+        query_id = query_ref[pl.ds(unit, 1), :]
+        key_id = jnp.broadcast_to(key_ref[pl.ds(unit, 1), :], (UNIT, UNIT)).T
+        allowed = key_id == query_id
+        heads = range(width // head_width)
+
+        def rows(part, head):
+            first = part * width + head * head_width
+            return qkv_ref[first : first + head_width, patches]
+
+        scores = [
+            lax.dot_general(
+                rows(1, head), rows(0, head), (((0,), (0,)), ((), ())), preferred_element_type=jnp.float32
+            )
+            for head in heads
+        ]
+        scores = [jnp.where(allowed, score, -1e30) for score in scores]
+        highest = [jnp.max(score, axis=0, keepdims=True) for score in scores]
+        factor = 1.0 / (math.sqrt(head_width) * math.log(2.0))
+        weights = [jnp.exp2((score - top) * factor) for score, top in zip(scores, highest)]
+        totals = [jnp.sum(weight, axis=0, keepdims=True) for weight in weights]
+        weights = [
+            (weight * jnp.where(query_id >= 0, 1.0 / total, 0.0)).astype(jnp.bfloat16)
+            for weight, total in zip(weights, totals)
+        ]
+        for head, weight in zip(heads, weights):
+            context_ref[head * head_width : (head + 1) * head_width, :] = jnp.dot(
+                rows(2, head), weight, preferred_element_type=jnp.float32
+            ).astype(jnp.bfloat16)
+        out_ref[...] = context_ref[...].T
+
+
+def attention(w, normed, key_id, query_id):
     width, count = normed.shape
     chunk = 3 * width // 4
-    return pl.pallas_call(
-        project_kernel,
-        grid=(4,),
+    units = count // UNIT
+    whole = lambda *shape: pl.BlockSpec(shape, lambda n: (0,) * len(shape))
+    return pl.pallas_call(
+        lambda *refs: attention_kernel(*refs, head_width=width // HEADS),
+        grid=(4 + units,),
         in_specs=[
-            pl.BlockSpec((chunk, width), lambda n: (n, 0)),
-            pl.BlockSpec((width, count), lambda n: (0, 0)),
+            whole(width, count),
+            pl.BlockSpec((chunk, width), lambda n: (jnp.minimum(n, 3), 0)),
+            whole(units, UNIT),
+            whole(units, UNIT),
         ],
-        out_specs=pl.BlockSpec((chunk, count), lambda n: (n, 0)),
-        out_shape=pltpu.HBM((3 * width, count), jnp.bfloat16),
+        out_specs=pl.BlockSpec((UNIT, width), lambda n: (jnp.maximum(n - 4, 0), 0)),
+        out_shape=jax.ShapeDtypeStruct((count, width), jnp.bfloat16),
+        scratch_shapes=[
+            pltpu.VMEM((3 * width, count), jnp.bfloat16),
+            pltpu.VMEM((width, UNIT), jnp.bfloat16),
+        ],
         compiler_params=pltpu.CompilerParams(
-            dimension_semantics=("arbitrary",), vmem_limit_bytes=20 << 20
-        ),
-        name="project",
-    )(in_hbm(w), normed)
-
-
-def attention_kernel(qkv_ref, key_ref, query_ref, out_ref, context_ref, *, head_width):
-    width = out_ref.shape[1]
-    query_id = query_ref[pl.ds(pl.program_id(0), 1), :]
-    allowed = key_ref[...] == query_id
-    for head in range(width // head_width):
-        query, key, value = (
-            qkv_ref[part * width + head * head_width : part * width + (head + 1) * head_width, :]
-            for part in range(3)
-        )
-        scores = lax.dot_general(
-            key, query, (((0,), (0,)), ((), ())), preferred_element_type=jnp.float32
-        )
-        scores = jnp.where(allowed, scores, -1e30)
-        highest = jnp.max(scores, axis=0, keepdims=True)
-        weights = jnp.exp2((scores - highest) * (1.0 / (math.sqrt(head_width) * math.log(2.0))))
-        total = jnp.sum(weights, axis=0, keepdims=True)
-        weights = weights * jnp.where(query_id >= 0, 1.0 / total, 0.0)
-        context_ref[head * head_width : (head + 1) * head_width, :] = jnp.dot(
-            value, weights.astype(jnp.bfloat16), preferred_element_type=jnp.float32
-        ).astype(jnp.bfloat16)
-    out_ref[...] = context_ref[...].T
-
-
-def attention(qkv, key_id, query_id):
-    width, count = qkv.shape[0] // 3, qkv.shape[1]
-    units = count // UNIT
-    return pl.pallas_call(
-        lambda *refs: attention_kernel(*refs, head_width=width // HEADS),
-        grid=(units,),
-        in_specs=[
-            pl.BlockSpec((3 * width, UNIT), lambda n: (0, n)),
-            pl.BlockSpec((UNIT, 1), lambda n: (n, 0)),
-            pl.BlockSpec((units, UNIT), lambda n: (0, 0)),
-        ],
-        out_specs=pl.BlockSpec((UNIT, width), lambda n: (n, 0)),
-        out_shape=jax.ShapeDtypeStruct((count, width), jnp.bfloat16),
-        scratch_shapes=[pltpu.VMEM((width, UNIT), jnp.bfloat16)],
-        compiler_params=pltpu.CompilerParams(
-            dimension_semantics=("arbitrary",), vmem_limit_bytes=16 << 20
+            dimension_semantics=("arbitrary",), vmem_limit_bytes=32 << 20
         ),
         name="attention",
-    )(in_hbm(qkv), key_id, query_id)
+    )(normed, in_hbm(w), key_id, query_id)
 
 
 def merge_kernel(
@@ -169,15 +175,16 @@
     scale = lax.rsqrt(square * (1.0 / width) + epsilon)
     merged_ref[:, :half] = (low * scale * gain_ref[:, :half]).astype(jnp.bfloat16)
     merged_ref[:, half:] = (high * scale * gain_ref[:, half:]).astype(jnp.bfloat16)
-    tokens = out_ref.shape[0]
+    tokens = out_ref.shape[0] * out_ref.shape[1]
     units = count // UNIT
     to_row = lax.broadcasted_iota(jnp.int32, (tokens, count), 0)
     from_row = lax.broadcasted_iota(jnp.int32, (tokens, count), 1)
     first_row = (to_row % units) * UNIT + (to_row // units) * 4
     for member in range(4):
         choice = (from_row == first_row + member).astype(jnp.bfloat16)
-        out_ref[:, member * width : (member + 1) * width] = jnp.dot(
-            choice, merged_ref[...], preferred_element_type=jnp.float32
+        part = jnp.dot(choice, merged_ref[...], preferred_element_type=jnp.float32)
+        out_ref[:, :, member * width : (member + 1) * width] = part.reshape(
+            -1, units, width
         ).astype(jnp.bfloat16)
 
 
@@ -187,7 +194,7 @@
         merge_kernel,
         in_specs=[pl.BlockSpec(memory_space=pltpu.SMEM)] + in_vmem(5),
         out_specs=pl.BlockSpec(memory_space=pltpu.VMEM),
-        out_shape=jax.ShapeDtypeStruct((count // 4, 4 * width), jnp.bfloat16),
+        out_shape=jax.ShapeDtypeStruct((UNIT // 4, count // UNIT, 4 * width), jnp.bfloat16),
         scratch_shapes=[
             pltpu.VMEM((2, count, width // 2), jnp.float32),
             pltpu.VMEM((count, width), jnp.bfloat16),
@@ -229,28 +236,27 @@
     rows = lax.all_to_all(payload, "tensor", 0, 0, tiled=True)
     slab = rows[:, :, :qkv_part].reshape(width, qkv_part).T
     w_all = lax.all_gather(slab, "pipe", axis=0, tiled=True)
-    info = rows[:, 0, qkv_part : qkv_part + 2 * slots].astype(jnp.int32)
 
     slab, w_out, patches = together((slab, w_out, patches))
+    blocks = copy_for_each(w_out, "pipe")
     normed = normalize_rows(patches, attn_gain[None, :])
     live = jnp.arange(patch_count, dtype=jnp.int32) < jnp.sum(image_patches)
-    key_id = jnp.where(live, window_ids, -1)[:, None]
+    key_id = jnp.where(live, window_ids, -1).reshape(patch_count // UNIT, UNIT)
     query_id = jnp.where(live, window_ids, -2).reshape(patch_count // UNIT, UNIT)
-    blocks = copy_for_each(w_out, "pipe")
-    blocks, normed, key_id, query_id = together((blocks, normed, key_id, query_id))
+    info = rows[:, 0, qkv_part : qkv_part + 2 * slots].astype(jnp.int32)
+    merge_row = merge_gain[None, :]
+    blocks, normed, key_id, query_id, info, merge_row = together(
+        (blocks, normed, key_id, query_id, info, merge_row)
+    )
     out_rows = jnp.moveaxis(blocks, 0, 1).reshape(row_count, 2, half)
     out_rows = lax.dynamic_index_in_dim(out_rows, core[0], axis=1, keepdims=False)
-    out_own = copy_for_each(out_rows, "tensor")
-    qkv = project(w_all, normed)
-    qkv, out_own = together((qkv, out_own))
-    out_own = out_own.reshape(width, half)
+    out_own = copy_for_each(out_rows, "tensor").reshape(width, half)
     out_other = partner_copy(out_own)
-    context = attention(qkv, key_id, query_id)
-    tokens = merge_tokens(core, context, out_own, out_other, patches, merge_gain[None, :])
+    context = attention(w_all, normed, key_id, query_id)
+    tokens = merge_tokens(core, context, out_own, out_other, patches, merge_row)
     tokens, info = together((tokens, info))
     dest_rows = destination_rows(info[:, :slots], info[:, slots:])
-    outgoing = tokens.reshape(group_size, token_count // group_size, 4 * width)
-    received = lax.all_to_all(outgoing, "tensor", split_axis=0, concat_axis=0, tiled=True)
+    received = lax.all_to_all(tokens, "tensor", split_axis=0, concat_axis=0, tiled=True)
     placement = (
         jnp.arange(token_count, dtype=jnp.int32)[:, None] == dest_rows.reshape(1, token_count)
     ).astype(jnp.bfloat16)

time: 187 us -> 179 us (0.957)
  the two profiles are of different devices: /device:TPU:4 before, /device:TPU:2 now
where the time goes in v8:
time: 179 us; the launch traced here: 178 us
  blocking collectives  79.5 us (44%)
  waiting for transfers between devices  42 us (23%)
  Pallas kernels  17.9 us (10%)
  starting transfers between devices  15 us (8%)
  between operations  13.7 us (8%)
  local copies, waits for them, and re-layouts  6.88 us (4%)
    all_to_all x1, blocking collectives, copy_for_each(): lax.all_to_all(jnp.broadcast_to(x[None], (size, *x.shape)), axis, 0, 0, t...  46.5 us
    all_to_all x1, waiting for transfers between devices, body(): lax.all_to_all(tokens, 'tensor', split_axis=0, concat_axis=0, tiled=True)  33.1 us
    all_to_all x1, blocking collectives, body(): rows = lax.all_to_all(payload, 'tensor', 0, 0, tiled=True)  33 us
    pallas_call x1, Pallas kernels, attention(): pl.pallas_call(lambda *refs: attention_kernel(*refs, head_width=width //...  11.2 us
    all_to_all x1, waiting for transfers between devices, copy_for_each(): lax.all_to_all(jnp.broadcast_to(x[None], (size, *x.shape)), axis, 0, 0, t...  8.78 us
    all_to_all x1, starting transfers between devices, copy_for_each(): lax.all_to_all(jnp.broadcast_to(x[None], (size, *x.shape)), axis, 0, 0, t...  7.21 us
    all_to_all x1, starting transfers between devices, body(): lax.all_to_all(tokens, 'tensor', split_axis=0, concat_axis=0, tiled=True)  5.78 us
    pallas_call x1, Pallas kernels, merge_tokens(): pl.pallas_call(merge_kernel, in_specs=[pl.BlockSpec(memory_space=pltpu.SM...  5.15 us
  transfers between devices with their start and end apart: 4, of which 2 were waited for; matrix products, arithmetic and copies ran while one was open for 2% of the time, Pallas kernels for 7%

profile of v8, /device:TPU:2, one launch (start us, length us, event | category | flops | bytes accessed | tf_op | source)
XLA Modules:
  0.0 178.1 jit_solution(6964457669955256572)
XLA Ops:
  6.5 0.8 payload_copies.1
  7.4 33.0 %all_to_all.20 = bf16[32,40,256]{2,1,0:T(8,128)(2,1)S(1)} all-to-all(bf16[32,40,256]{2,1,0:T(8,128)(2,1)S(1)} %payload_copies.1), channel_id=1, replica_groups=mesh['pipe'=16,'tensor'=32] {'tensor'}, dimensions={0} | all-to-all | bytes 1310720 | tf_op jit(solution)/shard_map/all_to_all | solution.py:236
  40.5 1.0 copy.21
  41.5 0.6 reduce_sum.36
  42.2 0.7 select_bitcast_fusion
  42.9 0.7 broadcast_in_dim.74
  43.6 7.2 %all-to-all-start.1 = ((bf16[16,40,80]{2,1,0:T(8,128)(2,1)}), bf16[16,40,80]{2,1,0:T(8,128)(2,1)S(1)}, u32[]{:S(2)}, u32[]{:S(2)}) async-start(bf16[16,40,80]{2,1,0:T(8,128)(2,1)} %broadcast_in_dim.74), calls=%async_computation.1 | async-start | bytes 327680 | tf_op jit(solution)/shard_map/all_to_all | solution.py:18
  50.8 0.7 normalize_rows.1.refs_0_
  51.5 1.0 copy-done.2
  52.6 8.8 %all-to-all-done.1 = bf16[16,40,80]{2,1,0:T(8,128)(2,1)S(1)} async-done(((bf16[16,40,80]{2,1,0:T(8,128)(2,1)}), bf16[16,40,80]{2,1,0:T(8,128)(2,1)S(1)}, u32[]{:S(2)}, u32[]{:S(2)}) %all-to-all-start.1) | async-done | bytes 102432 | tf_op jit(solution)/shard_map/all_to_all | solution.py:18
  61.4 0.3 reshape.61
  61.7 0.1 constant_dynamic-slice_fusion
  61.9 0.1 broadcast_in_dim.80
  62.0 46.5 %all_to_all.21 = bf16[32,40,640]{2,1,0:T(8,128)(2,1)S(1)} all-to-all(bf16[32,40,640]{2,1,0:T(8,128)(2,1)S(1)} %broadcast_in_dim.80), channel_id=1, replica_groups=mesh['pipe'=16,'tensor'=32] {'tensor'}, dimensions={0} | all-to-all | bytes 3276800 | tf_op jit(solution)/shard_map/all_to_all | solution.py:18
  108.4 2.0 %collective-permute-start = (bf16[1280,640]{1,0:T(8,128)(2,1)S(1)}, bf16[1280,640]{1,0:T(8,128)(2,1)}, u32[]{:S(2)}, u32[]{:S(2)}) collective-permute-start(bf16[1280,640]{1,0:T(8,128)(2,1)S(1)} %bitcast.18), channel_id=1, source_target_pairs={{0,32},{32,0},{64,96},{96,64},{128,160},{160,128},{192,224},{224,1... | collective-permute-start | bytes 4915208 | tf_op jit(solution)/shard_map/ppermute | solution.py:23
  110.5 1.3 copy-done.3
  111.8 11.2 %attention.1.context_ref = bf16[512,1280]{1,0:T(8,128)(2,1)S(1)} custom-call(bf16[1280,512]{1,0:T(8,128)(2,1)S(1)} %copy-done.3, bf16[3840,1280]{1,0:T(8,128)(2,1)} %all-gather.2.cloned.1.call-done.refs_1_, s32[4,128]{1,0:T(4,128)S(1)} %get-tuple-element.18.refs_2_, s32[4,128]{1,0:T(4,128)S(1)} %get-tuple-element.19.refs_3_), custom_call_target="tpu_custom_call" | custom-call | tf_op jit(solution)/shard_map/attention/pallas_call | solution.py:138
  123.1 5.1 %merge_tokens.1 = bf16[32,4,5120]{2,1,0:T(4,128)(2,1)S(1)} custom-call(s32[1]{0:T(128)} %bitcast.core_ref, bf16[512,1280]{1,0:T(8,128)(2,1)S(1)} %attention.1.context_ref, bf16[1280,640]{1,0:T(8,128)(2,1)S(1)} %bitcast.19, bf16[1280,640]{1,0:T(8,128)(2,1)} %collective-permute-done.w_other_ref, bf16[512,1280]{1,0:T(8,128)(2,1)S(1)} %copy-done, ...), custom_call_target="tpu_custom_call" | custom-call | tf_op jit(solution)/shard_map/merge_tokens/pallas_call | solution.py:193
  128.2 1.0 copy-done.1
  129.3 5.8 %all-to-all-start.3 = ((bf16[32,4,5120]{2,1,0:T(4,128)(2,1)}), bf16[32,4,5120]{2,1,0:T(4,128)(2,1)S(1)}, u32[]{:S(2)}, u32[]{:S(2)}) async-start(bf16[32,4,5120]{2,1,0:T(4,128)(2,1)} %copy-done.1), calls=%async_computation.3 | async-start | bytes 2621440 | tf_op jit(solution)/shard_map/all_to_all | solution.py:259
  135.6 0.1 select_reduce_fusion
  136.3 33.1 %all-to-all-done.3 = bf16[32,4,5120]{2,1,0:T(4,128)(2,1)S(1)} async-done(((bf16[32,4,5120]{2,1,0:T(4,128)(2,1)}), bf16[32,4,5120]{2,1,0:T(4,128)(2,1)S(1)}, u32[]{:S(2)}, u32[]{:S(2)}) %all-to-all-start.3) | async-done | bytes 1310752 | tf_op jit(solution)/shard_map/all_to_all | solution.py:259
  169.4 0.3 reshape.64
  169.7 1.6 fusion
  (40 shorter events, 1.3 us)
Async XLA Ops:
  6.5 104.0 %all-gather.2.cloned.1.call-start = ((), (), s32[]{:S(2)}) async-start(), calls=%async_computation.4 | async-start | bytes 10444800 | tf_op jit(solution)/shard_map/all_gather | solution.py:238
  7.4 34.2 %copy-start.8 = (s32[4]{0:T(128)S(1)}, s32[4]{0:T(128)}, u32[]{:S(2)}) copy-start(s32[4]{0:T(128)} %patches_ref.1) | copy-start | bytes 52
  7.4 34.8 %copy-start.5 = (f32[1280]{0:T(1024)S(1)}, f32[1280]{0:T(1024)}, u32[]{:S(2)}) copy-start(f32[1280]{0:T(1024)} %param.9) | copy-start | bytes 15364
  7.4 34.8 %copy-start.6 = (f32[1280]{0:T(1024)S(1)}, f32[1280]{0:T(1024)}, u32[]{:S(2)}) copy-start(f32[1280]{0:T(1024)} %param.12) | copy-start | bytes 15364
  7.4 34.8 %copy-start.7 = (s32[512]{0:T(512)S(1)}, s32[512]{0:T(512)}, u32[]{:S(2)}) copy-start(s32[512]{0:T(512)} %param.13) | copy-start | bytes 6148
  7.4 35.5 %copy-start.4 = (bf16[40,80]{1,0:T(8,128)(2,1)S(1)}, bf16[40,80]{1,0:T(8,128)(2,1)}, u32[]{:S(2)}) copy-start(bf16[40,80]{1,0:T(8,128)(2,1)} %param.11) | copy-start | bytes 19204
  40.5 10.3 %copy-start = (bf16[512,1280]{1,0:T(8,128)(2,1)S(1)}, bf16[512,1280]{1,0:T(8,128)(2,1)}, u32[]{:S(2)}) copy-start(bf16[512,1280]{1,0:T(8,128)(2,1)} %x_ref.1) | copy-start | bytes 3932164
  43.6 17.8 %all-to-all-start.1 = ((bf16[16,40,80]{2,1,0:T(8,128)(2,1)}), bf16[16,40,80]{2,1,0:T(8,128)(2,1)S(1)}, u32[]{:S(2)}, u32[]{:S(2)}) async-start(bf16[16,40,80]{2,1,0:T(8,128)(2,1)} %broadcast_in_dim.74), calls=%async_computation.1 | async-start | bytes 327680 | tf_op jit(solution)/shard_map/all_to_all | solution.py:18
  51.5 1.1 copy-start.2
  108.4 14.6 %collective-permute-start = (bf16[1280,640]{1,0:T(8,128)(2,1)S(1)}, bf16[1280,640]{1,0:T(8,128)(2,1)}, u32[]{:S(2)}, u32[]{:S(2)}) collective-permute-start(bf16[1280,640]{1,0:T(8,128)(2,1)S(1)} %bitcast.18), channel_id=1, source_target_pairs={{0,32},{32,0},{64,96},{96,64},{128,160},{160,128},{192,224},{224,1... | collective-permute-start | bytes 4915208 | tf_op jit(solution)/shard_map/ppermute | solution.py:23
  110.5 1.3 copy-start.3
  128.2 1.1 copy-start.1
  129.3 40.1 %all-to-all-start.3 = ((bf16[32,4,5120]{2,1,0:T(4,128)(2,1)}), bf16[32,4,5120]{2,1,0:T(4,128)(2,1)S(1)}, u32[]{:S(2)}, u32[]{:S(2)}) async-start(bf16[32,4,5120]{2,1,0:T(4,128)(2,1)} %copy-done.1), calls=%async_computation.3 | async-start | bytes 2621440 | tf_op jit(solution)/shard_map/all_to_all | solution.py:259
Sparse Core Ops, SparseCore 0:
  41.7 64.7 all-gather.1

commit v9 on v8

--- a/solution.py
+++ b/solution.py
@@ -154,19 +154,24 @@
             dimension_semantics=("arbitrary",), vmem_limit_bytes=32 << 20
         ),
         name="attention",
-    )(normed, in_hbm(w), key_id, query_id)
+    )(in_hbm(normed), in_hbm(w), key_id, query_id)
 
 
 def merge_kernel(
-    core_ref, context_ref, w_own_ref, w_other_ref, x_ref, gain_ref, out_ref, hidden_ref, merged_ref
+    core_ref, context_ref, w_own_ref, w_other_ref, x_ref, gain_ref, out_ref, hidden_ref, merged_ref, held_ref, sem
 ):
     core = core_ref[0]
     count, width = context_ref.shape
     half = width // 2
-    for w_ref, place in ((w_own_ref, core), (w_other_ref, 1 - core)):
-        hidden_ref[place] = jnp.dot(
-            context_ref[...], w_ref[...], preferred_element_type=jnp.float32
-        )
+    load = pltpu.make_async_copy(w_other_ref, held_ref, sem)
+    load.start()
+    hidden_ref[core] = jnp.dot(
+        context_ref[...], w_own_ref[...], preferred_element_type=jnp.float32
+    )
+    load.wait()
+    hidden_ref[1 - core] = jnp.dot(
+        context_ref[...], held_ref[...], preferred_element_type=jnp.float32
+    )
     low = x_ref[:, :half].astype(jnp.float32) + hidden_ref[0]
     high = x_ref[:, half:].astype(jnp.float32) + hidden_ref[1]
     square = jnp.sum(low * low, axis=-1, keepdims=True) + jnp.sum(
@@ -192,12 +197,17 @@
     count, width = x.shape
     return pl.pallas_call(
         merge_kernel,
-        in_specs=[pl.BlockSpec(memory_space=pltpu.SMEM)] + in_vmem(5),
+        in_specs=[pl.BlockSpec(memory_space=pltpu.SMEM)]
+        + in_vmem(2)
+        + [pl.BlockSpec(memory_space=pltpu.HBM)]
+        + in_vmem(2),
         out_specs=pl.BlockSpec(memory_space=pltpu.VMEM),
-        out_shape=jax.ShapeDtypeStruct((UNIT // 4, count // UNIT, 4 * width), jnp.bfloat16),
+        out_shape=pltpu.HBM((UNIT // 4, count // UNIT, 4 * width), jnp.bfloat16),
         scratch_shapes=[
             pltpu.VMEM((2, count, width // 2), jnp.float32),
             pltpu.VMEM((count, width), jnp.bfloat16),
+            pltpu.VMEM(w_other.shape, jnp.bfloat16),
+            pltpu.SemaphoreType.DMA,
         ],
         compiler_params=pltpu.CompilerParams(vmem_limit_bytes=28 << 20),
         name="merge_tokens",

time: 179 us -> 177 us (0.989)
  the two profiles are of different devices: /device:TPU:2 before, /device:TPU:4 now
where the time goes in v9:
time: 177 us
  blocking collectives  79.8 us (45%)
  waiting for transfers between devices  41.9 us (24%)
  Pallas kernels  18.8 us (11%)
  starting transfers between devices  14.6 us (8%)
  between operations  13.7 us (8%)
  local copies, waits for them, and re-layouts  4.52 us (3%)
    all_to_all x1, blocking collectives, copy_for_each(): lax.all_to_all(jnp.broadcast_to(x[None], (size, *x.shape)), axis, 0, 0, t...  46.8 us
    all_to_all x1, waiting for transfers between devices, body(): lax.all_to_all(tokens, 'tensor', split_axis=0, concat_axis=0, tiled=True)  33.1 us
    all_to_all x1, blocking collectives, body(): rows = lax.all_to_all(payload, 'tensor', 0, 0, tiled=True)  33 us
    pallas_call x1, Pallas kernels, attention(): pl.pallas_call(lambda *refs: attention_kernel(*refs, head_width=width //...  11.6 us
    all_to_all x1, waiting for transfers between devices, copy_for_each(): lax.all_to_all(jnp.broadcast_to(x[None], (size, *x.shape)), axis, 0, 0, t...  8.78 us
    all_to_all x1, starting transfers between devices, copy_for_each(): lax.all_to_all(jnp.broadcast_to(x[None], (size, *x.shape)), axis, 0, 0, t...  7.21 us
    pallas_call x1, Pallas kernels, merge_tokens(): pl.pallas_call(merge_kernel, in_specs=[pl.BlockSpec(memory_space=pltpu.SM...  5.68 us
    all_to_all x1, starting transfers between devices, body(): lax.all_to_all(tokens, 'tensor', split_axis=0, concat_axis=0, tiled=True)  5.43 us
  transfers between devices with their start and end apart: 4, of which 2 were waited for; matrix products, arithmetic and copies ran while one was open for 2% of the time, Pallas kernels for 7%

profile of v9, /device:TPU:4, one launch (start us, length us, event | category | flops | bytes accessed | tf_op | source)
XLA Modules:
  0.0 176.7 jit_solution(6385876599322700344)
XLA Ops:
  6.5 0.8 payload_copies.1
  7.4 33.0 %all_to_all.20 = bf16[32,40,256]{2,1,0:T(8,128)(2,1)S(1)} all-to-all(bf16[32,40,256]{2,1,0:T(8,128)(2,1)S(1)} %payload_copies.1), channel_id=1, replica_groups=mesh['pipe'=16,'tensor'=32] {'tensor'}, dimensions={0} | all-to-all | bytes 1310720 | tf_op jit(solution)/shard_map/all_to_all | solution.py:246
  40.4 1.0 copy.21
  41.5 0.6 reduce_sum.36
  42.2 0.7 select_bitcast_fusion
  42.9 0.7 broadcast_in_dim.74
  43.5 7.2 %all-to-all-start.1 = ((bf16[16,40,80]{2,1,0:T(8,128)(2,1)}), bf16[16,40,80]{2,1,0:T(8,128)(2,1)S(1)}, u32[]{:S(2)}, u32[]{:S(2)}) async-start(bf16[16,40,80]{2,1,0:T(8,128)(2,1)} %broadcast_in_dim.74), calls=%async_computation.1 | async-start | bytes 327680 | tf_op jit(solution)/shard_map/all_to_all | solution.py:18
  50.8 0.7 normalize_rows.1.refs_0_
  51.5 1.0 copy-done.1
  52.6 8.8 %all-to-all-done.1 = bf16[16,40,80]{2,1,0:T(8,128)(2,1)S(1)} async-done(((bf16[16,40,80]{2,1,0:T(8,128)(2,1)}), bf16[16,40,80]{2,1,0:T(8,128)(2,1)S(1)}, u32[]{:S(2)}, u32[]{:S(2)}) %all-to-all-start.1) | async-done | bytes 102432 | tf_op jit(solution)/shard_map/all_to_all | solution.py:18
  61.4 0.3 reshape.61
  61.7 0.1 constant_dynamic-slice_fusion
  61.8 0.1 broadcast_in_dim.80
  62.0 46.8 %all_to_all.21 = bf16[32,40,640]{2,1,0:T(8,128)(2,1)S(1)} all-to-all(bf16[32,40,640]{2,1,0:T(8,128)(2,1)S(1)} %broadcast_in_dim.80), channel_id=1, replica_groups=mesh['pipe'=16,'tensor'=32] {'tensor'}, dimensions={0} | all-to-all | bytes 3276800 | tf_op jit(solution)/shard_map/all_to_all | solution.py:18
  108.8 2.0 %collective-permute-start = (bf16[1280,640]{1,0:T(8,128)(2,1)S(1)}, bf16[1280,640]{1,0:T(8,128)(2,1)}, u32[]{:S(2)}, u32[]{:S(2)}) collective-permute-start(bf16[1280,640]{1,0:T(8,128)(2,1)S(1)} %bitcast.18), channel_id=1, source_target_pairs={{0,32},{32,0},{64,96},{96,64},{128,160},{160,128},{192,224},{224,1... | collective-permute-start | bytes 4915208 | tf_op jit(solution)/shard_map/ppermute | solution.py:23
  110.8 11.6 %attention.1.context_ref = bf16[512,1280]{1,0:T(8,128)(2,1)S(1)} custom-call(bf16[1280,512]{1,0:T(8,128)(2,1)} %copy-done.1, bf16[3840,1280]{1,0:T(8,128)(2,1)} %all-gather.2.cloned.1.call-done.refs_1_, s32[4,128]{1,0:T(4,128)S(1)} %get-tuple-element.18.refs_2_, s32[4,128]{1,0:T(4,128)S(1)} %get-tuple-element.19.refs_3_), custom_call_target="tpu_custom_call" | custom-call | tf_op jit(solution)/shard_map/attention/pallas_call | solution.py:138
  122.5 5.7 %merge_tokens.1 = bf16[32,4,5120]{2,1,0:T(4,128)(2,1)} custom-call(s32[1]{0:T(128)} %bitcast.core_ref, bf16[512,1280]{1,0:T(8,128)(2,1)S(1)} %attention.1.context_ref, bf16[1280,640]{1,0:T(8,128)(2,1)S(1)} %bitcast.19, bf16[1280,640]{1,0:T(8,128)(2,1)} %collective-permute-done.w_other_ref, bf16[512,1280]{1,0:T(8,128)(2,1)S(1)} %copy-done, ...), custom_call_target="tpu_custom_call" | custom-call | tf_op jit(solution)/shard_map/merge_tokens/pallas_call | solution.py:198
  128.2 5.4 %all-to-all-start.3 = ((bf16[32,4,5120]{2,1,0:T(4,128)(2,1)}), bf16[32,4,5120]{2,1,0:T(4,128)(2,1)S(1)}, u32[]{:S(2)}, u32[]{:S(2)}) async-start(bf16[32,4,5120]{2,1,0:T(4,128)(2,1)} %merge_tokens.1), calls=%async_computation.3 | async-start | bytes 2621440 | tf_op jit(solution)/shard_map/all_to_all | solution.py:269
  134.0 0.1 lt.75
  134.2 0.1 select_reduce_fusion
  134.7 0.1 select_n.49
  134.8 33.1 %all-to-all-done.3 = bf16[32,4,5120]{2,1,0:T(4,128)(2,1)S(1)} async-done(((bf16[32,4,5120]{2,1,0:T(4,128)(2,1)}), bf16[32,4,5120]{2,1,0:T(4,128)(2,1)S(1)}, u32[]{:S(2)}, u32[]{:S(2)}) %all-to-all-start.3) | async-done | bytes 1310752 | tf_op jit(solution)/shard_map/all_to_all | solution.py:269
  167.9 0.3 reshape.64
  168.3 1.6 fusion
  (36 shorter events, 1.1 us)
Async XLA Ops:
  6.5 104.3 %all-gather.2.cloned.1.call-start = ((), (), s32[]{:S(2)}) async-start(), calls=%async_computation.4 | async-start | bytes 10444800 | tf_op jit(solution)/shard_map/all_gather | solution.py:248
  7.4 34.2 %copy-start.6 = (s32[4]{0:T(128)S(1)}, s32[4]{0:T(128)}, u32[]{:S(2)}) copy-start(s32[4]{0:T(128)} %patches_ref.1) | copy-start | bytes 52
  7.4 34.8 %copy-start.3 = (f32[1280]{0:T(1024)S(1)}, f32[1280]{0:T(1024)}, u32[]{:S(2)}) copy-start(f32[1280]{0:T(1024)} %param.9) | copy-start | bytes 15364
  7.4 34.8 %copy-start.4 = (f32[1280]{0:T(1024)S(1)}, f32[1280]{0:T(1024)}, u32[]{:S(2)}) copy-start(f32[1280]{0:T(1024)} %param.12) | copy-start | bytes 15364
  7.4 34.8 %copy-start.5 = (s32[512]{0:T(512)S(1)}, s32[512]{0:T(512)}, u32[]{:S(2)}) copy-start(s32[512]{0:T(512)} %param.13) | copy-start | bytes 6148
  7.4 35.4 %copy-start.2 = (bf16[40,80]{1,0:T(8,128)(2,1)S(1)}, bf16[40,80]{1,0:T(8,128)(2,1)}, u32[]{:S(2)}) copy-start(bf16[40,80]{1,0:T(8,128)(2,1)} %param.11) | copy-start | bytes 19204
  40.4 10.3 %copy-start = (bf16[512,1280]{1,0:T(8,128)(2,1)S(1)}, bf16[512,1280]{1,0:T(8,128)(2,1)}, u32[]{:S(2)}) copy-start(bf16[512,1280]{1,0:T(8,128)(2,1)} %x_ref.1) | copy-start | bytes 3932164
  43.5 17.8 %all-to-all-start.1 = ((bf16[16,40,80]{2,1,0:T(8,128)(2,1)}), bf16[16,40,80]{2,1,0:T(8,128)(2,1)S(1)}, u32[]{:S(2)}, u32[]{:S(2)}) async-start(bf16[16,40,80]{2,1,0:T(8,128)(2,1)} %broadcast_in_dim.74), calls=%async_computation.1 | async-start | bytes 327680 | tf_op jit(solution)/shard_map/all_to_all | solution.py:18
  51.4 1.1 copy-start.1
  108.8 13.7 %collective-permute-start = (bf16[1280,640]{1,0:T(8,128)(2,1)S(1)}, bf16[1280,640]{1,0:T(8,128)(2,1)}, u32[]{:S(2)}, u32[]{:S(2)}) collective-permute-start(bf16[1280,640]{1,0:T(8,128)(2,1)S(1)} %bitcast.18), channel_id=1, source_target_pairs={{0,32},{32,0},{64,96},{96,64},{128,160},{160,128},{192,224},{224,1... | collective-permute-start | bytes 4915208 | tf_op jit(solution)/shard_map/ppermute | solution.py:23
  128.2 39.8 %all-to-all-start.3 = ((bf16[32,4,5120]{2,1,0:T(4,128)(2,1)}), bf16[32,4,5120]{2,1,0:T(4,128)(2,1)S(1)}, u32[]{:S(2)}, u32[]{:S(2)}) async-start(bf16[32,4,5120]{2,1,0:T(4,128)(2,1)} %merge_tokens.1), calls=%async_computation.3 | async-start | bytes 2621440 | tf_op jit(solution)/shard_map/all_to_all | solution.py:269
Sparse Core Ops, SparseCore 0:
  41.6 64.6 all-gather.1

commit v10 on v9

--- a/solution.py
+++ b/solution.py
@@ -31,7 +31,7 @@
     return [pl.BlockSpec(memory_space=pltpu.VMEM)] * count
 
 
-def payload_kernel(patches_ref, sample_ref, w_ref, out_ref, wide_ref):
+def payload_kernel(patches_ref, sample_ref, w_ref, proj_ref, out_ref, proj_out_ref, wide_ref):
     copies, rows, lanes = out_ref.shape
     columns = w_ref.shape[1]
     slots = patches_ref.shape[0]
@@ -49,20 +49,25 @@
     for copy in range(copies):
         out_ref[copy, :, :last] = head
         out_ref[copy, :, last:] = tail
-
-
-def payload_copies(image_patches, image_sample, w, copies):
+    for copy in range(proj_out_ref.shape[0]):
+        proj_out_ref[copy] = proj_ref[...]
+
+
+def payload_copies(image_patches, image_sample, w, copies, w_out, out_copies):
     rows, columns = w.shape
     lanes = -(-(columns + 2 * image_patches.shape[0]) // 128) * 128
     return pl.pallas_call(
         payload_kernel,
-        in_specs=[pl.BlockSpec(memory_space=pltpu.SMEM)] * 2 + in_vmem(1),
-        out_specs=pl.BlockSpec(memory_space=pltpu.VMEM),
-        out_shape=jax.ShapeDtypeStruct((copies, rows, lanes), jnp.bfloat16),
+        in_specs=[pl.BlockSpec(memory_space=pltpu.SMEM)] * 2 + in_vmem(2),
+        out_specs=in_vmem(2),
+        out_shape=[
+            jax.ShapeDtypeStruct((copies, rows, lanes), jnp.bfloat16),
+            jax.ShapeDtypeStruct((out_copies, *w_out.shape), jnp.bfloat16),
+        ],
         scratch_shapes=[pltpu.VMEM((rows, lanes), jnp.float32)],
         compiler_params=pltpu.CompilerParams(vmem_limit_bytes=8 << 20),
         name="payload_copies",
-    )(in_hbm(image_patches), in_hbm(image_sample), in_hbm(w))
+    )(in_hbm(image_patches), in_hbm(image_sample), in_hbm(w), in_hbm(w_out))
 
 
 def normalize_kernel(x_ref, gain_ref, out_ref):
@@ -158,7 +163,7 @@
 
 
 def merge_kernel(
-    core_ref, context_ref, w_own_ref, w_other_ref, x_ref, gain_ref, out_ref, hidden_ref, merged_ref, held_ref, sem
+    core_ref, context_ref, w_own_ref, w_other_ref, x_ref, gain_ref, out_ref, hidden_ref, merged_ref, held_ref, formed_ref, sem, sems
 ):
     core = core_ref[0]
     count, width = context_ref.shape
@@ -184,13 +189,21 @@
     units = count // UNIT
     to_row = lax.broadcasted_iota(jnp.int32, (tokens, count), 0)
     from_row = lax.broadcasted_iota(jnp.int32, (tokens, count), 1)
+    stores = []
     first_row = (to_row % units) * UNIT + (to_row // units) * 4
     for member in range(4):
         choice = (from_row == first_row + member).astype(jnp.bfloat16)
         part = jnp.dot(choice, merged_ref[...], preferred_element_type=jnp.float32)
-        out_ref[:, :, member * width : (member + 1) * width] = part.reshape(
-            -1, units, width
-        ).astype(jnp.bfloat16)
+        columns = slice(member * width, (member + 1) * width)
+        formed_ref[:, :, columns] = part.reshape(-1, units, width).astype(jnp.bfloat16)
+        stores.append(
+            pltpu.make_async_copy(
+                formed_ref.at[:, :, columns], out_ref.at[:, :, columns], sems.at[member]
+            )
+        )
+        stores[-1].start()
+    for store in stores:
+        store.wait()
 
 
 def merge_tokens(core, context, w_own, w_other, x, gain):
@@ -201,13 +214,15 @@
         + in_vmem(2)
         + [pl.BlockSpec(memory_space=pltpu.HBM)]
         + in_vmem(2),
-        out_specs=pl.BlockSpec(memory_space=pltpu.VMEM),
+        out_specs=pl.BlockSpec(memory_space=pltpu.HBM),
         out_shape=pltpu.HBM((UNIT // 4, count // UNIT, 4 * width), jnp.bfloat16),
         scratch_shapes=[
             pltpu.VMEM((2, count, width // 2), jnp.float32),
             pltpu.VMEM((count, width), jnp.bfloat16),
             pltpu.VMEM(w_other.shape, jnp.bfloat16),
+            pltpu.VMEM((UNIT // 4, count // UNIT, 4 * width), jnp.bfloat16),
             pltpu.SemaphoreType.DMA,
+            pltpu.SemaphoreType.DMA((4,)),
         ],
         compiler_params=pltpu.CompilerParams(vmem_limit_bytes=28 << 20),
         name="merge_tokens",
@@ -242,13 +257,15 @@
     row_count, qkv_part = w_qkv.shape
 
     together = lax.optimization_barrier
-    payload = payload_copies(image_patches, image_sample, w_qkv, group_size)
+    payload, out_copies = payload_copies(
+        image_patches, image_sample, w_qkv, group_size, w_out, lax.axis_size("pipe")
+    )
     rows = lax.all_to_all(payload, "tensor", 0, 0, tiled=True)
     slab = rows[:, :, :qkv_part].reshape(width, qkv_part).T
     w_all = lax.all_gather(slab, "pipe", axis=0, tiled=True)
 
-    slab, w_out, patches = together((slab, w_out, patches))
-    blocks = copy_for_each(w_out, "pipe")
+    slab, out_copies, patches = together((slab, out_copies, patches))
+    blocks = lax.all_to_all(out_copies, "pipe", 0, 0, tiled=True)
     normed = normalize_rows(patches, attn_gain[None, :])
     live = jnp.arange(patch_count, dtype=jnp.int32) < jnp.sum(image_patches)
     key_id = jnp.where(live, window_ids, -1).reshape(patch_count // UNIT, UNIT)

time: 177 us -> 175 us (0.989)
  no operation moved by 1% of the time
where the time goes in v10:
time: 175 us
  blocking collectives  79.5 us (45%)
  waiting for transfers between devices  40.8 us (23%)
  Pallas kernels  19 us (11%)
  starting transfers between devices  14.9 us (9%)
  between operations  13.6 us (8%)
  local copies, waits for them, and re-layouts  3.83 us (2%)
    all_to_all x1, blocking collectives, copy_for_each(): lax.all_to_all(jnp.broadcast_to(x[None], (size, *x.shape)), axis, 0, 0, t...  46.5 us
    all_to_all x1, blocking collectives, body(): rows = lax.all_to_all(payload, 'tensor', 0, 0, tiled=True)  33 us
    all_to_all x1, waiting for transfers between devices, body(): lax.all_to_all(tokens, 'tensor', split_axis=0, concat_axis=0, tiled=True)  32.7 us
    pallas_call x1, Pallas kernels, attention(): pl.pallas_call(lambda *refs: attention_kernel(*refs, head_width=width //...  11.6 us
    all_to_all x1, waiting for transfers between devices, body(): blocks = lax.all_to_all(out_copies, 'pipe', 0, 0, tiled=True)  8.04 us
    all_to_all x1, starting transfers between devices, body(): blocks = lax.all_to_all(out_copies, 'pipe', 0, 0, tiled=True)  7.22 us
    all_to_all x1, starting transfers between devices, body(): lax.all_to_all(tokens, 'tensor', split_axis=0, concat_axis=0, tiled=True)  5.58 us
    pallas_call x1, Pallas kernels, merge_tokens(): pl.pallas_call(merge_kernel, in_specs=[pl.BlockSpec(memory_space=pltpu.SM...  5.26 us
  transfers between devices with their start and end apart: 4, of which 2 were waited for; matrix products, arithmetic and copies ran while one was open for 2% of the time, Pallas kernels for 7%

profile of v10, /device:TPU:4, one launch (start us, length us, event | category | flops | bytes accessed | tf_op | source)
XLA Modules:
  0.0 174.9 jit_solution(8417444330100151595)
XLA Ops:
  6.5 1.5 payload_copies.1
  8.0 33.0 %all_to_all.20 = bf16[32,40,256]{2,1,0:T(8,128)(2,1)S(1)} all-to-all(bf16[32,40,256]{2,1,0:T(8,128)(2,1)S(1)} %get-tuple-element.17), channel_id=1, replica_groups=mesh['pipe'=16,'tensor'=32] {'tensor'}, dimensions={0} | all-to-all | bytes 1310720 | tf_op jit(solution)/shard_map/all_to_all | solution.py:263
  41.0 1.0 copy.21
  42.1 0.6 reduce_sum.36
  42.8 0.7 select_bitcast_fusion
  43.5 7.2 %all-to-all-start.1 = ((bf16[16,40,80]{2,1,0:T(8,128)(2,1)}), bf16[16,40,80]{2,1,0:T(8,128)(2,1)S(1)}, u32[]{:S(2)}, u32[]{:S(2)}) async-start(bf16[16,40,80]{2,1,0:T(8,128)(2,1)} %get-tuple-element.19), calls=%async_computation.1 | async-start | bytes 327680 | tf_op jit(solution)/shard_map/all_to_all | solution.py:268
  50.7 0.7 normalize_rows.1.refs_0_
  51.4 1.0 copy-done.1
  52.5 8.0 %all-to-all-done.1 = bf16[16,40,80]{2,1,0:T(8,128)(2,1)S(1)} async-done(((bf16[16,40,80]{2,1,0:T(8,128)(2,1)}), bf16[16,40,80]{2,1,0:T(8,128)(2,1)S(1)}, u32[]{:S(2)}, u32[]{:S(2)}) %all-to-all-start.1) | async-done | bytes 102432 | tf_op jit(solution)/shard_map/all_to_all | solution.py:268
  60.6 0.3 reshape.60
  60.9 0.1 constant_dynamic-slice_fusion
  61.0 0.1 broadcast_in_dim.73
  61.1 46.5 %all_to_all.21 = bf16[32,40,640]{2,1,0:T(8,128)(2,1)S(1)} all-to-all(bf16[32,40,640]{2,1,0:T(8,128)(2,1)S(1)} %broadcast_in_dim.73), channel_id=1, replica_groups=mesh['pipe'=16,'tensor'=32] {'tensor'}, dimensions={0} | all-to-all | bytes 3276800 | tf_op jit(solution)/shard_map/all_to_all | solution.py:18
  107.6 2.1 %collective-permute-start = (bf16[1280,640]{1,0:T(8,128)(2,1)S(1)}, bf16[1280,640]{1,0:T(8,128)(2,1)}, u32[]{:S(2)}, u32[]{:S(2)}) collective-permute-start(bf16[1280,640]{1,0:T(8,128)(2,1)S(1)} %bitcast.18), channel_id=1, source_target_pairs={{0,32},{32,0},{64,96},{96,64},{128,160},{160,128},{192,224},{224,1... | collective-permute-start | bytes 4915208 | tf_op jit(solution)/shard_map/ppermute | solution.py:23
  109.8 11.6 %attention.1.context_ref = bf16[512,1280]{1,0:T(8,128)(2,1)S(1)} custom-call(bf16[1280,512]{1,0:T(8,128)(2,1)} %copy-done.1, bf16[3840,1280]{1,0:T(8,128)(2,1)} %all-gather.2.cloned.1.call-done.refs_1_, s32[4,128]{1,0:T(4,128)S(1)} %get-tuple-element.22.refs_2_, s32[4,128]{1,0:T(4,128)S(1)} %get-tuple-element.23.refs_3_), custom_call_target="tpu_custom_call" | custom-call | tf_op jit(solution)/shard_map/attention/pallas_call | solution.py:143
  121.4 5.3 %merge_tokens.1 = bf16[32,4,5120]{2,1,0:T(4,128)(2,1)} custom-call(s32[1]{0:T(128)} %bitcast.core_ref, bf16[512,1280]{1,0:T(8,128)(2,1)S(1)} %attention.1.context_ref, bf16[1280,640]{1,0:T(8,128)(2,1)S(1)} %bitcast.19, bf16[1280,640]{1,0:T(8,128)(2,1)} %collective-permute-done.w_other_ref, bf16[512,1280]{1,0:T(8,128)(2,1)S(1)} %copy-done, ...), custom_call_target="tpu_custom_call" | custom-call | tf_op jit(solution)/shard_map/merge_tokens/pallas_call | solution.py:211
  126.7 5.6 %all-to-all-start.3 = ((bf16[32,4,5120]{2,1,0:T(4,128)(2,1)}), bf16[32,4,5120]{2,1,0:T(4,128)(2,1)S(1)}, u32[]{:S(2)}, u32[]{:S(2)}) async-start(bf16[32,4,5120]{2,1,0:T(4,128)(2,1)} %merge_tokens.1), calls=%async_computation.3 | async-start | bytes 2621440 | tf_op jit(solution)/shard_map/all_to_all | solution.py:286
  132.3 0.1 broadcast_in_dim.76
  132.7 0.1 lt.75
  132.8 0.1 select_reduce_fusion
  133.4 0.1 select_n.49
  133.5 32.7 %all-to-all-done.3 = bf16[32,4,5120]{2,1,0:T(4,128)(2,1)S(1)} async-done(((bf16[32,4,5120]{2,1,0:T(4,128)(2,1)}), bf16[32,4,5120]{2,1,0:T(4,128)(2,1)S(1)}, u32[]{:S(2)}, u32[]{:S(2)}) %all-to-all-start.3) | async-done | bytes 1310752 | tf_op jit(solution)/shard_map/all_to_all | solution.py:286
  166.2 0.3 reshape.63
  166.5 1.6 fusion
  (33 shorter events, 0.9 us)
Async XLA Ops:
  6.5 103.2 %all-gather.2.cloned.1.call-start = ((), (), s32[]{:S(2)}) async-start(), calls=%async_computation.4 | async-start | bytes 10444800 | tf_op jit(solution)/shard_map/all_gather | solution.py:265
  8.0 34.1 %copy-start.5 = (s32[4]{0:T(128)S(1)}, s32[4]{0:T(128)}, u32[]{:S(2)}) copy-start(s32[4]{0:T(128)} %patches_ref.1) | copy-start | bytes 52
  8.0 34.8 %copy-start.2 = (f32[1280]{0:T(1024)S(1)}, f32[1280]{0:T(1024)}, u32[]{:S(2)}) copy-start(f32[1280]{0:T(1024)} %param.9) | copy-start | bytes 15364
  8.0 34.8 %copy-start.3 = (f32[1280]{0:T(1024)S(1)}, f32[1280]{0:T(1024)}, u32[]{:S(2)}) copy-start(f32[1280]{0:T(1024)} %param.12) | copy-start | bytes 15364
  8.0 34.8 %copy-start.4 = (s32[512]{0:T(512)S(1)}, s32[512]{0:T(512)}, u32[]{:S(2)}) copy-start(s32[512]{0:T(512)} %param.13) | copy-start | bytes 6148
  41.0 9.7 %copy-start = (bf16[512,1280]{1,0:T(8,128)(2,1)S(1)}, bf16[512,1280]{1,0:T(8,128)(2,1)}, u32[]{:S(2)}) copy-start(bf16[512,1280]{1,0:T(8,128)(2,1)} %x_ref.1) | copy-start | bytes 3932164
  43.5 17.1 %all-to-all-start.1 = ((bf16[16,40,80]{2,1,0:T(8,128)(2,1)}), bf16[16,40,80]{2,1,0:T(8,128)(2,1)S(1)}, u32[]{:S(2)}, u32[]{:S(2)}) async-start(bf16[16,40,80]{2,1,0:T(8,128)(2,1)} %get-tuple-element.19), calls=%async_computation.1 | async-start | bytes 327680 | tf_op jit(solution)/shard_map/all_to_all | solution.py:268
  51.4 1.1 copy-start.1
  107.6 13.8 %collective-permute-start = (bf16[1280,640]{1,0:T(8,128)(2,1)S(1)}, bf16[1280,640]{1,0:T(8,128)(2,1)}, u32[]{:S(2)}, u32[]{:S(2)}) collective-permute-start(bf16[1280,640]{1,0:T(8,128)(2,1)S(1)} %bitcast.18), channel_id=1, source_target_pairs={{0,32},{32,0},{64,96},{96,64},{128,160},{160,128},{192,224},{224,1... | collective-permute-start | bytes 4915208 | tf_op jit(solution)/shard_map/ppermute | solution.py:23
  126.7 39.5 %all-to-all-start.3 = ((bf16[32,4,5120]{2,1,0:T(4,128)(2,1)}), bf16[32,4,5120]{2,1,0:T(4,128)(2,1)S(1)}, u32[]{:S(2)}, u32[]{:S(2)}) async-start(bf16[32,4,5120]{2,1,0:T(4,128)(2,1)} %merge_tokens.1), calls=%async_computation.3 | async-start | bytes 2621440 | tf_op jit(solution)/shard_map/all_to_all | solution.py:286
Sparse Core Ops, SparseCore 0:
  42.2 64.0 all-gather.1
